TPU v7x, 16 devices: a whole 2x2x2 slice. The times are simulated.
16 devices in a mesh: dp: 4 (over z, y), tp: 4 (over x, core).
Axes of the slice: x: 2, y: 2, z: 2, core: 2. Of those that a mesh axis runs over, the one named last changes fastest.
Arguments:
- x_in: bfloat16 [32, 2048, 1024], P('dp'), parts along dimension 0
- start_pos: int32 [32], P('dp'), parts along dimension 0
- kv_state: float32 [32, 4, 256, 512], P('dp', 'tp'), parts along dimension 0
- ln1_gain: float32 [1024], replicated
- ln1_bias: float32 [1024], replicated
- w_q: bfloat16 [1024, 1024], P(None, 'tp')
- w_k: bfloat16 [1024, 1024], P(None, 'tp')
- w_v: bfloat16 [1024, 2048], P(None, 'tp')
- w_g: bfloat16 [1024, 2048], P(None, 'tp')
- w_o: bfloat16 [2048, 1024], P('tp')
- ln2_gain: float32 [1024], replicated
- ln2_bias: float32 [1024], replicated
- w_up: bfloat16 [1024, 2048], P(None, 'tp')
- w_down: bfloat16 [2048, 1024], P('tp')
Outputs:
- output 1: bfloat16 [32, 2048, 1024], P('dp'), parts along dimension 0
- output 2: float32 [32, 4, 256, 512], P('dp', 'tp'), parts along dimension 0
There are 4 independent parts. A program takes and returns all parts, laid end to end along the dimension named above; an argument that names none is the same for every part.
All inputs are finite; a program needn't handle non-finite values.
Results may differ from a plain program's by a relative error of at most 0.0132695.
Values are sent between devices in bfloat16 or wider.
A program may use at most 1 GiB of HBM per device.

v0:
```python
import jax
import jax.numpy as jnp
from jax import lax
from jax.sharding import PartitionSpec as P

NORM_EPS = 1e-5
GROUP_EPS = 1e-6
ROPE_BASE = 10000.0


def layer_norm(x_f32, norm_gain, norm_bias):
    row_mean = jnp.mean(x_f32, axis=-1, keepdims=True)
    centered = x_f32 - row_mean
    variance = jnp.mean(centered * centered, axis=-1, keepdims=True)
    return centered * lax.rsqrt(variance + NORM_EPS) * norm_gain + norm_bias


def rotate_half(head_vecs, cos_t, sin_t):
    half_dim = head_vecs.shape[-1] // 2
    first_half = head_vecs[..., :half_dim]
    second_half = head_vecs[..., half_dim:]
    return jnp.concatenate([first_half * cos_t - second_half * sin_t, second_half * cos_t + first_half * sin_t], axis=-1)


def rope_tables(first_pos, chunk_len, key_dim):
    half_dim = key_dim // 2
    inv_freq = jnp.power(ROPE_BASE, -jnp.arange(half_dim).astype(jnp.float32) / half_dim)
    positions = (first_pos[:, None] + jnp.arange(chunk_len)[None, :]).astype(jnp.float32)
    angles = positions[:, :, None] * inv_freq
    return jnp.cos(angles)[:, :, None, :], jnp.sin(angles)[:, :, None, :]


def head_log_decay(head_ids):
    return jnp.log1p(-jnp.exp2(-5.0 - head_ids.astype(jnp.float32)))


def project_heads(h_one, cos_t, sin_t, w_q, w_k, w_v, w_g, num_heads):
    d_model = h_one.shape[-1]
    key_dim = w_q.shape[1] // num_heads
    val_dim = w_v.shape[1] // num_heads
    q_raw = jnp.einsum('bcd,dhk->bchk', h_one, w_q.reshape(d_model, num_heads, key_dim), preferred_element_type=jnp.float32)
    k_raw = jnp.einsum('bcd,dhk->bchk', h_one, w_k.reshape(d_model, num_heads, key_dim), preferred_element_type=jnp.float32)
    queries = rotate_half(q_raw, cos_t, sin_t).astype(jnp.bfloat16)
    keys = (rotate_half(k_raw, cos_t, sin_t) * key_dim ** -0.5).astype(jnp.bfloat16)
    values = jnp.einsum('bcd,dhe->bche', h_one, w_v.reshape(d_model, num_heads, val_dim), preferred_element_type=jnp.float32).astype(jnp.bfloat16)
    gates = jnp.einsum('bcd,dhe->bche', h_one, w_g.reshape(d_model, num_heads, val_dim), preferred_element_type=jnp.float32)
    return queries, keys, values, gates


def mix_heads(queries, keys, values_f32, gates, state_in, log_gamma, w_o):
    chunk_len = queries.shape[1]
    num_heads = queries.shape[2]
    val_dim = values_f32.shape[3]
    step_ids = jnp.arange(chunk_len)
    step_gap = step_ids[:, None] - step_ids[None, :]
    inner_decay = jnp.where(step_gap[None] >= 0, jnp.exp(jnp.maximum(step_gap, 0).astype(jnp.float32)[None] * log_gamma[:, None, None]), 0.0)
    query_decay = jnp.exp((step_ids + 1).astype(jnp.float32)[:, None] * log_gamma[None, :])
    scores = jnp.einsum('bchk,bjhk->bhcj', queries, keys, preferred_element_type=jnp.float32) * inner_decay
    retained = jnp.einsum('bhcj,bjhe->bche', scores, values_f32) + jnp.einsum('bchk,bhke->bche', queries.astype(jnp.float32), state_in) * query_decay[:, :, None]
    row_mean = jnp.mean(retained, axis=-1, keepdims=True)
    centered = retained - row_mean
    variance = jnp.mean(centered * centered, axis=-1, keepdims=True)
    normed = centered * lax.rsqrt(variance + GROUP_EPS)
    mixed = (jax.nn.silu(gates) * normed).astype(jnp.bfloat16)
    return jnp.einsum('bche,hed->bcd', mixed, w_o.reshape(num_heads, val_dim, w_o.shape[1]), preferred_element_type=jnp.float32)


def chunk_state(keys, values_f32, log_gamma):
    chunk_len = keys.shape[1]
    step_ids = jnp.arange(chunk_len)
    key_decay = jnp.exp((chunk_len - 1 - step_ids).astype(jnp.float32)[:, None] * log_gamma[None, :])
    return jnp.einsum('bjhk,bjhe->bhke', keys.astype(jnp.float32) * key_decay[:, :, None], values_f32)


def feed_forward(x_mid, ln2_gain, ln2_bias, w_up, w_down):
    h_two = layer_norm(x_mid.astype(jnp.float32), ln2_gain, ln2_bias).astype(jnp.bfloat16)
    activated = jax.nn.gelu(jnp.einsum('bcd,df->bcf', h_two, w_up, preferred_element_type=jnp.float32), approximate=False).astype(jnp.bfloat16)
    return jnp.einsum('bcf,fd->bcd', activated, w_down, preferred_element_type=jnp.float32)


def solution(mesh):
    def local_layer(x_in, start_pos, kv_state, ln1_gain, ln1_bias, w_q, w_k, w_v, w_g, w_o, ln2_gain, ln2_bias, w_up, w_down):
        local_heads = kv_state.shape[1]
        chunk_len = x_in.shape[1]
        head_ids = lax.axis_index('tp') * local_heads + jnp.arange(local_heads)
        log_gamma = head_log_decay(head_ids)
        x_f32 = x_in.astype(jnp.float32)
        h_one = layer_norm(x_f32, ln1_gain, ln1_bias).astype(jnp.bfloat16)
        cos_t, sin_t = rope_tables(start_pos, chunk_len, kv_state.shape[2])
        queries, keys, values, gates = project_heads(h_one, cos_t, sin_t, w_q, w_k, w_v, w_g, local_heads)
        values_f32 = values.astype(jnp.float32)
        attn_part = mix_heads(queries, keys, values_f32, gates, kv_state, log_gamma, w_o).astype(jnp.bfloat16)
        new_state = jnp.exp(chunk_len * log_gamma)[:, None, None] * kv_state + chunk_state(keys, values_f32, log_gamma)
        attn_out = lax.psum(attn_part, 'tp')
        x_mid = (x_f32 + attn_out.astype(jnp.float32)).astype(jnp.bfloat16)
        ffn_part = feed_forward(x_mid, ln2_gain, ln2_bias, w_up, w_down).astype(jnp.bfloat16)
        ffn_out = lax.psum(ffn_part, 'tp')
        x_out = (x_mid.astype(jnp.float32) + ffn_out.astype(jnp.float32)).astype(jnp.bfloat16)
        return x_out, new_state

    in_specs = (P('dp', None, None), P('dp'), P('dp', 'tp', None, None), P(), P(), P(None, 'tp'), P(None, 'tp'), P(None, 'tp'), P(None, 'tp'), P('tp', None), P(), P(), P(None, 'tp'), P('tp', None))
    out_specs = (P('dp', None, None), P('dp', 'tp', None, None))
    return jax.shard_map(local_layer, mesh=mesh, in_specs=in_specs, out_specs=out_specs, check_vma=False)
```

profile of v0, /device:TPU:0, one launch (start us, length us, event | category | flops | bytes accessed | tf_op | source)
XLA Modules:
  0.0 1702.1 jit_solution(5384103375785826610)
XLA Ops:
  7.2 0.0 all-reduce.3.cloned.1.call-start
  7.3 8.5 exponential_select_fusion
  15.9 0.6 multiply_exponential_fusion.1
  16.5 11.7 convert_reduce_fusion.1
  28.2 13.0 fusion.10
  41.3 23.9 %convolution_bitcast_fusion.1 = f32[8,2048,1,256]{1,3,0,2:T(8,128)} fusion(bf16[1024,256]{1,0:T(8,128)(2,1)S(1)} %copy-done.12, bf16[8,2048,1024]{2,1,0:T(8,128)(2,1)} %param.14, f32[1024]{0:T(1024)S(1)} %copy-done.14, f32[1024]{0:T(1024)S(1)} %copy-done.16, f32[8,2048]{1,0:T(8,128)S(1)} %add_rsqrt_fusion.2, f32[8,2048]{1,0:T(8,128)S(1)} %broadcast_multiply_fusion.2), kind=kOutput, calls=%fused_computation.123 | convolution fusion | flops 8690597888 | bytes 50995200 | tf_op jit(solution)/shard_map/bcd,dhk->bchk/dot_general | solution.py:41
  65.2 23.8 %convolution_bitcast_fusion = f32[8,2048,1,256]{1,3,0,2:T(8,128)} fusion(bf16[1024,256]{1,0:T(8,128)(2,1)S(1)} %copy-done.13, bf16[8,2048,1024]{2,1,0:T(8,128)(2,1)} %param.14, f32[1024]{0:T(1024)S(1)} %copy-done.14, f32[1024]{0:T(1024)S(1)} %copy-done.16, f32[8,2048]{1,0:T(8,128)S(1)} %add_rsqrt_fusion.2, f32[8,2048]{1,0:T(8,128)S(1)} %broadcast_multiply_fusion.2), kind=kOutput, calls=%fused_computation.122 | convolution fusion | flops 8690597888 | bytes 50995200 | tf_op jit(solution)/shard_map/bcd,dhk->bchk/dot_general | solution.py:42
  89.0 0.1 add_convert_fusion
  89.1 26.7 %convolution_convert_fusion.2 = bf16[8,2048,512]{2,1,0:T(8,128)(2,1)} fusion(bf16[1024,512]{1,0:T(8,128)(2,1)S(1)} %copy-done.8, bf16[8,2048,1024]{2,1,0:T(8,128)(2,1)} %param.14, f32[1024]{0:T(1024)S(1)} %copy-done.14, f32[1024]{0:T(1024)S(1)} %copy-done.16, f32[8,2048]{1,0:T(8,128)S(1)} %add_rsqrt_fusion.2, f32[8,2048]{1,0:T(8,128)S(1)} %broadcast_multiply_fusion.2), kind=kOutput, calls=%fused_computation.99 | convolution fusion | flops 17288921088 | bytes 51519488 | tf_op jit(solution)/shard_map/bcd,dhe->bche/dot_general | solution.py:45
  115.8 39.3 %fusion.90 = (f32[8,2048,128]{1,2,0:T(8,128)}, f32[8,2048,128]{1,2,0:T(8,128)}, bf16[8,2048,128]{1,2,0:T(8,128)(2,1)}, bf16[8,2048,128]{1,2,0:T(8,128)(2,1)}) fusion(f32[8,2048,1,256]{1,3,0,2:T(8,128)} %convolution_bitcast_fusion, f32[128]{0:T(128)S(1)} %multiply_power_fusion, f32[8,2048]{1,0:T(8,128)S(1)} %add_convert_fusion, ...), kind=kLoop, calls=%fused_computation.115 | loop fusion | flops 31457280 | bytes 58786304 | tf_op jit(solution)/shard_map/concatenate | solution.py:22
  155.1 17.7 %fusion.96 = f32[8,2048,512]{2,1,0:T(8,128)} fusion(bf16[8,2048,128]{1,2,0:T(8,128)(2,1)} %get-tuple-element.12, bf16[8,2048,128]{1,2,0:T(8,128)(2,1)} %get-tuple-element.13, f32[8,1,256,512]{3,2,1,0:T(8,128)} %param.16), kind=kOutput, calls=%fused_computation.124 | convolution fusion | flops 4311744512 | bytes 46137344 | tf_op jit(solution)/shard_map/bchk,bhke->bche/dot_general | solution.py:59
  172.9 67.7 %fusion.38.clone.4 = f32[8,2048,2048]{2,1,0:T(8,128)} fusion(f32[2048,2048]{1,0:T(8,128)} %exponential_select_fusion, bf16[8,2048,128]{1,2,0:T(8,128)(2,1)} %get-tuple-element.12, bf16[8,2048,128]{1,2,0:T(8,128)(2,1)} %get-tuple-element.13, f32[8,2048,128]{1,2,0:T(8,128)} %get-tuple-element.9, ...), kind=kOutput, calls=%fused_computation.1.clone.clone.clone.clone.clone.1 | convolution fusion | flops 17242783744 | bytes 176160768 | tf_op jit(solution)/shard_map/bchk,bjhk->bhcj/dot_general | solution.py:58
  240.6 72.5 %fusion.164 = (f32[8,2048]{1,0:T(8,128)S(1)}, f32[8,2048,1,512]{3,1,0,2:T(8,128)}) fusion(f32[2048]{0:T(1024)S(1)} %copy-done.6, f32[8,2048,512]{2,1,0:T(8,128)} %fusion.96, bf16[8,2048,512]{2,1,0:T(8,128)(2,1)} %convolution_convert_fusion.2, f32[8,2048,2048]{2,1,0:T(8,128)} %fusion.38.clone.4), kind=kOutput, calls=%fused_computation.188 | convolution fusion | flops 34384887808 | bytes 218177536 | tf_op jit(solution)/shard_map/bhcj,bjhe->bche/dot_general | solution.py:59
  313.1 13.6 multiply_reduce_fusion
  326.7 49.8 %convolution_convert_fusion.1 = bf16[8,2048,1024]{2,1,0:T(8,128)(2,1)} fusion(f32[8,2048,1,512]{3,1,0,2:T(8,128)} %get-tuple-element.15, f32[8,2048]{1,0:T(8,128)S(1)} %add_rsqrt_fusion.1, f32[8,2048]{1,0:T(8,128)S(1)} %broadcast_multiply_fusion, bf16[512,1024]{1,0:T(8,128)(2,1)S(1)} %copy-done, bf16[1024,512]{1,0:T(8,128)(2,1)S(1)} %copy-done.9, ...), kind=kOutput, calls=%fused_computation.58 | convolution fusion | flops 34544287744 | bytes 103030784 | tf_op jit(solution)/shard_map/bche,hed->bcd/dot_general | solution.py:65
  376.6 0.0 all-reduce.5.cloned.1.call-start
  376.6 557.1 %all-reduce.3.cloned.1.call-done = bf16[8,2048,1024]{2,1,0:T(8,128)(2,1)} async-done(((bf16[8,2048,1024]{2,1,0:T(8,128)(2,1)}), bf16[8,2048,1024]{2,1,0:T(8,128)(2,1)}) %all-reduce.3.cloned.1.call-update) | async-done | bytes 33554448 | tf_op jit(solution)/shard_map/psum | solution.py:94
  933.8 32.9 %convert_reduce_fusion = (f32[8,2048]{1,0:T(8,128)S(1)}, bf16[8,2048,1024]{2,1,0:T(8,128)(2,1)}) fusion(bf16[8,2048,1024]{2,1,0:T(8,128)(2,1)} %all-reduce.3.cloned.1.call-done, bf16[8,2048,1024]{2,1,0:T(8,128)(2,1)} %param.14), kind=kLoop, calls=%fused_computation.4 | loop fusion | flops 100646912 | bytes 100728832 | tf_op jit(solution)/shard_map/reduce_sum | solution.py:12
  966.8 13.1 fusion.6
  979.9 35.7 %fusion.95 = (u8[2048,512]{1,0:T(8,128)(4,1)S(1)}, u8[2048,512]{1,0:T(8,128)(4,1)S(1)}, f32[8,2048,512]{2,1,0:T(8,128)}) fusion(bf16[1024,512]{1,0:T(8,128)(2,1)S(1)} %copy-done.10, bf16[8,2048,1024]{2,1,0:T(8,128)(2,1)} %get-tuple-element.7, f32[1024]{0:T(1024)S(1)} %copy-done.18, f32[1024]{0:T(1024)S(1)} %copy-done.19, f32[8,2048]{1,0:T(8,128)S(1)} %add_rsqrt_fusion, ...), kind=kOutput, calls=%fused_computation.121 | convolution fusion | flops 17387487232 | bytes 70393856 | tf_op jit(solution)/shard_map/bcd,df->bcf/dot_general | solution.py:77
  1015.6 91.7 %convolution_convert_fusion = bf16[8,2048,1024]{2,1,0:T(8,128)(2,1)} fusion(f32[8,2048,512]{2,1,0:T(8,128)} %get-tuple-element.16, u8[2048,512]{1,0:T(8,128)(4,1)S(1)} %get-tuple-element.5, u8[2048,512]{1,0:T(8,128)(4,1)S(1)} %get-tuple-element.4, bf16[512,1024]{1,0:T(8,128)(2,1)S(1)} %copy-done.11), kind=kOutput, calls=%fused_computation.57 | convolution fusion | flops 17783848960 | bytes 70254592 | tf_op jit(solution)/shard_map/bcf,fd->bcd/dot_general | solution.py:78
  1107.3 16.3 fusion.99
  1123.7 538.0 %all-reduce.5.cloned.1.call-done = bf16[8,2048,1024]{2,1,0:T(8,128)(2,1)} async-done(((bf16[8,2048,1024]{2,1,0:T(8,128)(2,1)}), bf16[8,2048,1024]{2,1,0:T(8,128)(2,1)}) %all-reduce.5.cloned.1.call-update) | async-done | bytes 33554448 | tf_op jit(solution)/shard_map/psum | solution.py:97
  1661.7 33.3 %fusion.15 = bf16[8,2048,1024]{2,1,0:T(8,128)(2,1)} fusion(bf16[8,2048,1024]{2,1,0:T(8,128)(2,1)} %get-tuple-element.7, bf16[8,2048,1024]{2,1,0:T(8,128)(2,1)} %all-reduce.5.cloned.1.call-done), kind=kLoop, calls=%fused_computation.21 | loop fusion | flops 67108864 | bytes 100663296 | tf_op jit(solution)/shard_map/convert_element_type | solution.py:98
  (50 shorter events, 0.2 us)
Async XLA Ops:
  7.2 319.5 %copy-start = (bf16[512,1024]{1,0:T(8,128)(2,1)S(1)}, bf16[512,1024]{1,0:T(8,128)(2,1)}, u32[]{:S(2)}) copy-start(bf16[512,1024]{1,0:T(8,128)(2,1)} %param.23) | copy-start | bytes 3145732
  7.2 926.6 %all-reduce.3.cloned.1.call-start = ((), (), s32[]{:S(2)}) async-start(), calls=%async_computation | async-start | bytes 67108864 | tf_op jit(solution)/shard_map/psum | solution.py:94
  16.5 24.8 %copy-start.12 = (bf16[1024,256]{1,0:T(8,128)(2,1)S(1)}, bf16[1024,256]{1,0:T(8,128)(2,1)}, u32[]{:S(2)}) copy-start(bf16[1024,256]{1,0:T(8,128)(2,1)} %param.19) | copy-start | bytes 1572868
  16.5 24.8 %copy-start.14 = (f32[1024]{0:T(1024)S(1)}, f32[1024]{0:T(1024)}, u32[]{:S(2)}) copy-start(f32[1024]{0:T(1024)} %param.18) | copy-start | bytes 12292
  16.5 24.8 %copy-start.16 = (f32[1024]{0:T(1024)S(1)}, f32[1024]{0:T(1024)}, u32[]{:S(2)}) copy-start(f32[1024]{0:T(1024)} %param.17) | copy-start | bytes 12292
  28.2 60.9 %copy-start.2 = (f32[8,2048]{1,0:T(8,128)}, f32[8,2048]{1,0:T(8,128)S(1)}, u32[]{:S(2)}) copy-start(f32[8,2048]{1,0:T(8,128)S(1)} %broadcast_multiply_fusion.2) | copy-start | bytes 196612
  41.3 47.8 %copy-start.4 = (f32[8,2048]{1,0:T(8,128)}, f32[8,2048]{1,0:T(8,128)S(1)}, u32[]{:S(2)}) copy-start(f32[8,2048]{1,0:T(8,128)S(1)} %add_rsqrt_fusion.2) | copy-start | bytes 196612
  41.3 23.9 %copy-start.13 = (bf16[1024,256]{1,0:T(8,128)(2,1)S(1)}, bf16[1024,256]{1,0:T(8,128)(2,1)}, u32[]{:S(2)}) copy-start(bf16[1024,256]{1,0:T(8,128)(2,1)} %param.20) | copy-start | bytes 1572868
  65.2 23.8 %copy-start.7 = (s32[8]{0:T(128)S(1)}, s32[8]{0:T(128)}, u32[]{:S(2)}) copy-start(s32[8]{0:T(128)} %param.15) | copy-start | bytes 100
  65.2 23.9 %copy-start.8 = (bf16[1024,512]{1,0:T(8,128)(2,1)S(1)}, bf16[1024,512]{1,0:T(8,128)(2,1)}, u32[]{:S(2)}) copy-start(bf16[1024,512]{1,0:T(8,128)(2,1)} %param.21) | copy-start | bytes 3145732
  172.9 67.7 %copy-start.6 = (f32[2048]{0:T(1024)S(1)}, f32[2048]{0:T(1024)}, u32[]{:S(2)}) copy-start(f32[2048]{0:T(1024)} %multiply_exponential_fusion.1) | copy-start | bytes 24580
  313.0 13.6 copy-start.3
  313.0 13.7 copy-start.5
  313.1 13.7 copy-start.9
  313.1 13.7 copy-start.15
  313.1 13.7 copy-start.17
  376.6 1285.1 %all-reduce.5.cloned.1.call-start = ((), (), s32[]{:S(2)}) async-start(), calls=%async_computation.1 | async-start | bytes 67108864 | tf_op jit(solution)/shard_map/psum | solution.py:97
  966.7 13.1 copy-start.10
  966.7 13.2 copy-start.18
  966.7 13.1 copy-start.19
  979.9 35.7 %copy-start.11 = (bf16[512,1024]{1,0:T(8,128)(2,1)S(1)}, bf16[512,1024]{1,0:T(8,128)(2,1)}, u32[]{:S(2)}) copy-start(bf16[512,1024]{1,0:T(8,128)(2,1)} %param.27) | copy-start | bytes 3145732
  1107.3 587.6 %copy-start.1 = (bf16[512,1024]{1,0:T(8,128)(2,1)S(1)}, bf16[512,1024]{1,0:T(8,128)(2,1)}, u32[]{:S(2)}) copy-start(bf16[512,1024]{1,0:T(8,128)(2,1)} %param.23) | copy-start | bytes 3145732
Sparse Core Ops, SparseCore 0:
  376.7 557.0 all-reduce.2
  1107.4 554.2 all-reduce.4
where the time goes:
time: 1710 us; the launch traced here: 1700 us
  waiting for transfers between devices  1100 us (64%)
  matrix products  426 us (25%)
  other arithmetic  166 us (10%)
    psum x1, waiting for transfers between devices, local_layer(): attn_out = lax.psum(attn_part, 'tp')  557 us
    psum x1, waiting for transfers between devices, local_layer(): ffn_out = lax.psum(ffn_part, 'tp')  538 us
    dot_general x1, matrix products, feed_forward(): jnp.einsum('bcf,fd->bcd', activated, w_down, preferred_element_type=jnp.f...  91.7 us
    dot_general x1, matrix products, mix_heads(): jnp.einsum('bhcj,bjhe->bche', scores, values_f32)  72.5 us
    dot_general x1, matrix products, mix_heads(): jnp.einsum('bchk,bjhk->bhcj', queries, keys, preferred_element_type=jnp.f...  67.7 us
    dot_general x1, matrix products, mix_heads(): jnp.einsum('bche,hed->bcd', mixed, w_o.reshape(num_heads, val_dim, w_o.sh...  49.8 us
    reduce_sum x2, other arithmetic, layer_norm(): row_mean = jnp.mean(x_f32, axis=-1, keepdims=True)  44.7 us
    concatenate x1, other arithmetic, rotate_half(): jnp.concatenate([first_half * cos_t - second_half * sin_t, second_half *...  39.3 us
  transfers between devices with their start and end apart: 2, of which 2 were waited for; matrix products, arithmetic and copies ran while one was open for 1% of the time, Pallas kernels for 0%

commit v1 on v0

v1 whole, which is shorter than its diff:
```python
import functools

import jax
import jax.numpy as jnp
from jax import lax
from jax.experimental import pallas as pl
from jax.experimental.pallas import tpu as pltpu
from jax.sharding import PartitionSpec as P


NORM_EPS = 1e-5
GROUP_EPS = 1e-6
ROPE_BASE = 10000.0
TILE = 256
BF16 = jnp.bfloat16
F32 = jnp.float32


def dot(a, b):
    return jnp.dot(a, b, preferred_element_type=F32)


def layer_norm(x_f32, norm_gain, norm_bias):
    row_mean = jnp.mean(x_f32, axis=-1, keepdims=True)
    centered = x_f32 - row_mean
    variance = jnp.mean(centered * centered, axis=-1, keepdims=True)
    return centered * lax.rsqrt(variance + NORM_EPS) * norm_gain + norm_bias


def rope_block(base_ref, step_ref):
    cos_a, sin_a = base_ref[0, 0, 0:1, :], base_ref[0, 0, 1:2, :]
    cos_b, sin_b = step_ref[0], step_ref[1]
    return cos_a * cos_b - sin_a * sin_b, sin_a * cos_b + cos_a * sin_b


def rotate(v, cos_t, sin_t):
    half = v.shape[-1] // 2
    a, b = v[:, :half], v[:, half:]
    return jnp.concatenate([a * cos_t - b * sin_t, b * cos_t + a * sin_t], axis=-1)


def widen(row_table, width):
    return jnp.concatenate([row_table] * (width // row_table.shape[-1]), axis=-1)


def head_block(h, w_ref, state_ref, inner_ref, rows_ref, cos_t, sin_t):
    key_dim, val_dim = state_ref.shape[1], state_ref.shape[2]
    q_raw = dot(h, w_ref[:, :key_dim])
    k_raw = dot(h, w_ref[:, key_dim:2 * key_dim])
    values = dot(h, w_ref[:, 2 * key_dim:2 * key_dim + val_dim]).astype(BF16)
    gates = dot(h, w_ref[:, 2 * key_dim + val_dim:])
    queries = rotate(q_raw, cos_t, sin_t).astype(BF16)
    keys = (rotate(k_raw, cos_t, sin_t) * key_dim ** -0.5).astype(BF16)
    scores = lax.dot_general(queries, keys, (((1,), (1,)), ((), ())), preferred_element_type=F32) * inner_ref[0]
    state = state_ref[0]
    carried = dot(queries, state.astype(BF16)) * widen(rows_ref[0, 0], val_dim)
    retained = dot(scores.astype(BF16), values) + carried
    faded = (keys.astype(F32) * widen(rows_ref[0, 1], key_dim)).astype(BF16)
    update = lax.dot_general(faded, values, (((0,), (0,)), ((), ())), preferred_element_type=F32)
    state_ref[0] = state * widen(rows_ref[0, 2, 0:1], val_dim) + update
    row_mean = jnp.mean(retained, axis=-1, keepdims=True)
    centered = retained - row_mean
    variance = jnp.mean(centered * centered, axis=-1, keepdims=True)
    normed = centered * lax.rsqrt(variance + GROUP_EPS)
    return (gates * lax.logistic(gates) * normed).astype(BF16)


def load_state(in_ref, out_ref):
    @pl.when(pl.program_id(1) == 0)
    def _():
        out_ref[...] = in_ref[...]


def heads_kernel(ids_ref, x_ref, gain_ref, bias_ref, base_ref, step_ref, wa_ref, s_ref, inner_ref, rows_ref, z_ref, state_ref):
    load_state(s_ref, state_ref)
    h = layer_norm(x_ref[0].astype(F32), gain_ref[...], bias_ref[...]).astype(BF16)
    cos_t, sin_t = rope_block(base_ref, step_ref)
    z_ref[0] = head_block(h, wa_ref, state_ref, inner_ref, rows_ref, cos_t, sin_t)


def tail_kernel(ids_ref, x_ref, gain_ref, bias_ref, base_ref, step_ref, wa_ref, s_ref, inner_ref, rows_ref,
                z0_ref, z1_ref, z2_ref, gain2_ref, bias2_ref, wb0, wb1, wb2, wb3, *outs):
    whole_ref, out_ref, state_ref = outs[-3:]
    load_state(s_ref, state_ref)
    h = layer_norm(x_ref[0].astype(F32), gain_ref[...], bias_ref[...]).astype(BF16)
    cos_t, sin_t = rope_block(base_ref, step_ref)
    val_dim, d_model = z0_ref.shape[2], x_ref.shape[2]
    blocks = (wb0, wb1, wb2, wb3)
    mixed = (z0_ref[0], z1_ref[0], z2_ref[0], head_block(h, wa_ref, state_ref, inner_ref, rows_ref, cos_t, sin_t))
    u = sum(dot(z, wb[:val_dim, :d_model]) for z, wb in zip(mixed, blocks))
    x_mid = (x_ref[0].astype(F32) + u.astype(BF16).astype(F32)).astype(BF16)
    h_two = layer_norm(x_mid.astype(F32), gain2_ref[...], bias2_ref[...]).astype(BF16)
    f = jnp.zeros(u.shape, F32)
    for wb in blocks:
        up = dot(h_two, wb[:, d_model:])
        act = (up * 0.5 * (1.0 + lax.erf(up * 0.5 ** 0.5))).astype(BF16)
        f = f + dot(act, wb[val_dim:, :d_model])
    x_out = (x_mid.astype(F32) + f.astype(BF16).astype(F32)).astype(BF16)
    out_ref[0] = x_out
    whole_ref[0] = x_out


def resident(arr):
    return pl.BlockSpec(arr.shape, lambda s, t, ids: (0,) * arr.ndim, pipeline_mode=pl.Buffered(1))


def token_flops(d_model, key_dim, val_dim):
    return 2 * (d_model * (2 * key_dim + 2 * val_dim) + TILE * (key_dim + val_dim) + 2 * key_dim * val_dim)


def head_specs(x, gain, bias, rope_base, rope_step, wa, state, inner, rows):
    state_spec = pl.BlockSpec((1,) + state.shape[1:], lambda s, t, ids: (s, 0, 0))
    specs = [
        pl.BlockSpec((1, TILE, x.shape[2]), lambda s, t, ids: (ids[s], t, 0)),
        resident(gain), resident(bias),
        pl.BlockSpec((1, 1) + rope_base.shape[2:], lambda s, t, ids: (ids[s], t, 0, 0)),
        resident(rope_step), resident(wa), state_spec, resident(inner), resident(rows),
    ]
    return specs, [x, gain, bias, rope_base, rope_step, wa, state, inner, rows], state_spec


def call(body, ids, specs, args, outs, flops, byte_count, aliases):
    n, steps = ids.shape[0], args[0].shape[1] // TILE
    return pl.pallas_call(
        body,
        grid_spec=pltpu.PrefetchScalarGridSpec(num_scalar_prefetch=1, grid=(n, steps), in_specs=specs, out_specs=[spec for spec, _ in outs]),
        out_shape=[shape for _, shape in outs],
        compiler_params=pltpu.CompilerParams(dimension_semantics=("arbitrary", "arbitrary"), vmem_limit_bytes=58 << 20),
        cost_estimate=pl.CostEstimate(flops=n * steps * TILE * flops, bytes_accessed=n * steps * TILE * byte_count, transcendentals=0),
        input_output_aliases=aliases,
    )(ids, *args)


def tile_of(width, offset=0):
    return pl.BlockSpec((1, TILE, width), lambda s, t, ids: (s + offset, t, 0))


def run_heads(ids, *head_args):
    specs, args, state_spec = head_specs(*head_args)
    x, state = head_args[0], head_args[6]
    n, (key_dim, val_dim) = ids.shape[0], state.shape[1:]
    outs = [(tile_of(val_dim), jax.ShapeDtypeStruct((n, x.shape[1], val_dim), BF16)), (state_spec, jax.ShapeDtypeStruct((n, key_dim, val_dim), F32))]
    return call(heads_kernel, ids, specs, args, outs, token_flops(x.shape[2], key_dim, val_dim), 2 * (x.shape[2] + val_dim), {})


def run_tail(ids, whole, offsets, zs, gain2, bias2, wb, *head_args):
    specs, args, state_spec = head_specs(*head_args)
    x, state = head_args[0], head_args[6]
    n, (key_dim, val_dim), d_model = ids.shape[0], state.shape[1:], x.shape[2]
    specs += [tile_of(val_dim, offset) for offset in offsets]
    specs += [resident(arr) for arr in (gain2, bias2, *wb)]
    args += [*zs, gain2, bias2, *wb]
    aliases = {}
    if whole is not None:
        specs.append(pl.BlockSpec(memory_space=pl.ANY))
        args.append(whole)
        aliases = {len(args): 0}
    outs = [(pl.BlockSpec((1, TILE, d_model), lambda s, t, ids: (ids[s], t, 0)), jax.ShapeDtypeStruct(x.shape, BF16)),
            (tile_of(d_model), jax.ShapeDtypeStruct((n, x.shape[1], d_model), BF16)), (state_spec, jax.ShapeDtypeStruct((n, key_dim, val_dim), F32))]
    flops = token_flops(d_model, key_dim, val_dim) + 24 * d_model * val_dim
    return call(tail_kernel, ids, specs, args, outs, flops, 2 * (3 * d_model + 3 * val_dim), aliases)


def rope_tables(start_pos, chunk_len, key_dim):
    half_dim = key_dim // 2
    inv_freq = jnp.power(ROPE_BASE, -jnp.arange(half_dim).astype(F32) / half_dim)
    starts = (start_pos[:, None] + jnp.arange(0, chunk_len, TILE)[None, :]).astype(F32)
    base = starts[:, :, None] * inv_freq
    step = jnp.arange(TILE).astype(F32)[:, None] * inv_freq[None, :]
    return jnp.stack([jnp.cos(base), jnp.sin(base)], axis=2), jnp.stack([jnp.cos(step), jnp.sin(step)])


def decay_tables(head_ids):
    log_gamma = jnp.log1p(-jnp.exp2(-5.0 - head_ids.astype(F32)))[:, None, None]
    step_ids = jnp.arange(TILE)
    gap = step_ids[:, None] - step_ids[None, :]
    inner = jnp.where(gap[None] >= 0, jnp.exp(jnp.maximum(gap, 0).astype(F32)[None] * log_gamma), 0.0)
    lanes = jnp.zeros((1, 1, 128), F32)
    into = jnp.exp((step_ids + 1).astype(F32)[None, :, None] * log_gamma) + lanes
    out_of = jnp.exp((TILE - 1 - step_ids).astype(F32)[None, :, None] * log_gamma) + lanes
    over = jnp.exp(TILE * log_gamma) + jnp.zeros((1, TILE, 128), F32)
    return inner, jnp.stack([into, out_of, over], axis=1)


def solution(mesh):
    n_tp, n_dp = mesh.shape["tp"], mesh.shape["dp"]
    core_pairs = [(i, i ^ 1) for i in range(n_tp)]
    chip_pairs = [(i, i ^ 2) for i in range(n_tp)]
    far_pairs = [(i, i ^ 3) for i in range(n_tp)]

    def local_layer(x_in, start_pos, kv_state, ln1_gain, ln1_bias, w_q, w_k, w_v, w_g, w_o, ln2_gain, ln2_bias, w_up, w_down):
        to_core = functools.partial(lax.ppermute, axis_name="tp", perm=core_pairs)
        to_chip = functools.partial(lax.ppermute, axis_name="tp", perm=chip_pairs)
        to_far = functools.partial(lax.ppermute, axis_name="tp", perm=far_pairs)
        tp = lax.axis_index("tp")
        group = lax.axis_index("dp")
        chip, core = tp // 2, tp % 2
        other = 1 - core
        chunk_len = x_in.shape[1]
        states = kv_state[:, 0]
        key_dim, _ = states.shape[1:]

        def head_weights(part):
            return jnp.concatenate([part(w_q), part(w_k), part(w_v), part(w_g)], axis=1)

        def mlp_weights(part):
            pieces = [part(w_o), part(w_down), part(w_up)]
            return jnp.concatenate([jnp.concatenate(pieces[:2], axis=0), pieces[2]], axis=1)

        def quarter(w):
            rows = w.shape[0] // n_dp
            return lax.dynamic_slice_in_dim(w, group * rows, rows, axis=0)

        def gather(part):
            return lax.all_gather(part, "dp", axis=0, tiled=True)

        def pick(arr, i, n=1):
            return lax.dynamic_slice_in_dim(arr, i, n, axis=0)

        single, twice = 2 * chip + core, 4 + 2 * core
        single_o, twice_o = 2 * chip + other, 4 + 2 * other
        ids = jnp.stack([single, twice, twice + 1]).astype(jnp.int32)

        w_heads, w_mlp = head_weights(lambda w: w), mlp_weights(lambda w: w)
        wa_part = to_chip(head_weights(quarter))
        su_pair = to_chip(pick(states, 2 * (1 - chip), 2))
        wb_part = to_chip(quarter(w_mlp))
        st_pair = to_chip(states[4:8])
        wa_core = to_core(w_heads)
        s_core = to_core(jnp.concatenate([pick(states, single_o), pick(states, twice_o, 2)]))
        wb_core = to_core(w_mlp)

        row2 = lambda v: v.reshape(1, -1)
        rope_base, rope_step = rope_tables(start_pos, chunk_len, key_dim)
        inner, row_decay = decay_tables(jnp.stack([tp, tp ^ 1, tp ^ 2, tp ^ 3]))
        common = (x_in, row2(ln1_gain), row2(ln1_bias), rope_base, rope_step)

        def tables(i):
            return inner[i:i + 1], row_decay[i:i + 1]

        s_own = jnp.concatenate([pick(states, single), pick(states, twice, 2)])
        z_own, new_own = run_heads(ids, *common, w_heads, s_own, *tables(0))
        z_own, wa_core, s_core, wa_part, wb_part = lax.optimization_barrier((z_own, wa_core, s_core, wa_part, wb_part))
        wa_chip, wb_chip = gather(wa_part), gather(wb_part)
        z_core, new_core = run_heads(ids, *common, wa_core, s_core, *tables(1))
        got_core = to_core(new_core)

        z_core, wa_chip, wb_chip, su_pair, st_pair = lax.optimization_barrier((z_core, wa_chip, wb_chip, su_pair, st_pair))
        wa_far, wb_far = to_core(wa_chip), to_core(wb_chip)
        s_far = to_core(jnp.concatenate([pick(su_pair, other), pick(st_pair, 2 * other, 2)]))
        z_chip, new_chip = run_heads(ids[:1], *common, wa_chip, pick(su_pair, core), *tables(2))
        z_chip, wa_far, wb_far, wb_core, s_far = lax.optimization_barrier((z_chip, wa_far, wb_far, wb_core, s_far))

        mlp_args = (row2(ln2_gain), row2(ln2_bias), (w_mlp, wb_core, wb_chip, wb_far), *common, wa_far)
        whole, x_single, new_far = run_tail(ids[:1], None, (0, 0, 0), (z_own, z_core, z_chip), *mlp_args, s_far[:1], *tables(3))
        x_single_chip = to_chip(x_single)
        x_single_core = to_core(x_single)
        got_chip = to_chip(new_chip)
        got_far = to_far(new_far)
        whole, st_own, z_own = lax.optimization_barrier((whole, pick(st_pair, 2 * core, 2), z_own))
        z_chip, _ = run_heads(ids[1:], *common, wa_chip, st_own, *tables(2))
        whole, x_a, _ = run_tail(ids[1:2], whole, (1, 1, 0), (z_own, z_core, z_chip), *mlp_args, s_far[1:2], *tables(3))
        x_a_core = to_core(x_a)
        whole, x_b, _ = run_tail(ids[2:], whole, (2, 2, 1), (z_own, z_core, z_chip), *mlp_args, s_far[2:], *tables(3))
        x_b_core = to_core(x_b)
        x_single_far = to_core(x_single_chip)

        for block, i in ((x_single_core, single_o), (x_single_chip, 2 * (1 - chip) + core), (x_a_core, twice_o), (x_single_far, 2 * (1 - chip) + other), (x_b_core, twice_o + 1)):
            whole = lax.dynamic_update_slice_in_dim(whole, block, i, axis=0)

        def by_core(mine, theirs):
            return jnp.where(core == 0, jnp.concatenate([mine, theirs]), jnp.concatenate([theirs, mine]))

        mine = new_own
        near_pair, far_pair = by_core(mine[:1], got_core[:1]), by_core(got_chip, got_far)
        singles = jnp.where(chip == 0, jnp.concatenate([near_pair, far_pair]), jnp.concatenate([far_pair, near_pair]))
        new_states = jnp.concatenate([singles, by_core(mine[1:], got_core[1:])])
        return whole, new_states[:, None]

    in_specs = (P("dp", None, None), P("dp"), P("dp", "tp", None, None), P(), P(), P(None, "tp"), P(None, "tp"), P(None, "tp"), P(None, "tp"), P("tp", None), P(), P(), P(None, "tp"), P("tp", None))
    out_specs = (P("dp", None, None), P("dp", "tp", None, None))
    return jax.shard_map(local_layer, mesh=mesh, in_specs=in_specs, out_specs=out_specs, check_vma=False)
```

time: 1710 us -> 454 us (0.27)
  waiting for transfers between devices: 1100 us -> 64 us
  matrix products: 426 us -> 0 us
  Pallas kernels: 0 us -> 297 us
  other arithmetic: 166 us -> 16.2 us
  local copies, waits for them, and re-layouts: 0.1 us -> 50.4 us
    psum x2 -> x0, waiting for transfers between devices: 1100 us -> none  [the longest x1 557 us: local_layer(): attn_out = lax.psum(attn_part, 'tp')]
    dot_general x10 -> x0, matrix products: 426 us -> none  [the longest x1 91.7 us: feed_forward(): jnp.einsum('bcf,fd->bcd', activated, w_down, preferred_element_type=jnp.f...]
    pallas_call x0 -> x7, Pallas kernels: none -> 297 us  [call(): pl.pallas_call(body, grid_spec=pltpu.PrefetchScalarGridSpec(num_scalar_pr...]
    reduce_sum x5 -> x0, other arithmetic: 84.3 us -> none  [the longest x2 44.7 us: layer_norm(): row_mean = jnp.mean(x_f32, axis=-1, keepdims=True)]
    ppermute x0 -> x18, waiting for transfers between devices: none -> 53 us  [the longest x1 22.4 us: local_layer(): su_pair = to_chip(pick(states, 2 * (1 - chip), 2))]
    convert_element_type x2 -> x4, other arithmetic: 33.4 us -> 0.11 us  [the longest x1 0.07 us: rope_tables(): (start_pos[:, None] + jnp.arange(0, chunk_len, TILE)[None, :]).astype(F32)]
    concatenate x1 -> x5, other arithmetic: 39.3 us -> 6.39 us  [the longest x1 2.62 us: local_layer(): s_own = jnp.concatenate([pick(states, single), pick(states, twice, 2)])]
    dynamic_update_slice x0 -> x5, local copies, waits for them, and re-layouts: none -> 23.2 us  [local_layer(): whole = lax.dynamic_update_slice_in_dim(whole, block, i, axis=0)]
  transfers between devices with their start and end apart: 2 -> 20, of which waited for: 2 -> 5; matrix products, arithmetic and copies ran while one was open for 1% -> 13% of each run, Pallas kernels for 0% -> 66%
where the time goes in v1:
time: 454 us; the launch traced here: 453 us
  Pallas kernels  297 us (65%)
  waiting for transfers between devices  64 us (14%)
  local copies, waits for them, and re-layouts  50.4 us (11%)
  other arithmetic  16.2 us (4%)
  between operations  14.4 us (3%)
  starting transfers between devices  11.4 us (3%)
    pallas_call x7, Pallas kernels, call(): pl.pallas_call(body, grid_spec=pltpu.PrefetchScalarGridSpec(num_scalar_pr...  297 us
    dynamic_update_slice x5, local copies, waits for them, and re-layouts, local_layer(): whole = lax.dynamic_update_slice_in_dim(whole, block, i, axis=0)  23.2 us
    ppermute x1, waiting for transfers between devices, local_layer(): su_pair = to_chip(pick(states, 2 * (1 - chip), 2))  22.4 us
    ppermute x1, waiting for transfers between devices, local_layer(): got_chip = to_chip(new_chip)  12.5 us
    ppermute x1, waiting for transfers between devices, local_layer(): got_far = to_far(new_far)  11.4 us
    all_gather x2, waiting for transfers between devices, gather(): return lax.all_gather(part, 'dp', axis=0, tiled=True)  10.4 us
    dynamic_slice x4, local copies, waits for them, and re-layouts, pick(): return lax.dynamic_slice_in_dim(arr, i, n, axis=0)  10.4 us
  transfers between devices with their start and end apart: 20, of which 5 were waited for; matrix products, arithmetic and copies ran while one was open for 13% of the time, Pallas kernels for 66%

profile of v1, /device:TPU:0, one launch (start us, length us, event | category | flops | bytes accessed | tf_op | source)
XLA Modules:
  0.0 453.4 jit_solution(1945977818965382012)
XLA Ops:
  11.1 3.2 collective-permute-start.2
  16.4 3.5 dynamic-slice_bitcast_fusion
  30.5 2.6 pad_maximum_fusion.1.s_ref
  37.0 45.5 %shard_map.149 = (bf16[3,2048,512]{2,1,0:T(8,128)(2,1)}, f32[3,256,512]{2,1,0:T(8,128)}) custom-call(s32[3]{0:T(128)} %pad_add_fusion.ids_ref, bf16[8,2048,1024]{2,1,0:T(8,128)(2,1)} %x_ref.13, f32[1,1024]{1,0:T(1,128)} %bitcast.31, f32[1,1024]{1,0:T(1,128)} %bitcast.38, f32[8,8,2,128]{3,2,1,0:T(2,128)} %pad_maximum_fusion.7.base_ref, ...), custom_call_target="tpu_custom_call" | custom-call | flops 24964497408 | bytes 18874368 | tf_op jit(solution)/shard_map/pallas_call | solution.py:124
  85.6 2.1 collective-permute-start.5
  87.7 45.9 %shard_map.150 = (bf16[3,2048,512]{2,1,0:T(8,128)(2,1)}, f32[3,256,512]{2,1,0:T(8,128)}) custom-call(s32[3]{0:T(128)} %pad_add_fusion.ids_ref, bf16[8,2048,1024]{2,1,0:T(8,128)(2,1)} %x_ref.13, f32[1,1024]{1,0:T(1,128)} %bitcast.32, f32[1,1024]{1,0:T(1,128)} %bitcast.39, f32[8,8,2,128]{3,2,1,0:T(2,128)} %pad_maximum_fusion.7.base_ref, ...), custom_call_target="tpu_custom_call" | custom-call | flops 24964497408 | bytes 18874368 | tf_op jit(solution)/shard_map/pallas_call | solution.py:124
  133.7 22.4 %collective-permute-done.4 = f32[2,256,512]{2,1,0:T(8,128)} collective-permute-done((f32[2,256,512]{2,1,0:T(8,128)}, f32[2,256,512]{2,1,0:T(8,128)}, u32[]{:S(2)}, u32[]{:S(2)}) %collective-permute-start.4) | collective-permute-done | bytes 1048608 | tf_op jit(solution)/shard_map/ppermute | solution.py:226
  156.1 10.4 %all-gather.5.cloned.1.call-done.wb2 = bf16[1024,1536]{1,0:T(8,128)(2,1)} async-done(((bf16[256,1536]{1,0:T(8,128)(2,1)}), bf16[1024,1536]{1,0:T(8,128)(2,1)}) %all-gather.5.cloned.1.call-update) | async-done | bytes 3145744 | tf_op jit(solution)/shard_map/all_gather | solution.py:215
  167.0 2.1 constant_dynamic-slice_fusion.2
  169.1 2.8 constant_dynamic-slice_fusion
  174.3 16.9 %shard_map.151 = (bf16[1,2048,512]{2,1,0:T(8,128)(2,1)}, f32[1,256,512]{2,1,0:T(8,128)}) custom-call(s32[1]{0:T(128)} %bitcast.4.ids_ref, bf16[8,2048,1024]{2,1,0:T(8,128)(2,1)} %x_ref.13, f32[1,1024]{1,0:T(1,128)} %bitcast.33, f32[1,1024]{1,0:T(1,128)} %bitcast.40, f32[8,8,2,128]{3,2,1,0:T(2,128)} %pad_maximum_fusion.7.base_ref, ...), custom_call_target="tpu_custom_call" | custom-call | flops 8321499136 | bytes 6291456 | tf_op jit(solution)/shard_map/pallas_call | solution.py:124
  192.4 52.2 %shard_map.152 = (bf16[8,2048,1024]{2,1,0:T(8,128)(2,1)}, bf16[1,2048,1024]{2,1,0:T(8,128)(2,1)}, f32[1,256,512]{2,1,0:T(8,128)}) custom-call(s32[1]{0:T(128)} %bitcast.4.ids_ref, bf16[8,2048,1024]{2,1,0:T(8,128)(2,1)} %x_ref.13, f32[1,1024]{1,0:T(1,128)} %bitcast.34, f32[1,1024]{1,0:T(1,128)} %bitcast.41, f32[8,8,2,128]{3,2,1,0:T(2,128)} %pad_maximum_fusion.7.base_ref, ...), custom_call_target="tpu_custom_call" | custom-call | flops 34091302912 | bytes 18874368 | tf_op jit(solution)/shard_map/pallas_call | solution.py:124
  246.1 31.6 %shard_map.153 = (bf16[2,2048,512]{2,1,0:T(8,128)(2,1)}, f32[2,256,512]{2,1,0:T(8,128)}) custom-call(s32[2]{0:T(128)} %pad_add_fusion.1.ids_ref, bf16[8,2048,1024]{2,1,0:T(8,128)(2,1)} %x_ref.13, f32[1,1024]{1,0:T(1,128)} %bitcast.35, f32[1,1024]{1,0:T(1,128)} %bitcast.42, f32[8,8,2,128]{3,2,1,0:T(2,128)} %pad_maximum_fusion.7.base_ref, ...), custom_call_target="tpu_custom_call" | custom-call | flops 16642998272 | bytes 12582912 | tf_op jit(solution)/shard_map/pallas_call | solution.py:124
  277.7 52.6 %shard_map.154 = (bf16[8,2048,1024]{2,1,0:T(8,128)(2,1)}, bf16[1,2048,1024]{2,1,0:T(8,128)(2,1)}, f32[1,256,512]{2,1,0:T(8,128)}) custom-call(s32[1]{0:T(128)} %bitcast.5.ids_ref, bf16[8,2048,1024]{2,1,0:T(8,128)(2,1)} %x_ref.13, f32[1,1024]{1,0:T(1,128)} %bitcast.36, f32[1,1024]{1,0:T(1,128)} %bitcast.43, ...), custom_call_target="tpu_custom_call", output_to_operand_aliasing={{0}: (19, {})} | custom-call | flops 34091302912 | bytes 18874368 | tf_op jit(solution)/shard_map/pallas_call | solution.py:124
  330.9 6.7 %collective-permute-done.11 = bf16[1,2048,1024]{2,1,0:T(8,128)(2,1)} collective-permute-done((bf16[1,2048,1024]{2,1,0:T(8,128)(2,1)}, bf16[1,2048,1024]{2,1,0:T(8,128)(2,1)}, u32[]{:S(2)}, u32[]{:S(2)}) %collective-permute-start.11) | collective-permute-done | bytes 4194336 | tf_op jit(solution)/shard_map/ppermute | solution.py:256
  337.5 52.4 %shard_map.155 = (bf16[8,2048,1024]{2,1,0:T(8,128)(2,1)}, bf16[1,2048,1024]{2,1,0:T(8,128)(2,1)}, f32[1,256,512]{2,1,0:T(8,128)}) custom-call(s32[1]{0:T(128)} %bitcast.ids_ref, bf16[8,2048,1024]{2,1,0:T(8,128)(2,1)} %x_ref.13, f32[1,1024]{1,0:T(1,128)} %bitcast.37, f32[1,1024]{1,0:T(1,128)} %bitcast.44, ...), custom_call_target="tpu_custom_call", output_to_operand_aliasing={{0}: (19, {})} | custom-call | flops 34091302912 | bytes 18874368 | tf_op jit(solution)/shard_map/pallas_call | solution.py:124
  391.9 12.5 %collective-permute-done.16 = f32[1,256,512]{2,1,0:T(8,128)} collective-permute-done((f32[1,256,512]{2,1,0:T(8,128)S(1)}, f32[1,256,512]{2,1,0:T(8,128)}, u32[]{:S(2)}, u32[]{:S(2)}) %collective-permute-start.16) | collective-permute-done | bytes 524320 | tf_op jit(solution)/shard_map/ppermute | solution.py:258
  407.5 11.4 %collective-permute-done.17 = f32[1,256,512]{2,1,0:T(8,128)} collective-permute-done((f32[1,256,512]{2,1,0:T(8,128)}, f32[1,256,512]{2,1,0:T(8,128)}, u32[]{:S(2)}, u32[]{:S(2)}) %collective-permute-start.17) | collective-permute-done | bytes 524320 | tf_op jit(solution)/shard_map/ppermute | solution.py:259
  420.9 2.5 maximum_bitcast_fusion
  423.4 4.6 %constant_dynamic-update-slice_fusion.8 = bf16[8,2048,1024]{2,1,0:T(8,128)(2,1)} fusion(bf16[8,2048,1024]{2,1,0:T(8,128)(2,1)} %get-tuple-element.58, bf16[1,2048,1024]{2,1,0:T(8,128)(2,1)} %collective-permute-done.10, s32[]{:T(128)S(6)} %select_n.91), kind=kLoop, calls=%fused_computation.35 | loop fusion | bytes 8388612 | tf_op jit(solution)/shard_map/dynamic_update_slice | solution.py:269
  428.0 4.6 %constant_dynamic-update-slice_fusion.7 = bf16[8,2048,1024]{2,1,0:T(8,128)(2,1)} fusion(bf16[8,2048,1024]{2,1,0:T(8,128)(2,1)} %constant_dynamic-update-slice_fusion.8, bf16[1,2048,1024]{2,1,0:T(8,128)(2,1)} %collective-permute-done.11, s32[]{:T(128)S(6)} %select_n.99), kind=kLoop, calls=%fused_computation.34 | loop fusion | bytes 8388612 | tf_op jit(solution)/shard_map/dynamic_update_slice | solution.py:269
  432.7 4.6 %constant_dynamic-update-slice_fusion.6 = bf16[8,2048,1024]{2,1,0:T(8,128)(2,1)} fusion(bf16[8,2048,1024]{2,1,0:T(8,128)(2,1)} %constant_dynamic-update-slice_fusion.7, bf16[1,2048,1024]{2,1,0:T(8,128)(2,1)} %collective-permute-done.12, s32[]{:T(128)S(6)} %select_n.92), kind=kLoop, calls=%fused_computation.33 | loop fusion | bytes 8388612 | tf_op jit(solution)/shard_map/dynamic_update_slice | solution.py:269
  437.3 4.6 %constant_dynamic-update-slice_fusion.5 = bf16[8,2048,1024]{2,1,0:T(8,128)(2,1)} fusion(bf16[8,2048,1024]{2,1,0:T(8,128)(2,1)} %constant_dynamic-update-slice_fusion.6, bf16[1,2048,1024]{2,1,0:T(8,128)(2,1)} %collective-permute-done.13, s32[]{:T(128)S(6)} %select_n.100), kind=kLoop, calls=%fused_computation.32 | loop fusion | bytes 8388612 | tf_op jit(solution)/shard_map/dynamic_update_slice | solution.py:269
  442.0 4.6 %constant_dynamic-update-slice_fusion.4 = bf16[8,2048,1024]{2,1,0:T(8,128)(2,1)} fusion(bf16[8,2048,1024]{2,1,0:T(8,128)(2,1)} %constant_dynamic-update-slice_fusion.5, bf16[1,2048,1024]{2,1,0:T(8,128)(2,1)} %collective-permute-done.14, s32[]{:T(128)S(6)} %select_n.101), kind=kLoop, calls=%fused_computation.31 | loop fusion | bytes 8388612 | tf_op jit(solution)/shard_map/dynamic_update_slice | solution.py:269
  (103 shorter events, 36.7 us)
Async XLA Ops:
  7.2 148.9 %all-gather.3.cloned.1.call-start = ((), (), s32[]{:S(2)}) async-start(), calls=%async_computation | async-start | bytes 3932160 | tf_op jit(solution)/shard_map/all_gather | solution.py:215
  11.1 71.4 %collective-permute-start.2 = (bf16[256,1536]{1,0:T(8,128)(2,1)}, bf16[256,1536]{1,0:T(8,128)(2,1)}, u32[]{:S(2)}, u32[]{:S(2)}) collective-permute-start(bf16[256,1536]{1,0:T(8,128)(2,1)} %pad_maximum_fusion.5), channel_id=1, source_target_pairs={{0,2},{1,3},{2,0},{3,1},{4,6},{5,7},{6,4},{7,5},{8,10},{9,11},{10,... | collective-permute-start | bytes 2359304 | tf_op jit(solution)/shard_map/ppermute | solution.py:225
  21.2 61.3 %collective-permute-start.1 = (f32[3,256,512]{2,1,0:T(8,128)}, f32[3,256,512]{2,1,0:T(8,128)}, u32[]{:S(2)}, u32[]{:S(2)}) collective-permute-start(f32[3,256,512]{2,1,0:T(8,128)} %pad_maximum_fusion.3), channel_id=1, source_target_pairs={{0,1},{1,0},{2,3},{3,2},{4,5},{5,4},{6,7},{7,6},{8,9},{9,8},{10,11... | collective-permute-start | bytes 4718600 | tf_op jit(solution)/shard_map/ppermute | solution.py:230
  22.5 60.8 %copy-start = (bf16[1024,1536]{1,0:T(8,128)(2,1)}, bf16[1024,1536]{1,0:T(8,128)(2,1)S(1)}, u32[]{:S(2)}) copy-start(bf16[1024,1536]{1,0:T(8,128)(2,1)S(1)} %pad_maximum_fusion.wb0) | copy-start | bytes 9437188
  23.5 3.9 copy-start.9
  23.5 59.0 %collective-permute-start.3 = (bf16[256,1536]{1,0:T(8,128)(2,1)}, bf16[256,1536]{1,0:T(8,128)(2,1)}, u32[]{:S(2)}, u32[]{:S(2)}) collective-permute-start(bf16[256,1536]{1,0:T(8,128)(2,1)} %constant_dynamic-slice_fusion.4), channel_id=1, source_target_pairs={{0,2},{1,3},{2,0},{3,1},{4,6},{5,7},{6,4},{7,5},{8,10},{9,11},{10,... | collective-permute-start | bytes 2359304 | tf_op jit(solution)/shard_map/ppermute | solution.py:227
  27.2 55.3 %collective-permute-start = (bf16[1024,1536]{1,0:T(8,128)(2,1)}, bf16[1024,1536]{1,0:T(8,128)(2,1)}, u32[]{:S(2)}, u32[]{:S(2)}) collective-permute-start(bf16[1024,1536]{1,0:T(8,128)(2,1)} %constant_dynamic-update-slice_fusion.wa_ref), channel_id=1, source_target_pairs={{0,1},{1,0},{2,3},{3,2},{4,5},{5,4},{6,7},{7,6},{8,9},{9,8},{10,11... | collective-permute-start | bytes 9437192 | tf_op jit(solution)/shard_map/ppermute | solution.py:229
  82.6 83.9 %all-gather.5.cloned.1.call-start = ((), (), s32[]{:S(2)}) async-start(), calls=%async_computation.1 | async-start | bytes 3932160 | tf_op jit(solution)/shard_map/all_gather | solution.py:215
  83.3 107.8 %collective-permute-start.8 = (bf16[1024,1536]{1,0:T(8,128)(2,1)S(1)}, bf16[1024,1536]{1,0:T(8,128)(2,1)}, u32[]{:S(2)}, u32[]{:S(2)}) collective-permute-start(bf16[1024,1536]{1,0:T(8,128)(2,1)S(1)} %pad_maximum_fusion.wb0), channel_id=1, source_target_pairs={{0,1},{1,0},{2,3},{3,2},{4,5},{5,4},{6,7},{7,6},{8,9},{9,8},{10,11... | collective-permute-start | bytes 9437192 | tf_op jit(solution)/shard_map/ppermute | solution.py:231
  85.6 70.5 %collective-permute-start.5 = (f32[4,256,512]{2,1,0:T(8,128)S(1)}, f32[4,256,512]{2,1,0:T(8,128)}, u32[]{:S(2)}, u32[]{:S(2)}) collective-permute-start(f32[4,256,512]{2,1,0:T(8,128)S(1)} %slice_bitcast_fusion), channel_id=1, source_target_pairs={{0,2},{1,3},{2,0},{3,1},{4,6},{5,7},{6,4},{7,5},{8,10},{9,11},{10,... | collective-permute-start | bytes 6291464 | tf_op jit(solution)/shard_map/ppermute | solution.py:228
  87.7 68.4 %collective-permute-start.4 = (f32[2,256,512]{2,1,0:T(8,128)}, f32[2,256,512]{2,1,0:T(8,128)}, u32[]{:S(2)}, u32[]{:S(2)}) collective-permute-start(f32[2,256,512]{2,1,0:T(8,128)} %get-tuple-element.72), channel_id=1, source_target_pairs={{0,2},{1,3},{2,0},{3,1},{4,6},{5,7},{6,4},{7,5},{8,10},{9,11},{10,... | collective-permute-start | bytes 3145736 | tf_op jit(solution)/shard_map/ppermute | solution.py:226
  166.5 24.7 %collective-permute-start.6 = (bf16[1024,1536]{1,0:T(8,128)(2,1)}, bf16[1024,1536]{1,0:T(8,128)(2,1)}, u32[]{:S(2)}, u32[]{:S(2)}) collective-permute-start(bf16[1024,1536]{1,0:T(8,128)(2,1)} %all-gather.3.cloned.1.call-done.wa_ref), channel_id=1, source_target_pairs={{0,1},{1,0},{2,3},{3,2},{4,5},{5,4},{6,7},{7,6},{8,9},{9,8},{10,11... | collective-permute-start | bytes 9437192 | tf_op jit(solution)/shard_map/ppermute | solution.py:249
  166.5 24.7 %collective-permute-start.7 = (bf16[1024,1536]{1,0:T(8,128)(2,1)}, bf16[1024,1536]{1,0:T(8,128)(2,1)}, u32[]{:S(2)}, u32[]{:S(2)}) collective-permute-start(bf16[1024,1536]{1,0:T(8,128)(2,1)} %all-gather.5.cloned.1.call-done.wb2), channel_id=1, source_target_pairs={{0,1},{1,0},{2,3},{3,2},{4,5},{5,4},{6,7},{7,6},{8,9},{9,8},{10,11... | collective-permute-start | bytes 9437192 | tf_op jit(solution)/shard_map/ppermute | solution.py:249
  173.1 18.0 %collective-permute-start.9 = (f32[3,256,512]{2,1,0:T(8,128)}, f32[3,256,512]{2,1,0:T(8,128)S(1)}, u32[]{:S(2)}, u32[]{:S(2)}) collective-permute-start(f32[3,256,512]{2,1,0:T(8,128)} %pad_maximum_fusion.4), channel_id=1, source_target_pairs={{0,1},{1,0},{2,3},{3,2},{4,5},{5,4},{6,7},{7,6},{8,9},{9,8},{10,11... | collective-permute-start | bytes 4718600 | tf_op jit(solution)/shard_map/ppermute | solution.py:250
  173.8 216.6 %collective-permute-start.15 = (f32[3,256,512]{2,1,0:T(8,128)}, f32[3,256,512]{2,1,0:T(8,128)}, u32[]{:S(2)}, u32[]{:S(2)}) collective-permute-start(f32[3,256,512]{2,1,0:T(8,128)} %get-tuple-element.63), channel_id=1, source_target_pairs={{0,1},{1,0},{2,3},{3,2},{4,5},{5,4},{6,7},{7,6},{8,9},{9,8},{10,11... | collective-permute-start | bytes 4718600 | tf_op jit(solution)/shard_map/ppermute | solution.py:246
  244.6 92.9 %collective-permute-start.11 = (bf16[1,2048,1024]{2,1,0:T(8,128)(2,1)}, bf16[1,2048,1024]{2,1,0:T(8,128)(2,1)}, u32[]{:S(2)}, u32[]{:S(2)}) collective-permute-start(bf16[1,2048,1024]{2,1,0:T(8,128)(2,1)} %get-tuple-element.59), channel_id=1, source_target_pairs={{0,2},{1,3},{2,0},{3,1},{4,6},{5,7},{6,4},{7,5},{8,10},{9,11},{10,... | collective-permute-start | bytes 12582920 | tf_op jit(solution)/shard_map/ppermute | solution.py:256
  246.1 177.3 %collective-permute-start.10 = (bf16[1,2048,1024]{2,1,0:T(8,128)(2,1)}, bf16[1,2048,1024]{2,1,0:T(8,128)(2,1)}, u32[]{:S(2)}, u32[]{:S(2)}) collective-permute-start(bf16[1,2048,1024]{2,1,0:T(8,128)(2,1)} %get-tuple-element.59), channel_id=1, source_target_pairs={{0,1},{1,0},{2,3},{3,2},{4,5},{5,4},{6,7},{7,6},{8,9},{9,8},{10,11... | collective-permute-start | bytes 12582920 | tf_op jit(solution)/shard_map/ppermute | solution.py:257
  330.3 102.3 %collective-permute-start.12 = (bf16[1,2048,1024]{2,1,0:T(8,128)(2,1)}, bf16[1,2048,1024]{2,1,0:T(8,128)(2,1)}, u32[]{:S(2)}, u32[]{:S(2)}) collective-permute-start(bf16[1,2048,1024]{2,1,0:T(8,128)(2,1)} %get-tuple-element.60), channel_id=1, source_target_pairs={{0,1},{1,0},{2,3},{3,2},{4,5},{5,4},{6,7},{7,6},{8,9},{9,8},{10,11... | collective-permute-start | bytes 12582920 | tf_op jit(solution)/shard_map/ppermute | solution.py:263
  337.5 99.8 %collective-permute-start.13 = (bf16[1,2048,1024]{2,1,0:T(8,128)(2,1)}, bf16[1,2048,1024]{2,1,0:T(8,128)(2,1)}, u32[]{:S(2)}, u32[]{:S(2)}) collective-permute-start(bf16[1,2048,1024]{2,1,0:T(8,128)(2,1)} %collective-permute-done.11), channel_id=1, source_target_pairs={{0,1},{1,0},{2,3},{3,2},{4,5},{5,4},{6,7},{7,6},{8,9},{9,8},{10,11... | collective-permute-start | bytes 12582920 | tf_op jit(solution)/shard_map/ppermute | solution.py:266
  337.5 52.9 %copy-start.10 = (f32[1,256,512]{2,1,0:T(8,128)S(1)}, f32[1,256,512]{2,1,0:T(8,128)}, u32[]{:S(2)}) copy-start(f32[1,256,512]{2,1,0:T(8,128)} %get-tuple-element.64) | copy-start | bytes 1572868
  337.5 67.2 %copy-start.3 = (f32[3,256,512]{2,1,0:T(8,128)S(1)}, f32[3,256,512]{2,1,0:T(8,128)}, u32[]{:S(2)}) copy-start(f32[3,256,512]{2,1,0:T(8,128)} %get-tuple-element.62) | copy-start | bytes 4718596
  389.9 52.1 %collective-permute-start.14 = (bf16[1,2048,1024]{2,1,0:T(8,128)(2,1)}, bf16[1,2048,1024]{2,1,0:T(8,128)(2,1)}, u32[]{:S(2)}, u32[]{:S(2)}) collective-permute-start(bf16[1,2048,1024]{2,1,0:T(8,128)(2,1)} %get-tuple-element.61), channel_id=1, source_target_pairs={{0,1},{1,0},{2,3},{3,2},{4,5},{5,4},{6,7},{7,6},{8,9},{9,8},{10,11... | collective-permute-start | bytes 12582920 | tf_op jit(solution)/shard_map/ppermute | solution.py:265
  390.4 14.0 %collective-permute-start.16 = (f32[1,256,512]{2,1,0:T(8,128)S(1)}, f32[1,256,512]{2,1,0:T(8,128)}, u32[]{:S(2)}, u32[]{:S(2)}) collective-permute-start(f32[1,256,512]{2,1,0:T(8,128)S(1)} %copy-done.10), channel_id=1, source_target_pairs={{0,2},{1,3},{2,0},{3,1},{4,6},{5,7},{6,4},{7,5},{8,10},{9,11},{10,... | collective-permute-start | bytes 1572872 | tf_op jit(solution)/shard_map/ppermute | solution.py:258
  404.4 14.5 %collective-permute-start.17 = (f32[1,256,512]{2,1,0:T(8,128)}, f32[1,256,512]{2,1,0:T(8,128)}, u32[]{:S(2)}, u32[]{:S(2)}) collective-permute-start(f32[1,256,512]{2,1,0:T(8,128)} %get-tuple-element.65), channel_id=1, source_target_pairs={{0,3},{1,2},{2,1},{3,0},{4,7},{5,6},{6,5},{7,4},{8,11},{9,10},{10,... | collective-permute-start | bytes 1572872 | tf_op jit(solution)/shard_map/ppermute | solution.py:259
  (7 other events, 17.9 us)
Sparse Core Ops, SparseCore 0:
  82.7 41.8 all-gather.2
  126.4 40.0 all-gather.4

commit v2 on v0

v2 whole, which is shorter than its diff:
```python
import functools

import jax
import jax.numpy as jnp
from jax import lax
from jax.experimental import pallas as pl
from jax.experimental.pallas import tpu as pltpu
from jax.sharding import PartitionSpec as P


NORM_EPS = 1e-5
GROUP_EPS = 1e-6
ROPE_BASE = 10000.0
TILE = 256
BF16 = jnp.bfloat16
F32 = jnp.float32
ANY = pl.BlockSpec(memory_space=pl.ANY)


def dot(a, b):
    return jnp.dot(a, b, preferred_element_type=F32)


def layer_norm(x_f32, norm_gain, norm_bias):
    row_mean = jnp.mean(x_f32, axis=-1, keepdims=True)
    centered = x_f32 - row_mean
    variance = jnp.mean(centered * centered, axis=-1, keepdims=True)
    return centered * lax.rsqrt(variance + NORM_EPS) * norm_gain + norm_bias


def rotate(v, cos_t, sin_t):
    half = v.shape[-1] // 2
    a, b = v[:, :half], v[:, half:]
    return jnp.concatenate([a * cos_t - b * sin_t, b * cos_t + a * sin_t], axis=-1)


def widen(row_table, width):
    return jnp.concatenate([row_table] * (width // row_table.shape[-1]), axis=-1)


def decay_row(consts_ref, head):
    return consts_ref[5:6, 128 * head:128 * (head + 1)]


def fill_decays(consts_ref, heads, inner_ref, rows_ref):
    gap = lax.broadcasted_iota(jnp.int32, (TILE, TILE), 0) - lax.broadcasted_iota(jnp.int32, (TILE, TILE), 1)
    row = lax.broadcasted_iota(jnp.int32, (TILE, 128), 0)
    for i, head in enumerate(heads):
        log_gamma = decay_row(consts_ref, head)
        inner_ref[i] = jnp.where(gap >= 0, jnp.exp(jnp.maximum(gap, 0).astype(F32) * widen(log_gamma, TILE)), 0.0)
        rows_ref[i, 0] = jnp.exp((row + 1).astype(F32) * log_gamma)
        rows_ref[i, 1] = jnp.exp((TILE - 1 - row).astype(F32) * log_gamma)


def head_block(h, w_ref, s_ref, inner, rows_ref, over, cos_t, sin_t):
    key_dim, val_dim = s_ref.shape
    q_raw = dot(h, w_ref[:, :key_dim])
    k_raw = dot(h, w_ref[:, key_dim:2 * key_dim])
    values = dot(h, w_ref[:, 2 * key_dim:2 * key_dim + val_dim]).astype(BF16)
    gates = dot(h, w_ref[:, 2 * key_dim + val_dim:])
    queries = rotate(q_raw, cos_t, sin_t).astype(BF16)
    keys = (rotate(k_raw, cos_t, sin_t) * key_dim ** -0.5).astype(BF16)
    scores = lax.dot_general(queries, keys, (((1,), (1,)), ((), ())), preferred_element_type=F32) * inner
    state = s_ref[...]
    carried = dot(queries, state.astype(BF16)) * widen(rows_ref[0], val_dim)
    retained = dot(scores.astype(BF16), values) + carried
    faded = (keys.astype(F32) * widen(rows_ref[1], key_dim)).astype(BF16)
    update = lax.dot_general(faded, values, (((0,), (0,)), ((), ())), preferred_element_type=F32)
    s_ref[...] = state * widen(over, val_dim) + update
    row_mean = jnp.mean(retained, axis=-1, keepdims=True)
    centered = retained - row_mean
    variance = jnp.mean(centered * centered, axis=-1, keepdims=True)
    normed = centered * lax.rsqrt(variance + GROUP_EPS)
    return (gates * lax.logistic(gates) * normed).astype(BF16)


def kernel_body(heads, n_z, pieces, meta_ref, x_ref, consts_ref, base_ref, step_ref, *refs):
    n_heads = len(heads)
    it = iter(refs)

    def take(n):
        return [next(it) for _ in range(n)]

    s_refs, z_refs = take(n_heads), take(n_z)
    sources = [take(len(p)) for p in pieces]
    if n_z:
        take(len(refs) - (n_heads + n_z + sum(map(len, pieces)) + 2 + n_heads + 3 + len(pieces)))
        whole_ref, out_ref = take(2)
    else:
        z_ref = take(1)[0]
    state_refs = take(n_heads)
    inner_ref, rows_ref, sem = take(3)
    weights = take(len(pieces))

    @pl.when((pl.program_id(0) == 0) & (pl.program_id(1) == 0))
    def _():
        copies = []
        for w_ref, refs_in, places in zip(weights, sources, pieces):
            for ref, (row, col, flip) in zip(refs_in, places):
                if flip is not None:
                    row = pl.multiple_of((meta_ref[2, 0] ^ flip) * ref.shape[0], 256)
                dst = w_ref.at[pl.ds(row, ref.shape[0]), pl.ds(col, ref.shape[1])]
                copies.append(pltpu.make_async_copy(ref, dst, sem.at[len(copies)]))
                copies[-1].start()
        fill_decays(consts_ref, heads, inner_ref, rows_ref)
        for copy in copies:
            copy.wait()

    @pl.when(pl.program_id(1) == 0)
    def _():
        for s_ref, state_ref in zip(s_refs, state_refs):
            state_ref[...] = s_ref[...]

    h = layer_norm(x_ref[0].astype(F32), consts_ref[0:1, :], consts_ref[1:2, :]).astype(BF16)
    at = pl.multiple_of(pl.program_id(1) * 8, 8)
    cos_a, sin_a = base_ref[0, pl.ds(at, 1), :], base_ref[0, pl.ds(at + 1, 1), :]
    cos_b, sin_b = step_ref[0], step_ref[1]
    cos_t, sin_t = cos_a * cos_b - sin_a * sin_b, sin_a * cos_b + cos_a * sin_b
    mixed = []
    for i, head in enumerate(heads):
        over = jnp.exp(TILE * decay_row(consts_ref, head))
        mixed.append(head_block(h, weights[i], state_refs[i].at[0], inner_ref[i], rows_ref.at[i], over, cos_t, sin_t))
    if not n_z:
        z_ref[0] = mixed[0]
        return
    mixed = [z[0] for z in z_refs] + mixed
    blocks = weights[n_heads:]
    val_dim, d_model = mixed[0].shape[1], x_ref.shape[2]
    u = sum(dot(z, wb[:val_dim, :d_model]) for z, wb in zip(mixed, blocks))
    x_mid = (x_ref[0].astype(F32) + u.astype(BF16).astype(F32)).astype(BF16)
    h_two = layer_norm(x_mid.astype(F32), consts_ref[2:3, :], consts_ref[3:4, :]).astype(BF16)
    f = jnp.zeros(u.shape, F32)
    for wb in blocks:
        up = dot(h_two, wb[:, d_model:])
        act = (up * 0.5 * (1.0 + lax.erf(up * 0.5 ** 0.5))).astype(BF16)
        f = f + dot(act, wb[val_dim:, :d_model])
    x_out = (x_mid.astype(F32) + f.astype(BF16).astype(F32)).astype(BF16)
    out_ref[0] = x_out
    whole_ref[0] = x_out


def run(meta, common, heads, states, weights, zs=(), whole=None, states_whole=False):
    x, consts, base, step = common
    n, chunk_len, d_model = meta.shape[1], x.shape[1], x.shape[2]
    key_dim, val_dim = states[0].shape[1:]
    whole_spec = pl.BlockSpec((1, TILE, d_model), lambda s, t, m: (m[0, s], t, 0))
    state_in = pl.BlockSpec((1, key_dim, val_dim), lambda s, t, m: (m[1, s], 0, 0))
    state_out = pl.BlockSpec((1, key_dim, val_dim), lambda s, t, m: (m[0, s] if states_whole else s, 0, 0))

    def tile_of(width, offset=0):
        return pl.BlockSpec((1, TILE, width), lambda s, t, m: (s + offset, t, 0))

    def resident(arr):
        return pl.BlockSpec(arr.shape, lambda s, t, m: (0,) * arr.ndim, pipeline_mode=pl.Buffered(1))

    specs = [whole_spec, resident(consts), pl.BlockSpec((1,) + base.shape[1:], lambda s, t, m: (m[0, s], 0, 0)), resident(step)]
    specs += [state_in] * len(heads) + [tile_of(val_dim, offset) for _, offset in zs]
    args = [x, consts, base, step, *states, *(z for z, _ in zs)]
    pieces = []
    for weight in weights:
        pieces.append(tuple(place for _, place in weight))
        args += [arr for arr, _ in weight]
        specs += [ANY] * len(weight)
    aliases = {}
    if whole is not None:
        aliases = {len(args) + 1: 0}
        args.append(whole)
        specs.append(ANY)
    state_shape = jax.ShapeDtypeStruct((x.shape[0] if states_whole else n, key_dim, val_dim), F32)
    if zs:
        outs = [(whole_spec, jax.ShapeDtypeStruct(x.shape, BF16)), (tile_of(d_model), jax.ShapeDtypeStruct((n, chunk_len, d_model), BF16))]
    else:
        outs = [(tile_of(val_dim), jax.ShapeDtypeStruct((n, chunk_len, val_dim), BF16))]
    outs += [(state_out, state_shape)] * len(heads)
    flops = len(heads) * 2 * (d_model * (2 * key_dim + 2 * val_dim) + TILE * (key_dim + val_dim) + 2 * key_dim * val_dim)
    flops += 24 * d_model * val_dim if zs else 0
    n_copies = sum(map(len, pieces))
    return pl.pallas_call(
        functools.partial(kernel_body, tuple(heads), len(zs), tuple(pieces)),
        grid_spec=pltpu.PrefetchScalarGridSpec(
            num_scalar_prefetch=1, grid=(n, chunk_len // TILE), in_specs=specs, out_specs=[spec for spec, _ in outs],
            scratch_shapes=[pltpu.VMEM((len(heads), TILE, TILE), F32), pltpu.VMEM((len(heads), 2, TILE, 128), F32), pltpu.SemaphoreType.DMA((n_copies,))]
            + [pltpu.VMEM((d_model, 2 * key_dim + 2 * val_dim), BF16) for _ in weights]),
        out_shape=[shape for _, shape in outs],
        compiler_params=pltpu.CompilerParams(dimension_semantics=("arbitrary", "arbitrary"), vmem_limit_bytes=58 << 20),
        cost_estimate=pl.CostEstimate(flops=n * chunk_len * flops, bytes_accessed=n * chunk_len * d_model * (8 if zs else 4), transcendentals=0),
        input_output_aliases=aliases,
        name="tail" if zs else "heads",
    )(meta, *args)


def place_kernel(n_x, n_s, ids_ref, *refs):
    x_refs, s_refs = refs[:n_x], refs[n_x:n_x + n_s]
    whole_ref, states_ref, sem = refs[n_x + n_s + 2:]
    t = pl.program_id(0)
    copies = []
    for i, ref in enumerate(x_refs):
        copies.append(pltpu.make_async_copy(ref.at[0], whole_ref.at[ids_ref[i], pl.ds(pl.multiple_of(t * TILE, TILE), TILE), :], sem.at[i]))
    rows = s_refs[0].shape[1]
    for i, ref in enumerate(s_refs):
        copies.append(pltpu.make_async_copy(ref.at[0], states_ref.at[ids_ref[n_x + i], pl.ds(pl.multiple_of(t * rows, rows), rows), :], sem.at[n_x + i]))
    for copy in copies:
        copy.start()
    for copy in copies:
        copy.wait()


def place(ids, blocks, states, whole, new_states):
    steps = whole.shape[1] // TILE
    rows = new_states.shape[1] // steps

    def spec(height, width, at):
        return pl.BlockSpec((1, height, width), lambda t, m: (at, t, 0))

    specs = [spec(TILE, whole.shape[2], at) for _, at in blocks] + [spec(rows, new_states.shape[2], at) for _, at in states]
    n = len(specs)
    return pl.pallas_call(
        functools.partial(place_kernel, len(blocks), len(states)),
        grid_spec=pltpu.PrefetchScalarGridSpec(num_scalar_prefetch=1, grid=(steps,), in_specs=specs + [ANY, ANY], out_specs=[ANY, ANY],
                                               scratch_shapes=[pltpu.SemaphoreType.DMA((n,))]),
        out_shape=[jax.ShapeDtypeStruct(whole.shape, whole.dtype), jax.ShapeDtypeStruct(new_states.shape, new_states.dtype)],
        compiler_params=pltpu.CompilerParams(dimension_semantics=("arbitrary",), vmem_limit_bytes=32 << 20),
        input_output_aliases={n + 1: 0, n + 2: 1},
        name="place",
    )(ids, *(arr for arr, _ in blocks), *(arr for arr, _ in states), whole, new_states)


def rope_tables(start_pos, chunk_len, key_dim):
    half_dim = key_dim // 2
    inv_freq = jnp.power(ROPE_BASE, -jnp.arange(half_dim).astype(F32) / half_dim)
    starts = (start_pos[:, None] + jnp.arange(0, chunk_len, TILE)[None, :]).astype(F32)
    base = starts[:, :, None, None] * inv_freq
    row = lax.broadcasted_iota(jnp.int32, (1, 1, 8, 1), 2)
    base = jnp.where(row == 0, jnp.cos(base), jnp.sin(base))
    step = jnp.arange(TILE).astype(F32)[None, :, None] * inv_freq
    kind = lax.broadcasted_iota(jnp.int32, (2, 1, 1), 0)
    return base.reshape(start_pos.shape[0], -1, half_dim), jnp.where(kind == 0, jnp.cos(step), jnp.sin(step))


def solution(mesh):
    n_dp = mesh.shape["dp"]

    def swap(axis, bits):
        return functools.partial(lax.ppermute, axis_name=axis, perm=[(i, i ^ bits) for i in range(mesh.shape[axis])])

    to_core, to_chip, to_far = swap("tp", 1), swap("tp", 2), swap("tp", 3)

    def local_layer(x_in, start_pos, kv_state, ln1_gain, ln1_bias, w_q, w_k, w_v, w_g, w_o, ln2_gain, ln2_bias, w_up, w_down):
        tp, group = lax.axis_index("tp"), lax.axis_index("dp")
        chip, core = tp // 2, tp % 2
        other = 1 - core
        chunk_len, d_model = x_in.shape[1:]
        own = kv_state[:, 0]
        key_dim, val_dim = own.shape[1:]

        def rows_of(w, i, n):
            return lax.dynamic_slice_in_dim(w, i * n, n, axis=0)

        def quarter(w):
            return rows_of(w, group, w.shape[0] // n_dp)

        def head_places(arrs):
            return [(w, (0, col, None)) for w, col in zip(arrs, (0, key_dim, 2 * key_dim, 2 * key_dim + val_dim))]

        def mlp_places(arrs):
            return [(w, at) for w, at in zip(arrs, ((0, 0, None), (val_dim, 0, None), (0, d_model, None)))]

        def heads_gathered(quarters):
            return [(w, (0, 0, flip)) for flip, w in enumerate(quarters)]

        def gather(part):
            return [part] + [swap("dp", flip)(part) for flip in range(1, n_dp)]

        head_w, mlp_w = (w_q, w_k, w_v, w_g), (w_o, w_down, w_up)
        wa_part = to_chip(jnp.concatenate([quarter(w) for w in head_w], axis=1))
        wa_core = [to_core(w) for w in head_w]
        s_core = to_core(own)
        n_rows = d_model // n_dp
        stacked = jnp.where(group < n_dp // 2, rows_of(w_o, group % 2, n_rows), rows_of(w_down, group % 2, n_rows))
        wb_part = to_chip(jnp.concatenate([stacked, quarter(w_up)], axis=1))
        su_chip = to_chip(rows_of(own, 1 - chip, 2))
        st_chip = to_chip(own[4:8])
        wb_core = [to_core(w) for w in mlp_w]

        single, twice = 2 * chip + core, 4 + 2 * core
        single_o, twice_o = 2 * chip + other, 4 + 2 * other
        far_c, far_o = 2 * (1 - chip) + core, 2 * (1 - chip) + other

        def meta(seqs, rows):
            return jnp.stack([jnp.stack(seqs), jnp.stack(rows), jnp.stack([group] * len(seqs))]).astype(jnp.int32)

        m_single, m_twice = meta([single], [single]), meta([twice, twice + 1], [twice, twice + 1])
        m_three = meta([single, twice, twice + 1], [single, twice, twice + 1])
        m_far_single = meta([single], [core])
        m_a, m_b = meta([twice], [2 * core]), meta([twice + 1], [2 * core + 1])

        base, step = rope_tables(start_pos, chunk_len, key_dim)
        log_gamma = jnp.log1p(-jnp.exp2(-5.0 - jnp.stack([tp, tp ^ 1, tp ^ 2, tp ^ 3]).astype(F32)))
        spread = jnp.repeat(log_gamma, 128, total_repeat_length=4 * 128)
        consts = jnp.stack([ln1_gain, ln1_bias, ln2_gain, ln2_bias, jnp.zeros_like(ln1_gain)] + [jnp.pad(spread, (0, d_model - 4 * 128))] * 3)
        common = (x_in, consts, base, step)

        z_own_single, new_own_single = run(m_single, common, (0,), (own,), (head_places(head_w),))
        z_own_single, wa_part = lax.optimization_barrier((z_own_single, wa_part))
        wa_quarters = gather(wa_part)
        z_own, new_states = run(m_twice, common, (0,), (own,), (head_places(head_w),), states_whole=True)
        z_own, wa_core, s_core, wb_part = lax.optimization_barrier((z_own, wa_core, s_core, wb_part))
        wb_quarters = gather(wb_part)
        z_core, new_core = run(m_three, common, (1,), (s_core,), (head_places(wa_core),))
        z_core, wa_quarters, wb_quarters, su_chip, st_chip = lax.optimization_barrier((z_core, wa_quarters, wb_quarters, su_chip, st_chip))
        wa_far, su_far = [to_core(w) for w in wa_quarters], to_core(su_chip)
        wb_far, st_far = [to_core(w) for w in wb_quarters], to_core(st_chip)
        got_core = to_core(new_core)

        w_chip, w_far = heads_gathered(wa_quarters), heads_gathered(wa_far)
        z_chip, new_chip = run(m_far_single, common, (2,), (su_chip,), (w_chip,))
        z_chip, wa_far, wb_far, wb_core, su_far, st_far = lax.optimization_barrier((z_chip, wa_far, wb_far, wb_core, su_far, st_far))
        w_far = heads_gathered(wa_far)
        mlp = (mlp_places(mlp_w), mlp_places(wb_core), heads_gathered(wb_quarters), heads_gathered(wb_far))
        whole, x_single, new_far = run(m_far_single, common, (3,), (su_far,), (w_far, *mlp), ((z_own_single, 0), (z_core, 0), (z_chip, 0)))
        x_single_chip = to_chip(x_single)
        x_single_core = to_core(x_single)
        got_chip = to_chip(new_chip)
        got_far = to_far(new_far)
        far_states = (st_chip, st_far)
        whole, x_a, _, _ = run(m_a, common, (2, 3), far_states, (w_chip, w_far, *mlp), ((z_own, 0), (z_core, 1)), whole)
        x_a_core = to_core(x_a)
        whole, x_b, _, _ = run(m_b, common, (2, 3), far_states, (w_chip, w_far, *mlp), ((z_own, 1), (z_core, 2)), whole)
        x_b_core = to_core(x_b)
        x_single_far = to_core(x_single_chip)

        ids = jnp.stack([single_o, twice_o, far_c, far_o, twice_o + 1, single, single_o, twice_o, twice_o + 1, far_c, far_o])
        blocks = [(x_single_core, 0), (x_a_core, 0), (x_single_chip, 0), (x_single_far, 0), (x_b_core, 0)]
        new = [(new_own_single, 0), (got_core, 0), (got_core, 1), (got_core, 2), (got_chip, 0), (got_far, 0)]
        whole, new_states = place(ids.astype(jnp.int32), blocks, new, whole, new_states)
        return whole, new_states[:, None]

    in_specs = (P("dp", None, None), P("dp"), P("dp", "tp", None, None), P(), P(), P(None, "tp"), P(None, "tp"), P(None, "tp"), P(None, "tp"), P("tp", None), P(), P(), P(None, "tp"), P("tp", None))
    out_specs = (P("dp", None, None), P("dp", "tp", None, None))
    return jax.shard_map(local_layer, mesh=mesh, in_specs=in_specs, out_specs=out_specs, check_vma=False)
```

time: 1710 us -> 468 us (0.27)
  waiting for transfers between devices: 1100 us -> 101 us
  matrix products: 426 us -> 0 us
  Pallas kernels: 0 us -> 316 us
  other arithmetic: 166 us -> 10.1 us
  starting transfers between devices: 0.08 us -> 23.3 us
    psum x2 -> x0, waiting for transfers between devices: 1100 us -> none  [the longest x1 557 us: local_layer(): attn_out = lax.psum(attn_part, 'tp')]
    dot_general x10 -> x0, matrix products: 426 us -> none  [the longest x1 91.7 us: feed_forward(): jnp.einsum('bcf,fd->bcd', activated, w_down, preferred_element_type=jnp.f...]
    pallas_call x0 -> x8, Pallas kernels: none -> 316 us  [the longest x7 298 us: run(): pl.pallas_call(functools.partial(kernel_body, tuple(heads), len(zs), tupl...]
    ppermute x0 -> x36, waiting for transfers between devices: none -> 101 us  [the longest x6 44.8 us: gather(): return [part] + [swap('dp', flip)(part) for flip in range(1, n_dp)]]
    reduce_sum x5 -> x0, other arithmetic: 84.3 us -> none  [the longest x2 44.7 us: layer_norm(): row_mean = jnp.mean(x_f32, axis=-1, keepdims=True)]
    concatenate x1 -> x2, other arithmetic: 39.3 us -> 1.9 us  [the longest x1 0.97 us: local_layer(): wb_part = to_chip(jnp.concatenate([stacked, quarter(w_up)], axis=1))]
    convert_element_type x2, other arithmetic: 33.4 us -> 0.07 us  [the longest x1 0.07 us: rope_tables(): (start_pos[:, None] + jnp.arange(0, chunk_len, TILE)[None, :]).astype(F32)]
    ppermute x0 -> x36, starting transfers between devices: none -> 23.3 us  [the longest x6 8.42 us: gather(): return [part] + [swap('dp', flip)(part) for flip in range(1, n_dp)]]
  transfers between devices with their start and end apart: 2 -> 36, of which waited for: 2 -> 14; matrix products, arithmetic and copies ran while one was open for 1% -> 4% of each run, Pallas kernels for 0% -> 52%
where the time goes in v2:
time: 468 us; the launch traced here: 467 us
  Pallas kernels  316 us (68%)
  waiting for transfers between devices  101 us (22%)
  starting transfers between devices  23.3 us (5%)
  local copies, waits for them, and re-layouts  15 us (3%)
  other arithmetic  10.1 us (2%)
    pallas_call x7, Pallas kernels, run(): pl.pallas_call(functools.partial(kernel_body, tuple(heads), len(zs), tupl...  298 us
    ppermute x6, waiting for transfers between devices, gather(): return [part] + [swap('dp', flip)(part) for flip in range(1, n_dp)]  44.8 us
    pallas_call x1, Pallas kernels, place(): pl.pallas_call(functools.partial(place_kernel, len(blocks), len(states)),...  18.6 us
    ppermute x1, waiting for transfers between devices, local_layer(): wa_part = to_chip(jnp.concatenate([quarter(w) for w in head_w], axis=1))  14.8 us
    ppermute x1, waiting for transfers between devices, local_layer(): got_chip = to_chip(new_chip)  12.4 us
    ppermute x1, waiting for transfers between devices, local_layer(): got_far = to_far(new_far)  12.3 us
  transfers between devices with their start and end apart: 36, of which 14 were waited for; matrix products, arithmetic and copies ran while one was open for 4% of the time, Pallas kernels for 52%

profile of v2, /device:TPU:0, one launch (start us, length us, event | category | flops | bytes accessed | tf_op | source)
XLA Modules:
  0.0 466.8 jit_solution(12458149774617811362)
XLA Ops:
  4.1 3.2 collective-permute-start.5
  12.6 2.6 compare_select_fusion.1
  16.7 2.3 dynamic-slice_bitcast_fusion
  23.7 2.3 collective-permute-done.5.refs_14_.refs_18_
  26.0 2.0 collective-permute-start.13
  28.1 14.8 %collective-permute-done.6.refs_1_.refs_4_ = bf16[256,1536]{1,0:T(8,128)(2,1)} collective-permute-done((bf16[256,1536]{1,0:T(8,128)(2,1)}, bf16[256,1536]{1,0:T(8,128)(2,1)}, u32[]{:S(2)}, u32[]{:S(2)}) %collective-permute-start.6) | collective-permute-done | bytes 786464 | tf_op jit(solution)/shard_map/ppermute | solution.py:275
  42.9 2.0 collective-permute-start.14
  44.9 32.6 %heads.4 = (bf16[2,2048,512]{2,1,0:T(8,128)(2,1)}, f32[8,256,512]{2,1,0:T(8,128)}) custom-call(s32[3,2]{1,0:T(4,128)} %pad_add_fusion.meta_ref, bf16[8,2048,1024]{2,1,0:T(8,128)(2,1)} %x_ref.13, f32[8,1024]{1,0:T(8,128)} %stack.144.consts_ref, f32[8,64,128]{2,1,0:T(8,128)} %bitcast_select_fusion.base_ref, f32[2,256,128]{2,1,0:T(8,128)} %broadcast_select_fusion.step_ref, ...), custom_call_target="tpu_custom_call" | custom-call | flops 16642998272 | bytes 16777216 | tf_op jit(solution)/shard_map/heads/pallas_call | solution.py:178
  78.2 18.5 %heads.6 = (bf16[1,2048,512]{2,1,0:T(8,128)(2,1)}, f32[1,256,512]{2,1,0:T(8,128)}) custom-call(s32[3,1]{1,0:T(4,128)} %copy.22.meta_ref, bf16[8,2048,1024]{2,1,0:T(8,128)(2,1)} %x_ref.13, f32[8,1024]{1,0:T(8,128)} %stack.144.consts_ref, f32[8,64,128]{2,1,0:T(8,128)} %bitcast_select_fusion.base_ref, f32[2,256,128]{2,1,0:T(8,128)} %broadcast_select_fusion.step_ref, ...), custom_call_target="tpu_custom_call" | custom-call | flops 8321499136 | bytes 8388608 | tf_op jit(solution)/shard_map/heads/pallas_call | solution.py:178
  102.5 14.8 %collective-permute-done.7.refs_2_.refs_5_ = bf16[256,1536]{1,0:T(8,128)(2,1)S(1)} collective-permute-done((bf16[256,1536]{1,0:T(8,128)(2,1)}, bf16[256,1536]{1,0:T(8,128)(2,1)S(1)}, u32[]{:S(2)}, u32[]{:S(2)}) %collective-permute-start.7) | collective-permute-done | bytes 786464 | tf_op jit(solution)/shard_map/ppermute | solution.py:272
  117.4 11.7 %collective-permute-done.8.refs_3_.refs_6_ = bf16[256,1536]{1,0:T(8,128)(2,1)} collective-permute-done((bf16[256,1536]{1,0:T(8,128)(2,1)}, bf16[256,1536]{1,0:T(8,128)(2,1)}, u32[]{:S(2)}, u32[]{:S(2)}) %collective-permute-start.8) | collective-permute-done | bytes 786464 | tf_op jit(solution)/shard_map/ppermute | solution.py:272
  129.0 6.3 %collective-permute-done.9.refs_4_.refs_7_ = bf16[256,1536]{1,0:T(8,128)(2,1)} collective-permute-done((bf16[256,1536]{1,0:T(8,128)(2,1)}, bf16[256,1536]{1,0:T(8,128)(2,1)}, u32[]{:S(2)}, u32[]{:S(2)}) %collective-permute-start.9) | collective-permute-done | bytes 786464 | tf_op jit(solution)/shard_map/ppermute | solution.py:272
  135.8 12.0 %collective-permute-done.10.refs_15_.refs_19_ = bf16[256,1536]{1,0:T(8,128)(2,1)} collective-permute-done((bf16[256,1536]{1,0:T(8,128)(2,1)}, bf16[256,1536]{1,0:T(8,128)(2,1)}, u32[]{:S(2)}, u32[]{:S(2)}) %collective-permute-start.10) | collective-permute-done | bytes 786464 | tf_op jit(solution)/shard_map/ppermute | solution.py:272
  147.8 2.9 collective-permute-start.12
  150.7 46.5 %heads.5 = (bf16[3,2048,512]{2,1,0:T(8,128)(2,1)}, f32[3,256,512]{2,1,0:T(8,128)}) custom-call(s32[3,3]{1,0:T(4,128)} %add_add_fusion.meta_ref, bf16[8,2048,1024]{2,1,0:T(8,128)(2,1)} %x_ref.13, f32[8,1024]{1,0:T(8,128)} %stack.144.consts_ref, f32[8,64,128]{2,1,0:T(8,128)} %bitcast_select_fusion.base_ref, f32[2,256,128]{2,1,0:T(8,128)} %broadcast_select_fusion.step_ref, ...), custom_call_target="tpu_custom_call" | custom-call | flops 24964497408 | bytes 25165824 | tf_op jit(solution)/shard_map/heads/pallas_call | solution.py:178
  201.1 4.0 collective-permute-done.16.refs_5_.refs_9_
  210.8 18.3 %heads.7 = (bf16[1,2048,512]{2,1,0:T(8,128)(2,1)}, f32[1,256,512]{2,1,0:T(8,128)}) custom-call(s32[3,1]{1,0:T(4,128)} %copy.25.meta_ref, bf16[8,2048,1024]{2,1,0:T(8,128)(2,1)} %x_ref.13, f32[8,1024]{1,0:T(8,128)} %stack.144.consts_ref, f32[8,64,128]{2,1,0:T(8,128)} %bitcast_select_fusion.base_ref, f32[2,256,128]{2,1,0:T(8,128)} %broadcast_select_fusion.step_ref, ...), custom_call_target="tpu_custom_call" | custom-call | flops 8321499136 | bytes 8388608 | tf_op jit(solution)/shard_map/heads/pallas_call | solution.py:178
  229.9 53.9 %tail.3 = (bf16[8,2048,1024]{2,1,0:T(8,128)(2,1)}, bf16[1,2048,1024]{2,1,0:T(8,128)(2,1)}, f32[1,256,512]{2,1,0:T(8,128)}) custom-call(s32[3,1]{1,0:T(4,128)} %copy.25.meta_ref, bf16[8,2048,1024]{2,1,0:T(8,128)(2,1)} %x_ref.13, f32[8,1024]{1,0:T(8,128)} %stack.144.consts_ref, f32[8,64,128]{2,1,0:T(8,128)} %bitcast_select_fusion.base_ref, ...), custom_call_target="tpu_custom_call" | custom-call | flops 34091302912 | bytes 16777216 | tf_op jit(solution)/shard_map/tail/pallas_call | solution.py:178
  284.5 63.8 %tail.4 = (bf16[8,2048,1024]{2,1,0:T(8,128)(2,1)}, bf16[1,2048,1024]{2,1,0:T(8,128)(2,1)}, f32[1,256,512]{2,1,0:T(8,128)}, f32[1,256,512]{2,1,0:T(8,128)}) custom-call(s32[3,1]{1,0:T(4,128)} %copy.26.meta_ref, bf16[8,2048,1024]{2,1,0:T(8,128)(2,1)} %x_ref.13, f32[8,1024]{1,0:T(8,128)} %stack.144.consts_ref, ...), custom_call_target="tpu_custom_call", output_to_operand_aliasing={{0}: (31, {})} | custom-call | flops 42412802048 | bytes 16777216 | tf_op jit(solution)/shard_map/tail/pallas_call | solution.py:178
  348.3 64.2 %tail.5 = (bf16[8,2048,1024]{2,1,0:T(8,128)(2,1)}, bf16[1,2048,1024]{2,1,0:T(8,128)(2,1)}, f32[1,256,512]{2,1,0:T(8,128)}, f32[1,256,512]{2,1,0:T(8,128)}) custom-call(s32[3,1]{1,0:T(4,128)} %copy.27.meta_ref, bf16[8,2048,1024]{2,1,0:T(8,128)(2,1)} %x_ref.13, f32[8,1024]{1,0:T(8,128)} %stack.144.consts_ref, ...), custom_call_target="tpu_custom_call", output_to_operand_aliasing={{0}: (31, {})} | custom-call | flops 42412802048 | bytes 16777216 | tf_op jit(solution)/shard_map/tail/pallas_call | solution.py:178
  415.0 12.4 %collective-permute-done.34.refs_9_ = f32[1,256,512]{2,1,0:T(8,128)S(1)} collective-permute-done((f32[1,256,512]{2,1,0:T(8,128)S(1)}, f32[1,256,512]{2,1,0:T(8,128)S(1)}, u32[]{:S(2)}, u32[]{:S(2)}) %collective-permute-start.34) | collective-permute-done | bytes 524320 | tf_op jit(solution)/shard_map/ppermute | solution.py:323
  427.4 6.8 %collective-permute-done.33.refs_6_.refs_7_.refs_8_ = f32[3,256,512]{2,1,0:T(8,128)S(1)} collective-permute-done((f32[3,256,512]{2,1,0:T(8,128)S(1)}, f32[3,256,512]{2,1,0:T(8,128)S(1)}, u32[]{:S(2)}, u32[]{:S(2)}) %collective-permute-start.33) | collective-permute-done | bytes 1572896 | tf_op jit(solution)/shard_map/ppermute | solution.py:313
  435.8 12.3 %collective-permute-done.35.refs_10_ = f32[1,256,512]{2,1,0:T(8,128)S(1)} collective-permute-done((f32[1,256,512]{2,1,0:T(8,128)}, f32[1,256,512]{2,1,0:T(8,128)S(1)}, u32[]{:S(2)}, u32[]{:S(2)}) %collective-permute-start.35) | collective-permute-done | bytes 524320 | tf_op jit(solution)/shard_map/ppermute | solution.py:324
  448.1 18.6 %place.1 = (bf16[8,2048,1024]{2,1,0:T(8,128)(2,1)}, f32[8,256,512]{2,1,0:T(8,128)}) custom-call(s32[11]{0:T(128)S(1)} %stack.132.ids_ref, bf16[1,2048,1024]{2,1,0:T(8,128)(2,1)} %collective-permute-done.28.refs_0_, bf16[1,2048,1024]{2,1,0:T(8,128)(2,1)} %collective-permute-done.29.refs_1_, ...), custom_call_target="tpu_custom_call", output_to_operand_aliasing={{0}: (12, {}), {1}: (13, {})} | custom-call | tf_op jit(solution)/shard_map/place/pallas_call | solution.py:217
  (137 shorter events, 36.9 us)
Async XLA Ops:
  4.1 21.9 %collective-permute-start.5 = (bf16[256,1536]{1,0:T(8,128)(2,1)}, bf16[256,1536]{1,0:T(8,128)(2,1)}, u32[]{:S(2)}, u32[]{:S(2)}) collective-permute-start(bf16[256,1536]{1,0:T(8,128)(2,1)} %pad_maximum_fusion), channel_id=1, source_target_pairs={{0,2},{1,3},{2,0},{3,1},{4,6},{5,7},{6,4},{7,5},{8,10},{9,11},{10,... | collective-permute-start | bytes 2359304 | tf_op jit(solution)/shard_map/ppermute | solution.py:280
  7.3 92.5 %collective-permute-start.4 = (f32[8,256,512]{2,1,0:T(8,128)}, f32[8,256,512]{2,1,0:T(8,128)}, u32[]{:S(2)}, u32[]{:S(2)}) collective-permute-start(f32[8,256,512]{2,1,0:T(8,128)} %bitcast.60), channel_id=1, source_target_pairs={{0,1},{1,0},{2,3},{3,2},{4,5},{5,4},{6,7},{7,6},{8,9},{9,8},{10,11... | collective-permute-start | bytes 12582920 | tf_op jit(solution)/shard_map/ppermute | solution.py:277
  11.6 31.2 %collective-permute-start.6 = (bf16[256,1536]{1,0:T(8,128)(2,1)}, bf16[256,1536]{1,0:T(8,128)(2,1)}, u32[]{:S(2)}, u32[]{:S(2)}) collective-permute-start(bf16[256,1536]{1,0:T(8,128)(2,1)} %pad_maximum_fusion.1), channel_id=1, source_target_pairs={{0,2},{1,3},{2,0},{3,1},{4,6},{5,7},{6,4},{7,5},{8,10},{9,11},{10,... | collective-permute-start | bytes 2359304 | tf_op jit(solution)/shard_map/ppermute | solution.py:275
  23.1 73.5 %collective-permute-start.2 = (bf16[1024,512]{1,0:T(8,128)(2,1)S(1)}, bf16[1024,512]{1,0:T(8,128)(2,1)}, u32[]{:S(2)}, u32[]{:S(2)}) collective-permute-start(bf16[1024,512]{1,0:T(8,128)(2,1)S(1)} %copy-done.1), channel_id=1, source_target_pairs={{0,1},{1,0},{2,3},{3,2},{4,5},{5,4},{6,7},{7,6},{8,9},{9,8},{10,11... | collective-permute-start | bytes 3145736 | tf_op jit(solution)/shard_map/ppermute | solution.py:276
  23.7 74.6 %collective-permute-start.3 = (bf16[1024,512]{1,0:T(8,128)(2,1)}, bf16[1024,512]{1,0:T(8,128)(2,1)}, u32[]{:S(2)}, u32[]{:S(2)}) collective-permute-start(bf16[1024,512]{1,0:T(8,128)(2,1)} %refs_4_.3), channel_id=1, source_target_pairs={{0,1},{1,0},{2,3},{3,2},{4,5},{5,4},{6,7},{7,6},{8,9},{9,8},{10,11... | collective-permute-start | bytes 3145736 | tf_op jit(solution)/shard_map/ppermute | solution.py:276
  26.0 74.2 %collective-permute-start.13 = (f32[2,256,512]{2,1,0:T(8,128)}, f32[2,256,512]{2,1,0:T(8,128)}, u32[]{:S(2)}, u32[]{:S(2)}) collective-permute-start(f32[2,256,512]{2,1,0:T(8,128)} %dynamic-slice_bitcast_fusion), channel_id=1, source_target_pairs={{0,2},{1,3},{2,0},{3,1},{4,6},{5,7},{6,4},{7,5},{8,10},{9,11},{10,... | collective-permute-start | bytes 3145736 | tf_op jit(solution)/shard_map/ppermute | solution.py:281
  42.9 92.5 %collective-permute-start.14 = (f32[4,256,512]{2,1,0:T(8,128)S(1)}, f32[4,256,512]{2,1,0:T(8,128)}, u32[]{:S(2)}, u32[]{:S(2)}) collective-permute-start(f32[4,256,512]{2,1,0:T(8,128)S(1)} %slice_bitcast_fusion), channel_id=1, source_target_pairs={{0,2},{1,3},{2,0},{3,1},{4,6},{5,7},{6,4},{7,5},{8,10},{9,11},{10,... | collective-permute-start | bytes 6291464 | tf_op jit(solution)/shard_map/ppermute | solution.py:282
  98.2 30.8 %collective-permute-start.8 = (bf16[256,1536]{1,0:T(8,128)(2,1)}, bf16[256,1536]{1,0:T(8,128)(2,1)}, u32[]{:S(2)}, u32[]{:S(2)}) collective-permute-start(bf16[256,1536]{1,0:T(8,128)(2,1)} %collective-permute-done.6.refs_1_.refs_4_), channel_id=1, source_target_pairs={{0,8},{4,12},{8,0},{12,4},{1,9},{5,13},{9,1},{13,5},{2,10},{6,14},... | collective-permute-start | bytes 2359304 | tf_op jit(solution)/shard_map/ppermute | solution.py:272
  99.8 35.5 %collective-permute-start.9 = (bf16[256,1536]{1,0:T(8,128)(2,1)}, bf16[256,1536]{1,0:T(8,128)(2,1)}, u32[]{:S(2)}, u32[]{:S(2)}) collective-permute-start(bf16[256,1536]{1,0:T(8,128)(2,1)} %collective-permute-done.6.refs_1_.refs_4_), channel_id=1, source_target_pairs={{0,12},{4,8},{8,4},{12,0},{1,13},{5,9},{9,5},{13,1},{2,14},{6,10},... | collective-permute-start | bytes 2359304 | tf_op jit(solution)/shard_map/ppermute | solution.py:272
  100.2 47.6 %collective-permute-start.10 = (bf16[256,1536]{1,0:T(8,128)(2,1)}, bf16[256,1536]{1,0:T(8,128)(2,1)}, u32[]{:S(2)}, u32[]{:S(2)}) collective-permute-start(bf16[256,1536]{1,0:T(8,128)(2,1)} %collective-permute-done.5.refs_14_.refs_18_), channel_id=1, source_target_pairs={{0,4},{4,0},{8,12},{12,8},{1,5},{5,1},{9,13},{13,9},{2,6},{6,2},{1... | collective-permute-start | bytes 2359304 | tf_op jit(solution)/shard_map/ppermute | solution.py:272
  117.4 81.6 %collective-permute-start.23 = (bf16[512,1024]{1,0:T(8,128)(2,1)S(1)}, bf16[512,1024]{1,0:T(8,128)(2,1)}, u32[]{:S(2)}, u32[]{:S(2)}) collective-permute-start(bf16[512,1024]{1,0:T(8,128)(2,1)S(1)} %copy-done.3), channel_id=1, source_target_pairs={{0,1},{1,0},{2,3},{3,2},{4,5},{5,4},{6,7},{7,6},{8,9},{9,8},{10,11... | collective-permute-start | bytes 3145736 | tf_op jit(solution)/shard_map/ppermute | solution.py:283
  129.0 70.0 %collective-permute-start.24 = (bf16[512,1024]{1,0:T(8,128)(2,1)S(1)}, bf16[512,1024]{1,0:T(8,128)(2,1)}, u32[]{:S(2)}, u32[]{:S(2)}) collective-permute-start(bf16[512,1024]{1,0:T(8,128)(2,1)S(1)} %copy-done.4), channel_id=1, source_target_pairs={{0,1},{1,0},{2,3},{3,2},{4,5},{5,4},{6,7},{7,6},{8,9},{9,8},{10,11... | collective-permute-start | bytes 3145736 | tf_op jit(solution)/shard_map/ppermute | solution.py:283
  135.4 64.1 %collective-permute-start.25 = (bf16[1024,512]{1,0:T(8,128)(2,1)}, bf16[1024,512]{1,0:T(8,128)(2,1)}, u32[]{:S(2)}, u32[]{:S(2)}) collective-permute-start(bf16[1024,512]{1,0:T(8,128)(2,1)} %refs_14_.3), channel_id=1, source_target_pairs={{0,1},{1,0},{2,3},{3,2},{4,5},{5,4},{6,7},{7,6},{8,9},{9,8},{10,11... | collective-permute-start | bytes 3145736 | tf_op jit(solution)/shard_map/ppermute | solution.py:283
  135.4 61.9 %collective-permute-start.11 = (bf16[256,1536]{1,0:T(8,128)(2,1)}, bf16[256,1536]{1,0:T(8,128)(2,1)S(1)}, u32[]{:S(2)}, u32[]{:S(2)}) collective-permute-start(bf16[256,1536]{1,0:T(8,128)(2,1)} %collective-permute-done.5.refs_14_.refs_18_), channel_id=1, source_target_pairs={{0,8},{4,12},{8,0},{12,4},{1,9},{5,13},{9,1},{13,5},{2,10},{6,14},... | collective-permute-start | bytes 2359304 | tf_op jit(solution)/shard_map/ppermute | solution.py:272
  147.8 49.5 %collective-permute-start.12 = (bf16[256,1536]{1,0:T(8,128)(2,1)}, bf16[256,1536]{1,0:T(8,128)(2,1)S(1)}, u32[]{:S(2)}, u32[]{:S(2)}) collective-permute-start(bf16[256,1536]{1,0:T(8,128)(2,1)} %collective-permute-done.5.refs_14_.refs_18_), channel_id=1, source_target_pairs={{0,12},{4,8},{8,4},{12,0},{1,13},{5,9},{9,5},{13,1},{2,14},{6,10},... | collective-permute-start | bytes 2359304 | tf_op jit(solution)/shard_map/ppermute | solution.py:272
  198.4 30.7 %collective-permute-start.27 = (f32[4,256,512]{2,1,0:T(8,128)}, f32[4,256,512]{2,1,0:T(8,128)S(1)}, u32[]{:S(2)}, u32[]{:S(2)}) collective-permute-start(f32[4,256,512]{2,1,0:T(8,128)} %collective-permute-done.14.refs_0_), channel_id=1, source_target_pairs={{0,1},{1,0},{2,3},{3,2},{4,5},{5,4},{6,7},{7,6},{8,9},{9,8},{10,11... | collective-permute-start | bytes 6291464 | tf_op jit(solution)/shard_map/ppermute | solution.py:312
  206.0 23.1 %collective-permute-start.26 = (f32[2,256,512]{2,1,0:T(8,128)}, f32[2,256,512]{2,1,0:T(8,128)}, u32[]{:S(2)}, u32[]{:S(2)}) collective-permute-start(f32[2,256,512]{2,1,0:T(8,128)} %collective-permute-done.13.refs_0_), channel_id=1, source_target_pairs={{0,1},{1,0},{2,3},{3,2},{4,5},{5,4},{6,7},{7,6},{8,9},{9,8},{10,11... | collective-permute-start | bytes 3145736 | tf_op jit(solution)/shard_map/ppermute | solution.py:311
  206.3 22.7 %collective-permute-start.20 = (bf16[256,1536]{1,0:T(8,128)(2,1)}, bf16[256,1536]{1,0:T(8,128)(2,1)S(1)}, u32[]{:S(2)}, u32[]{:S(2)}) collective-permute-start(bf16[256,1536]{1,0:T(8,128)(2,1)} %collective-permute-done.10.refs_15_.refs_19_), channel_id=1, source_target_pairs={{0,1},{1,0},{2,3},{3,2},{4,5},{5,4},{6,7},{7,6},{8,9},{9,8},{10,11... | collective-permute-start | bytes 2359304 | tf_op jit(solution)/shard_map/ppermute | solution.py:312
  207.4 21.6 %collective-permute-start.21 = (bf16[256,1536]{1,0:T(8,128)(2,1)}, bf16[256,1536]{1,0:T(8,128)(2,1)}, u32[]{:S(2)}, u32[]{:S(2)}) collective-permute-start(bf16[256,1536]{1,0:T(8,128)(2,1)} %copy-done.12), channel_id=1, source_target_pairs={{0,1},{1,0},{2,3},{3,2},{4,5},{5,4},{6,7},{7,6},{8,9},{9,8},{10,11... | collective-permute-start | bytes 2359304 | tf_op jit(solution)/shard_map/ppermute | solution.py:312
  283.9 129.2 %collective-permute-start.30 = (bf16[1,2048,1024]{2,1,0:T(8,128)(2,1)}, bf16[1,2048,1024]{2,1,0:T(8,128)(2,1)}, u32[]{:S(2)}, u32[]{:S(2)}) collective-permute-start(bf16[1,2048,1024]{2,1,0:T(8,128)(2,1)} %get-tuple-element.101), channel_id=1, source_target_pairs={{0,2},{1,3},{2,0},{3,1},{4,6},{5,7},{6,4},{7,5},{8,10},{9,11},{10,... | collective-permute-start | bytes 12582920 | tf_op jit(solution)/shard_map/ppermute | solution.py:321
  284.4 163.6 %collective-permute-start.28 = (bf16[1,2048,1024]{2,1,0:T(8,128)(2,1)}, bf16[1,2048,1024]{2,1,0:T(8,128)(2,1)}, u32[]{:S(2)}, u32[]{:S(2)}) collective-permute-start(bf16[1,2048,1024]{2,1,0:T(8,128)(2,1)} %get-tuple-element.101), channel_id=1, source_target_pairs={{0,1},{1,0},{2,3},{3,2},{4,5},{5,4},{6,7},{7,6},{8,9},{9,8},{10,11... | collective-permute-start | bytes 12582920 | tf_op jit(solution)/shard_map/ppermute | solution.py:322
  412.5 35.6 %collective-permute-start.32 = (bf16[1,2048,1024]{2,1,0:T(8,128)(2,1)}, bf16[1,2048,1024]{2,1,0:T(8,128)(2,1)}, u32[]{:S(2)}, u32[]{:S(2)}) collective-permute-start(bf16[1,2048,1024]{2,1,0:T(8,128)(2,1)} %get-tuple-element.107), channel_id=1, source_target_pairs={{0,1},{1,0},{2,3},{3,2},{4,5},{5,4},{6,7},{7,6},{8,9},{9,8},{10,11... | collective-permute-start | bytes 12582920 | tf_op jit(solution)/shard_map/ppermute | solution.py:329
  412.9 35.1 %collective-permute-start.29 = (bf16[1,2048,1024]{2,1,0:T(8,128)(2,1)}, bf16[1,2048,1024]{2,1,0:T(8,128)(2,1)}, u32[]{:S(2)}, u32[]{:S(2)}) collective-permute-start(bf16[1,2048,1024]{2,1,0:T(8,128)(2,1)} %get-tuple-element.105), channel_id=1, source_target_pairs={{0,1},{1,0},{2,3},{3,2},{4,5},{5,4},{6,7},{7,6},{8,9},{9,8},{10,11... | collective-permute-start | bytes 12582920 | tf_op jit(solution)/shard_map/ppermute | solution.py:327
  413.1 35.0 %collective-permute-start.31 = (bf16[1,2048,1024]{2,1,0:T(8,128)(2,1)}, bf16[1,2048,1024]{2,1,0:T(8,128)(2,1)}, u32[]{:S(2)}, u32[]{:S(2)}) collective-permute-start(bf16[1,2048,1024]{2,1,0:T(8,128)(2,1)} %collective-permute-done.30.refs_2_), channel_id=1, source_target_pairs={{0,1},{1,0},{2,3},{3,2},{4,5},{5,4},{6,7},{7,6},{8,9},{9,8},{10,11... | collective-permute-start | bytes 12582920 | tf_op jit(solution)/shard_map/ppermute | solution.py:330
  (30 other events, 703.5 us)

commit v3 on v2

v3 whole, which is shorter than its diff:
```python
import functools

import jax
import jax.numpy as jnp
import numpy as np
from jax import lax
from jax.experimental import pallas as pl
from jax.experimental.pallas import tpu as pltpu
from jax.sharding import PartitionSpec as P


NORM_EPS = 1e-5
GROUP_EPS = 1e-6
ROPE_BASE = 10000.0
TILE = 256
NUM_HEADS = 4
LOG_GAMMA = [float(np.log1p(-np.exp2(-5.0 - n))) for n in range(NUM_HEADS)]
SEQ, STATE_SINGLE, STATE_TWICE, GROUP, HEAD, PAIR, OTHER_CHIP = 0, 3, 4, 6, 7, 8, 9
BF16 = jnp.bfloat16
F32 = jnp.float32
ANY = pl.BlockSpec(memory_space=pl.ANY)


def dot(a, b):
    return jnp.dot(a, b, preferred_element_type=F32)


def layer_norm(x_f32, norm_gain, norm_bias):
    row_mean = jnp.mean(x_f32, axis=-1, keepdims=True)
    centered = x_f32 - row_mean
    variance = jnp.mean(centered * centered, axis=-1, keepdims=True)
    return centered * lax.rsqrt(variance + NORM_EPS) * norm_gain + norm_bias


def rotate(v, cos_t, sin_t):
    half = v.shape[-1] // 2
    a, b = v[:, :half], v[:, half:]
    return jnp.concatenate([a * cos_t - b * sin_t, b * cos_t + a * sin_t], axis=-1)


def widen(row_table, width):
    return jnp.concatenate([row_table] * (width // row_table.shape[-1]), axis=-1)


def log_decay(head):
    value = jnp.float32(LOG_GAMMA[0])
    for n, log_gamma in enumerate(LOG_GAMMA[1:], 1):
        value = jnp.where(head == n, jnp.float32(log_gamma), value)
    return value


def fill_decays(log_gammas, inner_ref, rows_ref):
    gap = lax.broadcasted_iota(jnp.int32, (TILE, TILE), 0) - lax.broadcasted_iota(jnp.int32, (TILE, TILE), 1)
    row = lax.broadcasted_iota(jnp.int32, (TILE, 128), 0)
    for i, log_gamma in enumerate(log_gammas):
        inner_ref[i] = jnp.where(gap >= 0, jnp.exp(jnp.maximum(gap, 0).astype(F32) * log_gamma), 0.0)
        rows_ref[i, 0] = jnp.exp((row + 1).astype(F32) * log_gamma)
        rows_ref[i, 1] = jnp.exp((TILE - 1 - row).astype(F32) * log_gamma)
        rows_ref[i, 2] = jnp.exp(jnp.full((TILE, 128), TILE, F32) * log_gamma)


def head_block(h, w_ref, s_ref, inner, rows_ref, cos_t, sin_t):
    key_dim, val_dim = s_ref.shape
    q_raw = dot(h, w_ref[:, :key_dim])
    k_raw = dot(h, w_ref[:, key_dim:2 * key_dim])
    queries = rotate(q_raw, cos_t, sin_t).astype(BF16)
    keys = (rotate(k_raw, cos_t, sin_t) * key_dim ** -0.5).astype(BF16)
    values = dot(h, w_ref[:, 2 * key_dim:2 * key_dim + val_dim]).astype(BF16)
    scores = lax.dot_general(queries, keys, (((1,), (1,)), ((), ())), preferred_element_type=F32) * inner
    state = s_ref[...]
    carried = dot(queries, state.astype(BF16)) * widen(rows_ref[0], val_dim)
    retained = dot(scores.astype(BF16), values) + carried
    gates = dot(h, w_ref[:, 2 * key_dim + val_dim:])
    faded = (keys.astype(F32) * widen(rows_ref[1], key_dim)).astype(BF16)
    update = lax.dot_general(faded, values, (((0,), (0,)), ((), ())), preferred_element_type=F32)
    s_ref[...] = state * widen(rows_ref[2, 0:1], val_dim) + update
    row_mean = jnp.mean(retained, axis=-1, keepdims=True)
    centered = retained - row_mean
    variance = jnp.mean(centered * centered, axis=-1, keepdims=True)
    normed = centered * lax.rsqrt(variance + GROUP_EPS)
    return (gates * lax.logistic(gates) * normed).astype(BF16)


def kernel_body(n_seqs, heads, n_z, pieces, with_whole, meta_ref, gain1, bias1, gain2, bias2, step_ref, *refs):
    it = iter(refs)

    def take(n):
        return [next(it) for _ in range(n)]

    x_refs, base_refs, s_refs, z_refs = take(n_seqs), take(n_seqs), [take(n_seqs) for _ in heads], take(n_z)
    sources = [take(len(p)) for p in pieces]
    take(with_whole)
    outs = take(2 if n_z else 1)
    state_refs = take(len(heads))
    inner_ref, rows_ref, sem = take(3)
    weights = take(len(pieces))

    @pl.when(pl.program_id(0) == 0)
    def _():
        copies = []
        for w_ref, refs_in, places in zip(weights, sources, pieces):
            for ref, (row, col, flip) in zip(refs_in, places):
                if flip is not None:
                    row = pl.multiple_of((meta_ref[GROUP] ^ flip) * ref.shape[0], 256)
                dst = w_ref.at[pl.ds(row, ref.shape[0]), pl.ds(col, ref.shape[1])]
                copies.append(pltpu.make_async_copy(ref, dst, sem.at[len(copies)]))
                copies[-1].start()
        fill_decays([log_decay(meta_ref[HEAD] ^ head) for head in heads], inner_ref, rows_ref)
        for per_head, state_ref in zip(s_refs, state_refs):
            for b, s_ref in enumerate(per_head):
                state_ref[b] = s_ref[0]
        for copy in copies:
            copy.wait()

    at = pl.multiple_of(pl.program_id(0) * 8, 8)
    cos_b, sin_b = step_ref[0], step_ref[1]
    normed, tables = [], []
    for x_ref, base_ref in zip(x_refs, base_refs):
        normed.append(layer_norm(x_ref[0].astype(F32), gain1[...], bias1[...]).astype(BF16))
        cos_a, sin_a = base_ref[0, pl.ds(at, 1), :], base_ref[0, pl.ds(at + 1, 1), :]
        tables.append((cos_a * cos_b - sin_a * sin_b, sin_a * cos_b + cos_a * sin_b))
    mixed = []
    for i in range(len(heads)):
        for b in range(n_seqs):
            mixed.append(head_block(normed[b], weights[i], state_refs[i].at[b], inner_ref[i], rows_ref.at[i], *tables[b]))
    if not n_z:
        for b in range(n_seqs):
            outs[0][b] = mixed[b]
        return
    mixed = [z[0] for z in z_refs] + mixed
    blocks = weights[len(heads):]
    val_dim, d_model = mixed[0].shape[1], x_refs[0].shape[2]
    u = sum(dot(z, wb[:val_dim, :d_model]) for z, wb in zip(mixed, blocks))
    x_mid = (x_refs[0][0].astype(F32) + u.astype(BF16).astype(F32)).astype(BF16)
    h_two = layer_norm(x_mid.astype(F32), gain2[...], bias2[...]).astype(BF16)
    f = jnp.zeros(u.shape, F32)
    for wb in blocks:
        up = dot(h_two, wb[:, d_model:])
        act = (up * 0.5 * (1.0 + lax.erf(up * 0.5 ** 0.5))).astype(BF16)
        f = f + dot(act, wb[val_dim:, :d_model])
    x_out = (x_mid.astype(F32) + f.astype(BF16).astype(F32)).astype(BF16)
    outs[0][0] = x_out
    outs[1][0] = x_out


def run(meta, common, seqs, state_rows, heads, states, weights, zs=(), whole=None, pair=False):
    x, norms, base, step = common
    n, chunk_len, d_model = len(seqs), x.shape[1], x.shape[2]
    key_dim, val_dim = states[0].shape[1:]

    def row_spec(shape, at):
        return pl.BlockSpec((1,) + shape, lambda t, m: (m[at], 0, 0))

    def token_spec(at):
        return pl.BlockSpec((1, TILE, d_model), lambda t, m: (m[at], t, 0))

    def tile_of(width, count=1, at=0):
        return pl.BlockSpec((count, TILE, width), lambda t, m: (at, t, 0))

    def resident(arr):
        return pl.BlockSpec(arr.shape, lambda t, m: (0,) * arr.ndim, pipeline_mode=pl.Buffered(1))

    specs = [resident(arr) for arr in (*norms, step)] + [token_spec(at) for at in seqs] + [row_spec(base.shape[1:], at) for at in seqs]
    args = [*norms, step] + [x] * n + [base] * n
    for state in states:
        specs += [row_spec(state.shape[1:], at) for at in state_rows]
        args += [state] * n
    specs += [tile_of(val_dim, 1, at) for _, at in zs]
    args += [z for z, _ in zs]
    pieces = []
    for weight in weights:
        pieces.append(tuple(place for _, place in weight))
        args += [arr for arr, _ in weight]
        specs += [ANY] * len(weight)
    aliases = {}
    if whole is not None:
        aliases = {len(args) + 1: 0}
        args.append(whole)
        specs.append(ANY)
    if zs:
        outs = [(token_spec(seqs[0]), jax.ShapeDtypeStruct(x.shape, BF16)), (tile_of(d_model), jax.ShapeDtypeStruct((1, chunk_len, d_model), BF16))]
    else:
        outs = [(tile_of(val_dim, n), jax.ShapeDtypeStruct((n, chunk_len, val_dim), BF16))]
    state_out = pl.BlockSpec((n, key_dim, val_dim), lambda t, m: (m[PAIR] if pair else 0, 0, 0))
    outs += [(state_out, jax.ShapeDtypeStruct((x.shape[0] if pair else n, key_dim, val_dim), F32))] * len(heads)
    flops = n * len(heads) * 2 * (d_model * (2 * key_dim + 2 * val_dim) + TILE * (key_dim + val_dim) + 2 * key_dim * val_dim)
    flops += 24 * d_model * val_dim if zs else 0
    return pl.pallas_call(
        functools.partial(kernel_body, n, tuple(heads), len(zs), tuple(pieces), whole is not None),
        grid_spec=pltpu.PrefetchScalarGridSpec(
            num_scalar_prefetch=1, grid=(chunk_len // TILE,), in_specs=specs, out_specs=[spec for spec, _ in outs],
            scratch_shapes=[pltpu.VMEM((len(heads), TILE, TILE), F32), pltpu.VMEM((len(heads), 3, TILE, 128), F32), pltpu.SemaphoreType.DMA((sum(map(len, pieces)),))]
            + [pltpu.VMEM((d_model, 2 * key_dim + 2 * val_dim), BF16) for _ in weights]),
        out_shape=[shape for _, shape in outs],
        compiler_params=pltpu.CompilerParams(dimension_semantics=("arbitrary",), vmem_limit_bytes=58 << 20),
        cost_estimate=pl.CostEstimate(flops=chunk_len * flops, bytes_accessed=n * chunk_len * d_model * (8 if zs else 4), transcendentals=0),
        input_output_aliases=aliases,
        name="tail" if zs else "heads",
    )(meta, *args)


def parts_kernel(meta_ref, w_q, w_k, w_v, w_g, w_o, w_down, w_up, own, heads_ref, mlp_ref, states_ref, sem):
    rows, group = heads_ref.shape[0], meta_ref[GROUP]
    at = pl.ds(pl.multiple_of(group * rows, rows), rows)
    half = pl.ds(pl.multiple_of((group % 2) * rows, rows), rows)
    d_model = w_o.shape[1]
    copies, col = [], 0
    for w in (w_q, w_k, w_v, w_g):
        copies.append(pltpu.make_async_copy(w.at[at], heads_ref.at[:, pl.ds(col, w.shape[1])], sem.at[len(copies)]))
        col += w.shape[1]
    copies.append(pltpu.make_async_copy(w_up.at[at], mlp_ref.at[:, pl.ds(d_model, w_up.shape[1])], sem.at[len(copies)]))
    copies.append(pltpu.make_async_copy(own.at[pl.ds(meta_ref[OTHER_CHIP], 2)], states_ref.at[pl.ds(0, 2)], sem.at[len(copies)]))
    copies.append(pltpu.make_async_copy(own.at[pl.ds(4, 4)], states_ref.at[pl.ds(2, 4)], sem.at[len(copies)]))
    for copy in copies:
        copy.start()
    last = [pltpu.make_async_copy(w.at[half], mlp_ref.at[:, pl.ds(0, d_model)], sem.at[len(copies)]) for w in (w_o, w_down)]

    @pl.when(group < 2)
    def _():
        last[0].start()

    @pl.when(group >= 2)
    def _():
        last[1].start()

    for copy in copies + last[:1]:
        copy.wait()


def cut_parts(meta, head_w, mlp_w, own):
    n_rows = mlp_w[0].shape[0] // 2
    shapes = [((n_rows, sum(w.shape[1] for w in head_w)), BF16), ((n_rows, mlp_w[0].shape[1] + mlp_w[2].shape[1]), BF16), ((6,) + own.shape[1:], F32)]
    return pl.pallas_call(
        parts_kernel,
        grid_spec=pltpu.PrefetchScalarGridSpec(num_scalar_prefetch=1, grid=(), in_specs=[ANY] * 8, out_specs=[pl.BlockSpec(memory_space=pltpu.VMEM)] * 3,
                                               scratch_shapes=[pltpu.SemaphoreType.DMA((8,))]),
        out_shape=[jax.ShapeDtypeStruct(shape, dtype) for shape, dtype in shapes],
        name="parts",
    )(meta, *head_w, *mlp_w, own)


def place_kernel(sources, n_wholes, ids_ref, *refs):
    in_refs, out_refs = refs[:len(sources)], refs[len(sources) + n_wholes:len(sources) + 2 * n_wholes]
    bufs, sem_in, sem_out = refs[len(sources) + 2 * n_wholes:-2], refs[-2], refs[-1]
    pulls, pushes, k = [], [], 0
    for i, ((seq, target, cuts), ref, buf) in enumerate(zip(sources, in_refs, bufs)):
        rows = buf.shape[0] // cuts
        for c in range(cuts):
            part = pl.ds(c * rows, rows)
            pulls.append(pltpu.make_async_copy(ref.at[seq, part], buf.at[part], sem_in.at[k]))
            pushes.append(pltpu.make_async_copy(buf.at[part], out_refs[target].at[ids_ref[i], part], sem_out.at[k]))
            k += 1
    for pull in pulls:
        pull.start()
    for pull, push in zip(pulls, pushes):
        pull.wait()
        push.start()
    for push in pushes:
        push.wait()


def place(ids, blocks, wholes):
    n, n_copies = len(blocks), sum(cuts for *_, cuts in blocks)
    return pl.pallas_call(
        functools.partial(place_kernel, tuple(block[1:] for block in blocks), len(wholes)),
        grid_spec=pltpu.PrefetchScalarGridSpec(
            num_scalar_prefetch=1, grid=(), in_specs=[ANY] * (n + len(wholes)), out_specs=[ANY] * len(wholes),
            scratch_shapes=[pltpu.VMEM(arr.shape[1:], arr.dtype) for arr, *_ in blocks] + [pltpu.SemaphoreType.DMA((n_copies,))] * 2),
        out_shape=[jax.ShapeDtypeStruct(arr.shape, arr.dtype) for arr in wholes],
        compiler_params=pltpu.CompilerParams(vmem_limit_bytes=40 << 20),
        input_output_aliases={1 + n + i: i for i in range(len(wholes))},
        name="place",
    )(ids, *(arr for arr, *_ in blocks), *wholes)


def rope_tables(start_pos, chunk_len, key_dim):
    half_dim = key_dim // 2
    inv_freq = jnp.power(ROPE_BASE, -jnp.arange(half_dim).astype(F32) / half_dim)
    starts = (start_pos[:, None] + jnp.arange(0, chunk_len, TILE)[None, :]).astype(F32)
    base = starts[:, :, None, None] * inv_freq
    row = lax.broadcasted_iota(jnp.int32, (1, 1, 8, 1), 2)
    base = jnp.where(row == 0, jnp.cos(base), jnp.sin(base))
    step = jnp.arange(TILE).astype(F32)[None, :, None] * inv_freq
    kind = lax.broadcasted_iota(jnp.int32, (2, 1, 1), 0)
    return base.reshape(start_pos.shape[0], -1, half_dim), jnp.where(kind == 0, jnp.cos(step), jnp.sin(step))


def solution(mesh):
    n_dp = mesh.shape["dp"]

    def swap(axis, bits):
        return functools.partial(lax.ppermute, axis_name=axis, perm=[(i, i ^ bits) for i in range(mesh.shape[axis])])

    to_core, to_chip, to_far = swap("tp", 1), swap("tp", 2), swap("tp", 3)

    def local_layer(x_in, start_pos, kv_state, ln1_gain, ln1_bias, w_q, w_k, w_v, w_g, w_o, ln2_gain, ln2_bias, w_up, w_down):
        tp, group = lax.axis_index("tp"), lax.axis_index("dp")
        chip, core = tp // 2, tp % 2
        other = 1 - core
        chunk_len, d_model = x_in.shape[1:]
        own = kv_state[:, 0]
        key_dim, val_dim = own.shape[1:]

        def head_places(arrs):
            return [(w, (0, col, None)) for w, col in zip(arrs, (0, key_dim, 2 * key_dim, 2 * key_dim + val_dim))]

        def mlp_places(arrs):
            return [(w, at) for w, at in zip(arrs, ((0, 0, None), (val_dim, 0, None), (0, d_model, None)))]

        def heads_gathered(quarters):
            return [(w, (0, 0, flip)) for flip, w in enumerate(quarters)]

        def gather(part):
            return [part] + [swap("dp", flip)(part) for flip in range(1, n_dp)]

        head_w, mlp_w = (w_q, w_k, w_v, w_g), (w_o, w_down, w_up)
        single, twice = 2 * chip + core, 4 + 2 * core
        meta = jnp.stack([single, twice, twice + 1, core, 2 + 2 * core, 3 + 2 * core, group, tp, twice // 2, 2 * (1 - chip)]).astype(jnp.int32)
        wa_core = [to_core(w) for w in head_w]
        s_core = to_core(own)
        wa_part, wb_part, s_part = cut_parts(meta, head_w, mlp_w, own)
        wa_part = to_chip(wa_part)
        wb_part = to_chip(wb_part)
        s_chip = to_chip(s_part)
        wb_core = [to_core(w) for w in mlp_w]

        norms = tuple(v.reshape(1, -1) for v in (ln1_gain, ln1_bias, ln2_gain, ln2_bias))
        common = (x_in, norms, *rope_tables(start_pos, chunk_len, key_dim))
        all_seqs, pair_seqs, one = (SEQ, SEQ + 1, SEQ + 2), (SEQ + 1, SEQ + 2), (SEQ,)

        z_own_single, new_own_single = run(meta, common, one, one, (0,), (own,), (head_places(head_w),))
        z_own_single, wa_part = lax.optimization_barrier((z_own_single, wa_part))
        wa_quarters = gather(wa_part)
        z_own, new_states = run(meta, common, pair_seqs, pair_seqs, (0,), (own,), (head_places(head_w),), pair=True)
        z_own, wa_core, s_core, wb_part = lax.optimization_barrier((z_own, wa_core, s_core, wb_part))
        wb_quarters = gather(wb_part)
        z_core, new_core = run(meta, common, all_seqs, all_seqs, (1,), (s_core,), (head_places(wa_core),))
        z_core, wa_quarters, wb_quarters, s_chip = lax.optimization_barrier((z_core, wa_quarters, wb_quarters, s_chip))
        wa_far, wb_far, s_far = [to_core(w) for w in wa_quarters], [to_core(w) for w in wb_quarters], to_core(s_chip)
        got_core = to_core(new_core)

        w_chip = heads_gathered(wa_quarters)
        z_chip, new_chip = run(meta, common, one, (STATE_SINGLE,), (2,), (s_chip,), (w_chip,))
        z_chip, wa_far, wb_far, wb_core, s_far = lax.optimization_barrier((z_chip, wa_far, wb_far, wb_core, s_far))
        w_far = heads_gathered(wa_far)
        mlp = (mlp_places(mlp_w), mlp_places(wb_core), heads_gathered(wb_quarters), heads_gathered(wb_far))
        whole, x_single, new_far = run(meta, common, one, (STATE_SINGLE,), (3,), (s_far,), (w_far, *mlp), ((z_own_single, 0), (z_core, 0), (z_chip, 0)))
        x_single_chip = to_chip(x_single)
        x_single_core = to_core(x_single)
        got_chip = to_chip(new_chip)
        got_far = to_far(new_far)
        far = ((2, 3), (s_chip, s_far), (w_chip, w_far, *mlp))
        whole, x_a, _, _ = run(meta, common, (SEQ + 1,), (STATE_TWICE,), *far, ((z_own, 0), (z_core, 1)), whole)
        x_a_core = to_core(x_a)
        whole, x_b, _, _ = run(meta, common, (SEQ + 2,), (STATE_TWICE + 1,), *far, ((z_own, 1), (z_core, 2)), whole)
        x_b_core = to_core(x_b)
        x_single_far = to_core(x_single_chip)

        single_o, twice_o = 2 * chip + other, 4 + 2 * other
        far_c, far_o = 2 * (1 - chip) + core, 2 * (1 - chip) + other
        ids = jnp.stack([single_o, twice_o, far_c, single, single_o, twice_o, twice_o + 1, far_c, far_o, far_o, twice_o + 1]).astype(jnp.int32)
        cuts = chunk_len // TILE
        near = [(x_single_core, 0, 0, cuts), (x_a_core, 0, 0, cuts), (x_single_chip, 0, 0, cuts)]
        near += [(arr, at, 1, 1) for arr, at in ((new_own_single, 0), (got_core, 0), (got_core, 1), (got_core, 2), (got_chip, 0), (got_far, 0))]
        whole, new_states = place(ids[:9], near, (whole, new_states))
        whole, = place(ids[9:], [(x_single_far, 0, 0, cuts), (x_b_core, 0, 0, cuts)], (whole,))
        return whole, new_states[:, None]

    in_specs = (P("dp", None, None), P("dp"), P("dp", "tp", None, None), P(), P(), P(None, "tp"), P(None, "tp"), P(None, "tp"), P(None, "tp"), P("tp", None), P(), P(), P(None, "tp"), P("tp", None))
    out_specs = (P("dp", None, None), P("dp", "tp", None, None))
    return jax.shard_map(local_layer, mesh=mesh, in_specs=in_specs, out_specs=out_specs, check_vma=False)
```

time: 468 us -> 418 us (0.89)
  waiting for transfers between devices: 101 us -> 83.8 us
  local copies, waits for them, and re-layouts: 15 us -> 3.81 us
  Pallas kernels: 316 us -> 307 us
  other arithmetic: 10.1 us -> 2.49 us
    ppermute x6, waiting for transfers between devices: 44.8 us -> 11.4 us  [gather(): return [part] + [swap('dp', flip)(part) for flip in range(1, n_dp)]]
    ppermute x14 -> x12, waiting for transfers between devices: 24.5 us -> 35.7 us  [the longest x1 32.7 us: local_layer(): wa_part = to_chip(wa_part)]
    pallas_call x8 -> x10, Pallas kernels: 316 us -> 307 us  [the longest x7 284 us: run(): pl.pallas_call(functools.partial(kernel_body, n, tuple(heads), len(zs), t...]
    ppermute x3, waiting for transfers between devices: 0.01 us -> 7.97 us  [local_layer(): wb_core = [to_core(w) for w in mlp_w]]
    dynamic_slice x6 -> x0, local copies, waits for them, and re-layouts: 6.14 us -> none  [rows_of(): return lax.dynamic_slice_in_dim(w, i * n, n, axis=0)]
  transfers between devices with their start and end apart: 36 -> 34, of which waited for: 14 -> 12; matrix products, arithmetic and copies ran while one was open for 4% -> 1% of each run, Pallas kernels for 52% -> 59%
where the time goes in v3:
time: 418 us
  Pallas kernels  307 us (73%)
  waiting for transfers between devices  83.8 us (20%)
  starting transfers between devices  19.7 us (5%)
    pallas_call x7, Pallas kernels, run(): pl.pallas_call(functools.partial(kernel_body, n, tuple(heads), len(zs), t...  284 us
    ppermute x1, waiting for transfers between devices, local_layer(): wa_part = to_chip(wa_part)  32.7 us
    pallas_call x2, Pallas kernels, place(): pl.pallas_call(functools.partial(place_kernel, tuple((block[1:] for block...  18.2 us
    ppermute x1, waiting for transfers between devices, local_layer(): got_far = to_far(new_far)  12.8 us
    ppermute x1, waiting for transfers between devices, local_layer(): got_chip = to_chip(new_chip)  12.5 us
    ppermute x6, waiting for transfers between devices, gather(): return [part] + [swap('dp', flip)(part) for flip in range(1, n_dp)]  11.4 us
  transfers between devices with their start and end apart: 34, of which 12 were waited for; matrix products, arithmetic and copies ran while one was open for 1% of the time, Pallas kernels for 59%

profile of v3, /device:TPU:0, one launch (start us, length us, event | category | flops | bytes accessed | tf_op | source)
XLA Modules:
  0.0 418.1 jit_solution(9770463485409519768)
XLA Ops:
  2.6 5.4 %parts.1 = (bf16[256,1536]{1,0:T(8,128)(2,1)}, bf16[256,1536]{1,0:T(8,128)(2,1)}, f32[6,256,512]{2,1,0:T(8,128)}) custom-call(s32[10]{0:T(128)} %stack.72.meta_ref, bf16[1024,256]{1,0:T(8,128)(2,1)} %refs_3_.1, bf16[1024,256]{1,0:T(8,128)(2,1)} %refs_4_.1, bf16[1024,512]{1,0:T(8,128)(2,1)} %refs_5_.1, bf16[1024,512]{1,0:T(8,128)(2,1)} %refs_6_.3, ...), custom_call_target="tpu_custom_call" | custom-call | tf_op jit(solution)/shard_map/parts/pallas_call | solution.py:233
  8.0 2.6 collective-permute-start.5
  13.2 32.7 %collective-permute-done.6.refs_3_.refs_6_ = bf16[256,1536]{1,0:T(8,128)(2,1)} collective-permute-done((bf16[256,1536]{1,0:T(8,128)(2,1)}, bf16[256,1536]{1,0:T(8,128)(2,1)}, u32[]{:S(2)}, u32[]{:S(2)}) %collective-permute-start.6) | collective-permute-done | bytes 786464 | tf_op jit(solution)/shard_map/ppermute | solution.py:322
  45.9 17.8 %heads.6 = (bf16[1,2048,512]{2,1,0:T(8,128)(2,1)}, f32[1,256,512]{2,1,0:T(8,128)}) custom-call(s32[10]{0:T(128)} %stack.72.meta_ref, f32[1,1024]{1,0:T(1,128)} %bitcast.33, f32[1,1024]{1,0:T(1,128)} %bitcast.40, f32[1,1024]{1,0:T(1,128)} %bitcast.47, f32[1,1024]{1,0:T(1,128)} %bitcast.54, f32[2,256,128]{2,1,0:T(8,128)} %broadcast_select_fusion.step_ref, ...), custom_call_target="tpu_custom_call" | custom-call | flops 8321499136 | bytes 8388608 | tf_op jit(solution)/shard_map/heads/pallas_call | solution.py:188
  65.3 1.7 collective-permute-start.13
  67.1 1.5 collective-permute-start.7
  68.6 1.6 collective-permute-start.8
  70.2 27.8 %heads.4 = (bf16[2,2048,512]{2,1,0:T(8,128)(2,1)}, f32[8,256,512]{2,1,0:T(8,128)}) custom-call(s32[10]{0:T(128)} %stack.72.meta_ref, f32[1,1024]{1,0:T(1,128)} %bitcast.34, f32[1,1024]{1,0:T(1,128)} %bitcast.41, f32[1,1024]{1,0:T(1,128)} %bitcast.48, f32[1,1024]{1,0:T(1,128)} %bitcast.55, f32[2,256,128]{2,1,0:T(8,128)} %broadcast_select_fusion.step_ref, ...), custom_call_target="tpu_custom_call" | custom-call | flops 16642998272 | bytes 16777216 | tf_op jit(solution)/shard_map/heads/pallas_call | solution.py:188
  98.5 1.5 collective-permute-start.10
  100.0 1.6 collective-permute-start.11
  102.0 38.7 %heads.5 = (bf16[3,2048,512]{2,1,0:T(8,128)(2,1)}, f32[3,256,512]{2,1,0:T(8,128)}) custom-call(s32[10]{0:T(128)} %stack.72.meta_ref, f32[1,1024]{1,0:T(1,128)} %bitcast.35, f32[1,1024]{1,0:T(1,128)} %bitcast.42, f32[1,1024]{1,0:T(1,128)} %bitcast.49, f32[1,1024]{1,0:T(1,128)} %bitcast.56, f32[2,256,128]{2,1,0:T(8,128)} %broadcast_select_fusion.step_ref, ...), custom_call_target="tpu_custom_call" | custom-call | flops 24964497408 | bytes 25165824 | tf_op jit(solution)/shard_map/heads/pallas_call | solution.py:188
  140.8 11.4 %collective-permute-done.12.refs_19_.refs_23_ = bf16[256,1536]{1,0:T(8,128)(2,1)} collective-permute-done((bf16[256,1536]{1,0:T(8,128)(2,1)}, bf16[256,1536]{1,0:T(8,128)(2,1)}, u32[]{:S(2)}, u32[]{:S(2)}) %collective-permute-start.12) | collective-permute-done | bytes 786464 | tf_op jit(solution)/shard_map/ppermute | solution.py:314
  153.2 6.1 %collective-permute-done.22.refs_13_.refs_17_ = bf16[512,1024]{1,0:T(8,128)(2,1)S(1)} collective-permute-done((bf16[512,1024]{1,0:T(8,128)(2,1)S(1)}, bf16[512,1024]{1,0:T(8,128)(2,1)S(1)}, u32[]{:S(2)}, u32[]{:S(2)}) %collective-permute-start.22) | collective-permute-done | bytes 1048608 | tf_op jit(solution)/shard_map/ppermute | solution.py:325
  159.4 1.4 collective-permute-done.23.refs_14_.refs_18_
  167.1 17.6 %heads.7 = (bf16[1,2048,512]{2,1,0:T(8,128)(2,1)}, f32[1,256,512]{2,1,0:T(8,128)}) custom-call(s32[10]{0:T(128)} %stack.72.meta_ref, f32[1,1024]{1,0:T(1,128)} %bitcast.36, f32[1,1024]{1,0:T(1,128)} %bitcast.43, f32[1,1024]{1,0:T(1,128)} %bitcast.50, f32[1,1024]{1,0:T(1,128)} %bitcast.57, f32[2,256,128]{2,1,0:T(8,128)} %broadcast_select_fusion.step_ref, ...), custom_call_target="tpu_custom_call" | custom-call | flops 8321499136 | bytes 8388608 | tf_op jit(solution)/shard_map/heads/pallas_call | solution.py:188
  184.7 54.2 %tail.3 = (bf16[8,2048,1024]{2,1,0:T(8,128)(2,1)}, bf16[1,2048,1024]{2,1,0:T(8,128)(2,1)}, f32[1,256,512]{2,1,0:T(8,128)}) custom-call(s32[10]{0:T(128)} %stack.72.meta_ref, f32[1,1024]{1,0:T(1,128)} %bitcast.37, f32[1,1024]{1,0:T(1,128)} %bitcast.44, f32[1,1024]{1,0:T(1,128)} %bitcast.51, f32[1,1024]{1,0:T(1,128)} %bitcast.58, ...), custom_call_target="tpu_custom_call" | custom-call | flops 34091302912 | bytes 16777216 | tf_op jit(solution)/shard_map/tail/pallas_call | solution.py:188
  239.6 63.6 %tail.4 = (bf16[8,2048,1024]{2,1,0:T(8,128)(2,1)}, bf16[1,2048,1024]{2,1,0:T(8,128)(2,1)}, f32[1,256,512]{2,1,0:T(8,128)}, f32[1,256,512]{2,1,0:T(8,128)}) custom-call(s32[10]{0:T(128)} %stack.72.meta_ref, f32[1,1024]{1,0:T(1,128)} %bitcast.38, f32[1,1024]{1,0:T(1,128)} %bitcast.45, f32[1,1024]{1,0:T(1,128)} %bitcast.52, ...), custom_call_target="tpu_custom_call", output_to_operand_aliasing={{0}: (34, {})} | custom-call | flops 42412802048 | bytes 16777216 | tf_op jit(solution)/shard_map/tail/pallas_call | solution.py:188
  303.7 63.9 %tail.5 = (bf16[8,2048,1024]{2,1,0:T(8,128)(2,1)}, bf16[1,2048,1024]{2,1,0:T(8,128)(2,1)}, f32[1,256,512]{2,1,0:T(8,128)}, f32[1,256,512]{2,1,0:T(8,128)}) custom-call(s32[10]{0:T(128)} %stack.72.meta_ref, f32[1,1024]{1,0:T(1,128)} %bitcast.39, f32[1,1024]{1,0:T(1,128)} %bitcast.46, f32[1,1024]{1,0:T(1,128)} %bitcast.53, ...), custom_call_target="tpu_custom_call", output_to_operand_aliasing={{0}: (34, {})} | custom-call | flops 42412802048 | bytes 16777216 | tf_op jit(solution)/shard_map/tail/pallas_call | solution.py:188
  368.2 1.5 collective-permute-start.32
  369.7 12.5 %collective-permute-done.32.refs_7_ = f32[1,256,512]{2,1,0:T(8,128)S(1)} collective-permute-done((f32[1,256,512]{2,1,0:T(8,128)S(1)}, f32[1,256,512]{2,1,0:T(8,128)S(1)}, u32[]{:S(2)}, u32[]{:S(2)}) %collective-permute-start.32) | collective-permute-done | bytes 524320 | tf_op jit(solution)/shard_map/ppermute | solution.py:350
  382.2 3.4 collective-permute-done.31.refs_4_.refs_5_.refs_6_
  386.9 12.8 %collective-permute-done.33.refs_8_ = f32[1,256,512]{2,1,0:T(8,128)S(1)} collective-permute-done((f32[1,256,512]{2,1,0:T(8,128)}, f32[1,256,512]{2,1,0:T(8,128)S(1)}, u32[]{:S(2)}, u32[]{:S(2)}) %collective-permute-start.33) | collective-permute-done | bytes 524320 | tf_op jit(solution)/shard_map/ppermute | solution.py:351
  399.7 11.1 %place.2 = (bf16[8,2048,1024]{2,1,0:T(8,128)(2,1)}, f32[8,256,512]{2,1,0:T(8,128)}) custom-call(s32[9]{0:T(128)S(1)} %stack.76.ids_ref, bf16[1,2048,1024]{2,1,0:T(8,128)(2,1)} %collective-permute-done.29.refs_0_, bf16[1,2048,1024]{2,1,0:T(8,128)(2,1)} %collective-permute-done.30.refs_1_, ...), custom_call_target="tpu_custom_call", output_to_operand_aliasing={{0}: (10, {}), {1}: (11, {})} | custom-call | tf_op jit(solution)/shard_map/place/pallas_call | solution.py:264
  410.8 7.1 %place.3 = bf16[8,2048,1024]{2,1,0:T(8,128)(2,1)} custom-call(s32[2]{0:T(128)S(1)} %pad_add_fusion.ids_ref, bf16[1,2048,1024]{2,1,0:T(8,128)(2,1)} %collective-permute-done.27.refs_0_, bf16[1,2048,1024]{2,1,0:T(8,128)(2,1)} %collective-permute-done.28.refs_1_, bf16[8,2048,1024]{2,1,0:T(8,128)(2,1)} %get-tuple-element.104.refs_2_), custom_call_target="tpu_custom_call", output_to_operand_aliasing={{}: (3, {})} | custom-call | tf_op jit(solution)/shard_map/place/pallas_call | solution.py:264
  (105 shorter events, 17.6 us)
Async XLA Ops:
  0.6 97.9 %collective-permute-start.4 = (f32[8,256,512]{2,1,0:T(8,128)}, f32[8,256,512]{2,1,0:T(8,128)}, u32[]{:S(2)}, u32[]{:S(2)}) collective-permute-start(f32[8,256,512]{2,1,0:T(8,128)} %bitcast.27), channel_id=1, source_target_pairs={{0,1},{1,0},{2,3},{3,2},{4,5},{5,4},{6,7},{7,6},{8,9},{9,8},{10,11... | collective-permute-start | bytes 12582920 | tf_op jit(solution)/shard_map/ppermute | solution.py:320
  1.4 67.2 %collective-permute-start.2 = (bf16[1024,512]{1,0:T(8,128)(2,1)}, bf16[1024,512]{1,0:T(8,128)(2,1)S(1)}, u32[]{:S(2)}, u32[]{:S(2)}) collective-permute-start(bf16[1024,512]{1,0:T(8,128)(2,1)} %refs_5_.1), channel_id=1, source_target_pairs={{0,1},{1,0},{2,3},{3,2},{4,5},{5,4},{6,7},{7,6},{8,9},{9,8},{10,11... | collective-permute-start | bytes 3145736 | tf_op jit(solution)/shard_map/ppermute | solution.py:319
  1.4 62.3 %collective-permute-start = (bf16[1024,256]{1,0:T(8,128)(2,1)}, bf16[1024,256]{1,0:T(8,128)(2,1)S(1)}, u32[]{:S(2)}, u32[]{:S(2)}) collective-permute-start(bf16[1024,256]{1,0:T(8,128)(2,1)} %refs_3_.1), channel_id=1, source_target_pairs={{0,1},{1,0},{2,3},{3,2},{4,5},{5,4},{6,7},{7,6},{8,9},{9,8},{10,11... | collective-permute-start | bytes 1572872 | tf_op jit(solution)/shard_map/ppermute | solution.py:319
  8.0 59.1 %collective-permute-start.5 = (bf16[256,1536]{1,0:T(8,128)(2,1)}, bf16[256,1536]{1,0:T(8,128)(2,1)S(1)}, u32[]{:S(2)}, u32[]{:S(2)}) collective-permute-start(bf16[256,1536]{1,0:T(8,128)(2,1)} %get-tuple-element.55), channel_id=1, source_target_pairs={{0,2},{1,3},{2,0},{3,1},{4,6},{5,7},{6,4},{7,5},{8,10},{9,11},{10,... | collective-permute-start | bytes 2359304 | tf_op jit(solution)/shard_map/ppermute | solution.py:323
  10.6 35.3 %collective-permute-start.6 = (bf16[256,1536]{1,0:T(8,128)(2,1)}, bf16[256,1536]{1,0:T(8,128)(2,1)}, u32[]{:S(2)}, u32[]{:S(2)}) collective-permute-start(bf16[256,1536]{1,0:T(8,128)(2,1)} %get-tuple-element.63), channel_id=1, source_target_pairs={{0,2},{1,3},{2,0},{3,1},{4,6},{5,7},{6,4},{7,5},{8,10},{9,11},{10,... | collective-permute-start | bytes 2359304 | tf_op jit(solution)/shard_map/ppermute | solution.py:322
  45.9 18.4 %collective-permute-start.1 = (bf16[1024,256]{1,0:T(8,128)(2,1)S(1)}, bf16[1024,256]{1,0:T(8,128)(2,1)S(1)}, u32[]{:S(2)}, u32[]{:S(2)}) collective-permute-start(bf16[1024,256]{1,0:T(8,128)(2,1)S(1)} %copy-done.2), channel_id=1, source_target_pairs={{0,1},{1,0},{2,3},{3,2},{4,5},{5,4},{6,7},{7,6},{8,9},{9,8},{10,11... | collective-permute-start | bytes 1572872 | tf_op jit(solution)/shard_map/ppermute | solution.py:319
  63.8 34.3 %collective-permute-start.3 = (bf16[1024,512]{1,0:T(8,128)(2,1)S(1)}, bf16[1024,512]{1,0:T(8,128)(2,1)}, u32[]{:S(2)}, u32[]{:S(2)}) collective-permute-start(bf16[1024,512]{1,0:T(8,128)(2,1)S(1)} %copy-done.1), channel_id=1, source_target_pairs={{0,1},{1,0},{2,3},{3,2},{4,5},{5,4},{6,7},{7,6},{8,9},{9,8},{10,11... | collective-permute-start | bytes 3145736 | tf_op jit(solution)/shard_map/ppermute | solution.py:319
  65.3 75.4 %collective-permute-start.13 = (f32[6,256,512]{2,1,0:T(8,128)}, f32[6,256,512]{2,1,0:T(8,128)S(1)}, u32[]{:S(2)}, u32[]{:S(2)}) collective-permute-start(f32[6,256,512]{2,1,0:T(8,128)} %get-tuple-element.66), channel_id=1, source_target_pairs={{0,2},{1,3},{2,0},{3,1},{4,6},{5,7},{6,4},{7,5},{8,10},{9,11},{10,... | collective-permute-start | bytes 9437192 | tf_op jit(solution)/shard_map/ppermute | solution.py:324
  67.1 32.9 %collective-permute-start.7 = (bf16[256,1536]{1,0:T(8,128)(2,1)}, bf16[256,1536]{1,0:T(8,128)(2,1)}, u32[]{:S(2)}, u32[]{:S(2)}) collective-permute-start(bf16[256,1536]{1,0:T(8,128)(2,1)} %collective-permute-done.6.refs_3_.refs_6_), channel_id=1, source_target_pairs={{0,4},{4,0},{8,12},{12,8},{1,5},{5,1},{9,13},{13,9},{2,6},{6,2},{1... | collective-permute-start | bytes 2359304 | tf_op jit(solution)/shard_map/ppermute | solution.py:314
  68.6 33.0 %collective-permute-start.8 = (bf16[256,1536]{1,0:T(8,128)(2,1)}, bf16[256,1536]{1,0:T(8,128)(2,1)}, u32[]{:S(2)}, u32[]{:S(2)}) collective-permute-start(bf16[256,1536]{1,0:T(8,128)(2,1)} %collective-permute-done.6.refs_3_.refs_6_), channel_id=1, source_target_pairs={{0,8},{4,12},{8,0},{12,4},{1,9},{5,13},{9,1},{13,5},{2,10},{6,14},... | collective-permute-start | bytes 2359304 | tf_op jit(solution)/shard_map/ppermute | solution.py:314
  98.0 42.7 %collective-permute-start.9 = (bf16[256,1536]{1,0:T(8,128)(2,1)}, bf16[256,1536]{1,0:T(8,128)(2,1)}, u32[]{:S(2)}, u32[]{:S(2)}) collective-permute-start(bf16[256,1536]{1,0:T(8,128)(2,1)} %collective-permute-done.6.refs_3_.refs_6_), channel_id=1, source_target_pairs={{0,12},{4,8},{8,4},{12,0},{1,13},{5,9},{9,5},{13,1},{2,14},{6,10},... | collective-permute-start | bytes 2359304 | tf_op jit(solution)/shard_map/ppermute | solution.py:314
  98.5 42.2 %collective-permute-start.10 = (bf16[256,1536]{1,0:T(8,128)(2,1)}, bf16[256,1536]{1,0:T(8,128)(2,1)}, u32[]{:S(2)}, u32[]{:S(2)}) collective-permute-start(bf16[256,1536]{1,0:T(8,128)(2,1)} %copy-done.14), channel_id=1, source_target_pairs={{0,4},{4,0},{8,12},{12,8},{1,5},{5,1},{9,13},{13,9},{2,6},{6,2},{1... | collective-permute-start | bytes 2359304 | tf_op jit(solution)/shard_map/ppermute | solution.py:314
  100.0 40.7 %collective-permute-start.11 = (bf16[256,1536]{1,0:T(8,128)(2,1)}, bf16[256,1536]{1,0:T(8,128)(2,1)}, u32[]{:S(2)}, u32[]{:S(2)}) collective-permute-start(bf16[256,1536]{1,0:T(8,128)(2,1)} %copy-done.14), channel_id=1, source_target_pairs={{0,8},{4,12},{8,0},{12,4},{1,9},{5,13},{9,1},{13,5},{2,10},{6,14},... | collective-permute-start | bytes 2359304 | tf_op jit(solution)/shard_map/ppermute | solution.py:314
  101.6 50.6 %collective-permute-start.12 = (bf16[256,1536]{1,0:T(8,128)(2,1)}, bf16[256,1536]{1,0:T(8,128)(2,1)}, u32[]{:S(2)}, u32[]{:S(2)}) collective-permute-start(bf16[256,1536]{1,0:T(8,128)(2,1)} %copy-done.14), channel_id=1, source_target_pairs={{0,12},{4,8},{8,4},{12,0},{1,13},{5,9},{9,5},{13,1},{2,14},{6,10},... | collective-permute-start | bytes 2359304 | tf_op jit(solution)/shard_map/ppermute | solution.py:314
  152.1 32.6 %collective-permute-start.25 = (f32[6,256,512]{2,1,0:T(8,128)S(1)}, f32[6,256,512]{2,1,0:T(8,128)}, u32[]{:S(2)}, u32[]{:S(2)}) collective-permute-start(f32[6,256,512]{2,1,0:T(8,128)S(1)} %collective-permute-done.13.refs_2_), channel_id=1, source_target_pairs={{0,1},{1,0},{2,3},{3,2},{4,5},{5,4},{6,7},{7,6},{8,9},{9,8},{10,11... | collective-permute-start | bytes 9437192 | tf_op jit(solution)/shard_map/ppermute | solution.py:339
  163.6 21.1 %collective-permute-start.18 = (bf16[256,1536]{1,0:T(8,128)(2,1)}, bf16[256,1536]{1,0:T(8,128)(2,1)}, u32[]{:S(2)}, u32[]{:S(2)}) collective-permute-start(bf16[256,1536]{1,0:T(8,128)(2,1)} %copy-done.14), channel_id=1, source_target_pairs={{0,1},{1,0},{2,3},{3,2},{4,5},{5,4},{6,7},{7,6},{8,9},{9,8},{10,11... | collective-permute-start | bytes 2359304 | tf_op jit(solution)/shard_map/ppermute | solution.py:339
  164.6 20.2 %collective-permute-start.19 = (bf16[256,1536]{1,0:T(8,128)(2,1)}, bf16[256,1536]{1,0:T(8,128)(2,1)}, u32[]{:S(2)}, u32[]{:S(2)}) collective-permute-start(bf16[256,1536]{1,0:T(8,128)(2,1)} %collective-permute-done.10.refs_17_.refs_21_), channel_id=1, source_target_pairs={{0,1},{1,0},{2,3},{3,2},{4,5},{5,4},{6,7},{7,6},{8,9},{9,8},{10,11... | collective-permute-start | bytes 2359304 | tf_op jit(solution)/shard_map/ppermute | solution.py:339
  165.7 19.0 %collective-permute-start.20 = (bf16[256,1536]{1,0:T(8,128)(2,1)}, bf16[256,1536]{1,0:T(8,128)(2,1)}, u32[]{:S(2)}, u32[]{:S(2)}) collective-permute-start(bf16[256,1536]{1,0:T(8,128)(2,1)} %collective-permute-done.11.refs_18_.refs_22_), channel_id=1, source_target_pairs={{0,1},{1,0},{2,3},{3,2},{4,5},{5,4},{6,7},{7,6},{8,9},{9,8},{10,11... | collective-permute-start | bytes 2359304 | tf_op jit(solution)/shard_map/ppermute | solution.py:339
  166.9 17.8 %collective-permute-start.21 = (bf16[256,1536]{1,0:T(8,128)(2,1)}, bf16[256,1536]{1,0:T(8,128)(2,1)}, u32[]{:S(2)}, u32[]{:S(2)}) collective-permute-start(bf16[256,1536]{1,0:T(8,128)(2,1)} %collective-permute-done.12.refs_19_.refs_23_), channel_id=1, source_target_pairs={{0,1},{1,0},{2,3},{3,2},{4,5},{5,4},{6,7},{7,6},{8,9},{9,8},{10,11... | collective-permute-start | bytes 2359304 | tf_op jit(solution)/shard_map/ppermute | solution.py:339
  239.0 128.8 %collective-permute-start.26 = (bf16[1,2048,1024]{2,1,0:T(8,128)(2,1)}, bf16[1,2048,1024]{2,1,0:T(8,128)(2,1)}, u32[]{:S(2)}, u32[]{:S(2)}) collective-permute-start(bf16[1,2048,1024]{2,1,0:T(8,128)(2,1)} %get-tuple-element.92), channel_id=1, source_target_pairs={{0,2},{1,3},{2,0},{3,1},{4,6},{5,7},{6,4},{7,5},{8,10},{9,11},{10,... | collective-permute-start | bytes 12582920 | tf_op jit(solution)/shard_map/ppermute | solution.py:348
  239.5 160.1 %collective-permute-start.29 = (bf16[1,2048,1024]{2,1,0:T(8,128)(2,1)}, bf16[1,2048,1024]{2,1,0:T(8,128)(2,1)}, u32[]{:S(2)}, u32[]{:S(2)}) collective-permute-start(bf16[1,2048,1024]{2,1,0:T(8,128)(2,1)} %get-tuple-element.92), channel_id=1, source_target_pairs={{0,1},{1,0},{2,3},{3,2},{4,5},{5,4},{6,7},{7,6},{8,9},{9,8},{10,11... | collective-permute-start | bytes 12582920 | tf_op jit(solution)/shard_map/ppermute | solution.py:349
  303.2 96.5 %collective-permute-start.30 = (bf16[1,2048,1024]{2,1,0:T(8,128)(2,1)}, bf16[1,2048,1024]{2,1,0:T(8,128)(2,1)}, u32[]{:S(2)}, u32[]{:S(2)}) collective-permute-start(bf16[1,2048,1024]{2,1,0:T(8,128)(2,1)} %get-tuple-element.97), channel_id=1, source_target_pairs={{0,1},{1,0},{2,3},{3,2},{4,5},{5,4},{6,7},{7,6},{8,9},{9,8},{10,11... | collective-permute-start | bytes 12582920 | tf_op jit(solution)/shard_map/ppermute | solution.py:354
  367.6 43.1 %collective-permute-start.28 = (bf16[1,2048,1024]{2,1,0:T(8,128)(2,1)}, bf16[1,2048,1024]{2,1,0:T(8,128)(2,1)}, u32[]{:S(2)}, u32[]{:S(2)}) collective-permute-start(bf16[1,2048,1024]{2,1,0:T(8,128)(2,1)} %get-tuple-element.96), channel_id=1, source_target_pairs={{0,1},{1,0},{2,3},{3,2},{4,5},{5,4},{6,7},{7,6},{8,9},{9,8},{10,11... | collective-permute-start | bytes 12582920 | tf_op jit(solution)/shard_map/ppermute | solution.py:356
  367.8 43.0 %collective-permute-start.27 = (bf16[1,2048,1024]{2,1,0:T(8,128)(2,1)}, bf16[1,2048,1024]{2,1,0:T(8,128)(2,1)}, u32[]{:S(2)}, u32[]{:S(2)}) collective-permute-start(bf16[1,2048,1024]{2,1,0:T(8,128)(2,1)} %collective-permute-done.26.refs_2_), channel_id=1, source_target_pairs={{0,1},{1,0},{2,3},{3,2},{4,5},{5,4},{6,7},{7,6},{8,9},{9,8},{10,11... | collective-permute-start | bytes 12582920 | tf_op jit(solution)/shard_map/ppermute | solution.py:357
  (28 other events, 627.4 us)

commit v4 on v3

--- a/solution.py
+++ b/solution.py
@@ -59,26 +59,29 @@
         rows_ref[i, 2] = jnp.exp(jnp.full((TILE, 128), TILE, F32) * log_gamma)
 
 
-def head_block(h, w_ref, s_ref, inner, rows_ref, cos_t, sin_t):
-    key_dim, val_dim = s_ref.shape
-    q_raw = dot(h, w_ref[:, :key_dim])
-    k_raw = dot(h, w_ref[:, key_dim:2 * key_dim])
-    queries = rotate(q_raw, cos_t, sin_t).astype(BF16)
-    keys = (rotate(k_raw, cos_t, sin_t) * key_dim ** -0.5).astype(BF16)
-    values = dot(h, w_ref[:, 2 * key_dim:2 * key_dim + val_dim]).astype(BF16)
-    scores = lax.dot_general(queries, keys, (((1,), (1,)), ((), ())), preferred_element_type=F32) * inner
-    state = s_ref[...]
-    carried = dot(queries, state.astype(BF16)) * widen(rows_ref[0], val_dim)
-    retained = dot(scores.astype(BF16), values) + carried
-    gates = dot(h, w_ref[:, 2 * key_dim + val_dim:])
-    faded = (keys.astype(F32) * widen(rows_ref[1], key_dim)).astype(BF16)
-    update = lax.dot_general(faded, values, (((0,), (0,)), ((), ())), preferred_element_type=F32)
-    s_ref[...] = state * widen(rows_ref[2, 0:1], val_dim) + update
-    row_mean = jnp.mean(retained, axis=-1, keepdims=True)
-    centered = retained - row_mean
-    variance = jnp.mean(centered * centered, axis=-1, keepdims=True)
-    normed = centered * lax.rsqrt(variance + GROUP_EPS)
-    return (gates * lax.logistic(gates) * normed).astype(BF16)
+def head_blocks(hs, w_ref, state_ref, inner, rows_ref, tables):
+    _, key_dim, val_dim = state_ref.shape
+    out = []
+    for b, h in enumerate(hs):
+        q_raw = dot(h, w_ref[:, :key_dim])
+        k_raw = dot(h, w_ref[:, key_dim:2 * key_dim])
+        queries = rotate(q_raw, *tables[b]).astype(BF16)
+        keys = (rotate(k_raw, *tables[b]) * key_dim ** -0.5).astype(BF16)
+        values = dot(h, w_ref[:, 2 * key_dim:2 * key_dim + val_dim]).astype(BF16)
+        scores = lax.dot_general(queries, keys, (((1,), (1,)), ((), ())), preferred_element_type=F32) * inner
+        state = state_ref[b]
+        carried = dot(queries, state.astype(BF16)) * widen(rows_ref[0], val_dim)
+        retained = dot(scores.astype(BF16), values) + carried
+        gates = dot(h, w_ref[:, 2 * key_dim + val_dim:])
+        faded = (keys.astype(F32) * widen(rows_ref[1], key_dim)).astype(BF16)
+        update = lax.dot_general(faded, values, (((0,), (0,)), ((), ())), preferred_element_type=F32)
+        state_ref[b] = state * widen(rows_ref[2, 0:1], val_dim) + update
+        row_mean = jnp.mean(retained, axis=-1, keepdims=True)
+        centered = retained - row_mean
+        variance = jnp.mean(centered * centered, axis=-1, keepdims=True)
+        normed = centered * lax.rsqrt(variance + GROUP_EPS)
+        out.append((gates * lax.logistic(gates) * normed).astype(BF16))
+    return out
 
 
 def kernel_body(n_seqs, heads, n_z, pieces, with_whole, meta_ref, gain1, bias1, gain2, bias2, step_ref, *refs):
@@ -87,10 +90,10 @@
     def take(n):
         return [next(it) for _ in range(n)]
 
-    x_refs, base_refs, s_refs, z_refs = take(n_seqs), take(n_seqs), [take(n_seqs) for _ in heads], take(n_z)
+    x_refs, base_refs, s_refs, z_refs = take(n_seqs), take(n_seqs), [take(n_seqs) for _ in heads], [take(n_seqs) for _ in range(n_z)]
     sources = [take(len(p)) for p in pieces]
     take(with_whole)
-    outs = take(2 if n_z else 1)
+    outs = take(1 + n_seqs if n_z else 1)
     state_refs = take(len(heads))
     inner_ref, rows_ref, sem = take(3)
     weights = take(len(pieces))
@@ -119,19 +122,16 @@
         normed.append(layer_norm(x_ref[0].astype(F32), gain1[...], bias1[...]).astype(BF16))
         cos_a, sin_a = base_ref[0, pl.ds(at, 1), :], base_ref[0, pl.ds(at + 1, 1), :]
         tables.append((cos_a * cos_b - sin_a * sin_b, sin_a * cos_b + cos_a * sin_b))
-    mixed = []
-    for i in range(len(heads)):
-        for b in range(n_seqs):
-            mixed.append(head_block(normed[b], weights[i], state_refs[i].at[b], inner_ref[i], rows_ref.at[i], *tables[b]))
+    mixed = [head_blocks(normed, weights[i], state_refs[i], inner_ref[i], rows_ref.at[i], tables) for i in range(len(heads))]
     if not n_z:
         for b in range(n_seqs):
-            outs[0][b] = mixed[b]
+            outs[0][b] = mixed[0][b]
         return
-    mixed = [z[0] for z in z_refs] + mixed
+    mixed = [[ref[0] for ref in refs_of] for refs_of in z_refs] + mixed
     blocks = weights[len(heads):]
-    val_dim, d_model = mixed[0].shape[1], x_refs[0].shape[2]
-    u = sum(dot(z, wb[:val_dim, :d_model]) for z, wb in zip(mixed, blocks))
-    x_mid = (x_refs[0][0].astype(F32) + u.astype(BF16).astype(F32)).astype(BF16)
+    val_dim, d_model = mixed[0][0].shape[1], x_refs[0].shape[2]
+    u = sum(dot(below(z), wb[:val_dim, :d_model]) for z, wb in zip(mixed, blocks))
+    x_mid = (below([x_ref[0] for x_ref in x_refs]).astype(F32) + u.astype(BF16).astype(F32)).astype(BF16)
     h_two = layer_norm(x_mid.astype(F32), gain2[...], bias2[...]).astype(BF16)
     f = jnp.zeros(u.shape, F32)
     for wb in blocks:
@@ -139,8 +139,13 @@
         act = (up * 0.5 * (1.0 + lax.erf(up * 0.5 ** 0.5))).astype(BF16)
         f = f + dot(act, wb[val_dim:, :d_model])
     x_out = (x_mid.astype(F32) + f.astype(BF16).astype(F32)).astype(BF16)
-    outs[0][0] = x_out
-    outs[1][0] = x_out
+    for b in range(n_seqs):
+        outs[0][b] = x_out[b * TILE:(b + 1) * TILE]
+        outs[1 + b][0] = x_out[b * TILE:(b + 1) * TILE]
+
+
+def below(blocks):
+    return blocks[0] if len(blocks) == 1 else jnp.concatenate(blocks, axis=0)
 
 
 def run(meta, common, seqs, state_rows, heads, states, weights, zs=(), whole=None, pair=False):
@@ -165,8 +170,9 @@
     for state in states:
         specs += [row_spec(state.shape[1:], at) for at in state_rows]
         args += [state] * n
-    specs += [tile_of(val_dim, 1, at) for _, at in zs]
-    args += [z for z, _ in zs]
+    for z, first in zs:
+        specs += [tile_of(val_dim, 1, first + b) for b in range(n)]
+        args += [z] * n
     pieces = []
     for weight in weights:
         pieces.append(tuple(place for _, place in weight))
@@ -178,13 +184,14 @@
         args.append(whole)
         specs.append(ANY)
     if zs:
-        outs = [(token_spec(seqs[0]), jax.ShapeDtypeStruct(x.shape, BF16)), (tile_of(d_model), jax.ShapeDtypeStruct((1, chunk_len, d_model), BF16))]
+        whole_spec = token_spec(seqs[0]) if n == 1 else pl.BlockSpec((n, TILE, d_model), lambda t, m: (m[PAIR], t, 0))
+        outs = [(whole_spec, jax.ShapeDtypeStruct(x.shape, BF16))] + [(tile_of(d_model), jax.ShapeDtypeStruct((1, chunk_len, d_model), BF16))] * n
     else:
         outs = [(tile_of(val_dim, n), jax.ShapeDtypeStruct((n, chunk_len, val_dim), BF16))]
     state_out = pl.BlockSpec((n, key_dim, val_dim), lambda t, m: (m[PAIR] if pair else 0, 0, 0))
     outs += [(state_out, jax.ShapeDtypeStruct((x.shape[0] if pair else n, key_dim, val_dim), F32))] * len(heads)
     flops = n * len(heads) * 2 * (d_model * (2 * key_dim + 2 * val_dim) + TILE * (key_dim + val_dim) + 2 * key_dim * val_dim)
-    flops += 24 * d_model * val_dim if zs else 0
+    flops += n * 24 * d_model * val_dim if zs else 0
     return pl.pallas_call(
         functools.partial(kernel_body, n, tuple(heads), len(zs), tuple(pieces), whole is not None),
         grid_spec=pltpu.PrefetchScalarGridSpec(
@@ -199,7 +206,7 @@
     )(meta, *args)
 
 
-def parts_kernel(meta_ref, w_q, w_k, w_v, w_g, w_o, w_down, w_up, own, heads_ref, mlp_ref, states_ref, sem):
+def parts_kernel(meta_ref, w_q, w_k, w_v, w_g, w_o, w_down, w_up, own, heads_ref, mlp_ref, single_ref, twice_ref, sem):
     rows, group = heads_ref.shape[0], meta_ref[GROUP]
     at = pl.ds(pl.multiple_of(group * rows, rows), rows)
     half = pl.ds(pl.multiple_of((group % 2) * rows, rows), rows)
@@ -209,8 +216,8 @@
         copies.append(pltpu.make_async_copy(w.at[at], heads_ref.at[:, pl.ds(col, w.shape[1])], sem.at[len(copies)]))
         col += w.shape[1]
     copies.append(pltpu.make_async_copy(w_up.at[at], mlp_ref.at[:, pl.ds(d_model, w_up.shape[1])], sem.at[len(copies)]))
-    copies.append(pltpu.make_async_copy(own.at[pl.ds(meta_ref[OTHER_CHIP], 2)], states_ref.at[pl.ds(0, 2)], sem.at[len(copies)]))
-    copies.append(pltpu.make_async_copy(own.at[pl.ds(4, 4)], states_ref.at[pl.ds(2, 4)], sem.at[len(copies)]))
+    copies.append(pltpu.make_async_copy(own.at[pl.ds(meta_ref[OTHER_CHIP], 2)], single_ref, sem.at[len(copies)]))
+    copies.append(pltpu.make_async_copy(own.at[pl.ds(4, 4)], twice_ref, sem.at[len(copies)]))
     for copy in copies:
         copy.start()
     last = [pltpu.make_async_copy(w.at[half], mlp_ref.at[:, pl.ds(0, d_model)], sem.at[len(copies)]) for w in (w_o, w_down)]
@@ -229,10 +236,10 @@
 
 def cut_parts(meta, head_w, mlp_w, own):
     n_rows = mlp_w[0].shape[0] // 2
-    shapes = [((n_rows, sum(w.shape[1] for w in head_w)), BF16), ((n_rows, mlp_w[0].shape[1] + mlp_w[2].shape[1]), BF16), ((6,) + own.shape[1:], F32)]
+    shapes = [((n_rows, sum(w.shape[1] for w in head_w)), BF16), ((n_rows, mlp_w[0].shape[1] + mlp_w[2].shape[1]), BF16), ((2,) + own.shape[1:], F32), ((4,) + own.shape[1:], F32)]
     return pl.pallas_call(
         parts_kernel,
-        grid_spec=pltpu.PrefetchScalarGridSpec(num_scalar_prefetch=1, grid=(), in_specs=[ANY] * 8, out_specs=[pl.BlockSpec(memory_space=pltpu.VMEM)] * 3,
+        grid_spec=pltpu.PrefetchScalarGridSpec(num_scalar_prefetch=1, grid=(), in_specs=[ANY] * 8, out_specs=[pl.BlockSpec(memory_space=pltpu.VMEM)] * 4,
                                                scratch_shapes=[pltpu.SemaphoreType.DMA((8,))]),
         out_shape=[jax.ShapeDtypeStruct(shape, dtype) for shape, dtype in shapes],
         name="parts",
@@ -315,13 +322,14 @@
 
         head_w, mlp_w = (w_q, w_k, w_v, w_g), (w_o, w_down, w_up)
         single, twice = 2 * chip + core, 4 + 2 * core
-        meta = jnp.stack([single, twice, twice + 1, core, 2 + 2 * core, 3 + 2 * core, group, tp, twice // 2, 2 * (1 - chip)]).astype(jnp.int32)
+        meta = jnp.stack([single, twice, twice + 1, core, 2 * core, 2 * core + 1, group, tp, twice // 2, 2 * (1 - chip)]).astype(jnp.int32)
         wa_core = [to_core(w) for w in head_w]
         s_core = to_core(own)
-        wa_part, wb_part, s_part = cut_parts(meta, head_w, mlp_w, own)
+        wa_part, wb_part, su_part, st_part = cut_parts(meta, head_w, mlp_w, own)
         wa_part = to_chip(wa_part)
         wb_part = to_chip(wb_part)
-        s_chip = to_chip(s_part)
+        su_chip = to_chip(su_part)
+        st_chip = to_chip(st_part)
         wb_core = [to_core(w) for w in mlp_w]
 
         norms = tuple(v.reshape(1, -1) for v in (ln1_gain, ln1_bias, ln2_gain, ln2_bias))
@@ -335,35 +343,38 @@
         z_own, wa_core, s_core, wb_part = lax.optimization_barrier((z_own, wa_core, s_core, wb_part))
         wb_quarters = gather(wb_part)
         z_core, new_core = run(meta, common, all_seqs, all_seqs, (1,), (s_core,), (head_places(wa_core),))
-        z_core, wa_quarters, wb_quarters, s_chip = lax.optimization_barrier((z_core, wa_quarters, wb_quarters, s_chip))
-        wa_far, wb_far, s_far = [to_core(w) for w in wa_quarters], [to_core(w) for w in wb_quarters], to_core(s_chip)
+        z_core, wa_quarters, wb_quarters, su_chip = lax.optimization_barrier((z_core, wa_quarters, wb_quarters, su_chip))
+        wa_far, wb_far, su_far = [to_core(w) for w in wa_quarters], [to_core(w) for w in wb_quarters], to_core(su_chip)
         got_core = to_core(new_core)
 
         w_chip = heads_gathered(wa_quarters)
-        z_chip, new_chip = run(meta, common, one, (STATE_SINGLE,), (2,), (s_chip,), (w_chip,))
-        z_chip, wa_far, wb_far, wb_core, s_far = lax.optimization_barrier((z_chip, wa_far, wb_far, wb_core, s_far))
+        z_chip, new_chip = run(meta, common, one, (STATE_SINGLE,), (2,), (su_chip,), (w_chip,))
+        z_chip, wa_far, wb_far, wb_core, su_far, st_chip = lax.optimization_barrier((z_chip, wa_far, wb_far, wb_core, su_far, st_chip))
+        st_far = to_core(st_chip)
         w_far = heads_gathered(wa_far)
         mlp = (mlp_places(mlp_w), mlp_places(wb_core), heads_gathered(wb_quarters), heads_gathered(wb_far))
-        whole, x_single, new_far = run(meta, common, one, (STATE_SINGLE,), (3,), (s_far,), (w_far, *mlp), ((z_own_single, 0), (z_core, 0), (z_chip, 0)))
+        whole, x_single, new_far = run(meta, common, one, (STATE_SINGLE,), (3,), (su_far,), (w_far, *mlp), ((z_own_single, 0), (z_core, 0), (z_chip, 0)))
         x_single_chip = to_chip(x_single)
         x_single_core = to_core(x_single)
         got_chip = to_chip(new_chip)
         got_far = to_far(new_far)
-        far = ((2, 3), (s_chip, s_far), (w_chip, w_far, *mlp))
-        whole, x_a, _, _ = run(meta, common, (SEQ + 1,), (STATE_TWICE,), *far, ((z_own, 0), (z_core, 1)), whole)
+        whole, x_a, x_b, _, _ = run(meta, common, pair_seqs, (STATE_TWICE, STATE_TWICE + 1), (2, 3), (st_chip, st_far), (w_chip, w_far, *mlp),
+                                    ((z_own, 0), (z_core, 1)), whole)
         x_a_core = to_core(x_a)
-        whole, x_b, _, _ = run(meta, common, (SEQ + 2,), (STATE_TWICE + 1,), *far, ((z_own, 1), (z_core, 2)), whole)
+        x_single_far = to_core(x_single_chip)
+
         x_b_core = to_core(x_b)
-        x_single_far = to_core(x_single_chip)
 
         single_o, twice_o = 2 * chip + other, 4 + 2 * other
         far_c, far_o = 2 * (1 - chip) + core, 2 * (1 - chip) + other
-        ids = jnp.stack([single_o, twice_o, far_c, single, single_o, twice_o, twice_o + 1, far_c, far_o, far_o, twice_o + 1]).astype(jnp.int32)
+        ids = jnp.stack([single_o, far_c, single, single_o, twice_o, twice_o + 1, far_c, far_o, twice_o, far_o, twice_o + 1]).astype(jnp.int32)
         cuts = chunk_len // TILE
-        near = [(x_single_core, 0, 0, cuts), (x_a_core, 0, 0, cuts), (x_single_chip, 0, 0, cuts)]
+        near = [(x_single_core, 0, 0, cuts), (x_single_chip, 0, 0, cuts)]
         near += [(arr, at, 1, 1) for arr, at in ((new_own_single, 0), (got_core, 0), (got_core, 1), (got_core, 2), (got_chip, 0), (got_far, 0))]
-        whole, new_states = place(ids[:9], near, (whole, new_states))
-        whole, = place(ids[9:], [(x_single_far, 0, 0, cuts), (x_b_core, 0, 0, cuts)], (whole,))
+        whole, new_states = place(ids[:8], near, (whole, new_states))
+        whole, = place(ids[8:9], [(x_a_core, 0, 0, cuts)], (whole,))
+        whole, = place(ids[9:10], [(x_single_far, 0, 0, cuts)], (whole,))
+        whole, = place(ids[10:], [(x_b_core, 0, 0, cuts)], (whole,))
         return whole, new_states[:, None]
 
     in_specs = (P("dp", None, None), P("dp"), P("dp", "tp", None, None), P(), P(), P(None, "tp"), P(None, "tp"), P(None, "tp"), P(None, "tp"), P("tp", None), P(), P(), P(None, "tp"), P("tp", None))

time: 418 us -> 435 us (1.041)
  waiting for transfers between devices: 83.8 us -> 111 us
  Pallas kernels: 307 us -> 291 us
    ppermute x6, waiting for transfers between devices: 11.4 us -> 60.1 us  [gather(): return [part] + [swap('dp', flip)(part) for flip in range(1, n_dp)]]
    ppermute x1, waiting for transfers between devices: 32.7 us -> 13 us  [local_layer(): wa_part = to_chip(wa_part)]
    pallas_call x7 -> x6, Pallas kernels: 284 us -> 266 us  [run(): pl.pallas_call(functools.partial(kernel_body, n, tuple(heads), len(zs), t...]
    ppermute x3, waiting for transfers between devices: 7.97 us -> 0.01 us  [local_layer(): wb_core = [to_core(w) for w in mlp_w]]
    pallas_call x2 -> x4, Pallas kernels: 18.2 us -> 18.9 us  [place(): pl.pallas_call(functools.partial(place_kernel, tuple((block[1:] for block...]
  transfers between devices with their start and end apart: 34 -> 36, of which waited for: 12 -> 12; matrix products, arithmetic and copies ran while one was open for 1% -> 1% of each run, Pallas kernels for 59% -> 66%
where the time goes in v4:
time: 435 us
  Pallas kernels  291 us (67%)
  waiting for transfers between devices  111 us (26%)
  starting transfers between devices  21.8 us (5%)
  other arithmetic  5.38 us (1%)
  local copies, waits for them, and re-layouts  4.94 us (1%)
    pallas_call x6, Pallas kernels, run(): pl.pallas_call(functools.partial(kernel_body, n, tuple(heads), len(zs), t...  266 us
    ppermute x6, waiting for transfers between devices, gather(): return [part] + [swap('dp', flip)(part) for flip in range(1, n_dp)]  60.1 us
    pallas_call x4, Pallas kernels, place(): pl.pallas_call(functools.partial(place_kernel, tuple((block[1:] for block...  18.9 us
    ppermute x1, waiting for transfers between devices, local_layer(): got_far = to_far(new_far)  13.4 us
    ppermute x1, waiting for transfers between devices, local_layer(): got_chip = to_chip(new_chip)  13.4 us
    ppermute x1, waiting for transfers between devices, local_layer(): wa_part = to_chip(wa_part)  13 us
  transfers between devices with their start and end apart: 36, of which 12 were waited for; matrix products, arithmetic and copies ran while one was open for 1% of the time, Pallas kernels for 66%

profile of v4, /device:TPU:0, one launch (start us, length us, event | category | flops | bytes accessed | tf_op | source)
XLA Modules:
  0.0 434.8 jit_solution(7070464250405580999)
XLA Ops:
  2.6 5.4 %parts.1 = (bf16[256,1536]{1,0:T(8,128)(2,1)}, bf16[256,1536]{1,0:T(8,128)(2,1)}, f32[2,256,512]{2,1,0:T(8,128)}, f32[4,256,512]{2,1,0:T(8,128)}) custom-call(s32[10]{0:T(128)} %stack.68.meta_ref, bf16[1024,256]{1,0:T(8,128)(2,1)} %refs_3_.1, bf16[1024,256]{1,0:T(8,128)(2,1)} %refs_4_.1, bf16[1024,512]{1,0:T(8,128)(2,1)} %refs_5_.1, ...), custom_call_target="tpu_custom_call" | custom-call | tf_op jit(solution)/shard_map/parts/pallas_call | solution.py:240
  8.0 3.0 collective-permute-start.6
  14.7 1.7 broadcast_select_fusion.step_ref
  16.6 13.0 %collective-permute-done.6.refs_3_.refs_12_ = bf16[256,1536]{1,0:T(8,128)(2,1)S(1)} collective-permute-done((bf16[256,1536]{1,0:T(8,128)(2,1)}, bf16[256,1536]{1,0:T(8,128)(2,1)S(1)}, u32[]{:S(2)}, u32[]{:S(2)}) %collective-permute-start.6) | collective-permute-done | bytes 786464 | tf_op jit(solution)/shard_map/ppermute | solution.py:329
  29.5 2.0 collective-permute-start.13
  31.6 27.8 %heads.4 = (bf16[2,2048,512]{2,1,0:T(8,128)(2,1)}, f32[8,256,512]{2,1,0:T(8,128)}) custom-call(s32[10]{0:T(128)} %stack.68.meta_ref, f32[1,1024]{1,0:T(1,128)} %bitcast.33, f32[1,1024]{1,0:T(1,128)} %bitcast.39, f32[1,1024]{1,0:T(1,128)} %bitcast.45, f32[1,1024]{1,0:T(1,128)} %bitcast.51, f32[2,256,128]{2,1,0:T(8,128)} %broadcast_select_fusion.step_ref, ...), custom_call_target="tpu_custom_call" | custom-call | flops 16642998272 | bytes 16777216 | tf_op jit(solution)/shard_map/heads/pallas_call | solution.py:195
  59.4 17.8 %heads.6 = (bf16[1,2048,512]{2,1,0:T(8,128)(2,1)}, f32[1,256,512]{2,1,0:T(8,128)}) custom-call(s32[10]{0:T(128)} %stack.68.meta_ref, f32[1,1024]{1,0:T(1,128)} %bitcast.34, f32[1,1024]{1,0:T(1,128)} %bitcast.40, f32[1,1024]{1,0:T(1,128)} %bitcast.46, f32[1,1024]{1,0:T(1,128)} %bitcast.52, f32[2,256,128]{2,1,0:T(8,128)} %broadcast_select_fusion.step_ref, ...), custom_call_target="tpu_custom_call" | custom-call | flops 8321499136 | bytes 8388608 | tf_op jit(solution)/shard_map/heads/pallas_call | solution.py:195
  77.2 2.6 collective-permute-start.9
  80.7 2.5 collective-permute-start.12
  83.7 15.1 %collective-permute-done.9.refs_6_.refs_15_ = bf16[256,1536]{1,0:T(8,128)(2,1)S(1)} collective-permute-done((bf16[256,1536]{1,0:T(8,128)(2,1)}, bf16[256,1536]{1,0:T(8,128)(2,1)S(1)}, u32[]{:S(2)}, u32[]{:S(2)}) %collective-permute-start.9) | collective-permute-done | bytes 786464 | tf_op jit(solution)/shard_map/ppermute | solution.py:321
  98.8 16.9 %collective-permute-done.8.refs_5_.refs_14_ = bf16[256,1536]{1,0:T(8,128)(2,1)S(1)} collective-permute-done((bf16[256,1536]{1,0:T(8,128)(2,1)}, bf16[256,1536]{1,0:T(8,128)(2,1)S(1)}, u32[]{:S(2)}, u32[]{:S(2)}) %collective-permute-start.8) | collective-permute-done | bytes 786464 | tf_op jit(solution)/shard_map/ppermute | solution.py:321
  116.2 13.4 %collective-permute-done.12.refs_19_.refs_29_ = bf16[256,1536]{1,0:T(8,128)(2,1)S(1)} collective-permute-done((bf16[256,1536]{1,0:T(8,128)(2,1)}, bf16[256,1536]{1,0:T(8,128)(2,1)S(1)}, u32[]{:S(2)}, u32[]{:S(2)}) %collective-permute-start.12) | collective-permute-done | bytes 786464 | tf_op jit(solution)/shard_map/ppermute | solution.py:321
  131.7 14.7 %collective-permute-done.11.refs_18_.refs_28_ = bf16[256,1536]{1,0:T(8,128)(2,1)} collective-permute-done((bf16[256,1536]{1,0:T(8,128)(2,1)}, bf16[256,1536]{1,0:T(8,128)(2,1)}, u32[]{:S(2)}, u32[]{:S(2)}) %collective-permute-start.11) | collective-permute-done | bytes 786464 | tf_op jit(solution)/shard_map/ppermute | solution.py:321
  148.0 38.6 %heads.5 = (bf16[3,2048,512]{2,1,0:T(8,128)(2,1)}, f32[3,256,512]{2,1,0:T(8,128)}) custom-call(s32[10]{0:T(128)} %stack.68.meta_ref, f32[1,1024]{1,0:T(1,128)} %bitcast.35, f32[1,1024]{1,0:T(1,128)} %bitcast.41, f32[1,1024]{1,0:T(1,128)} %bitcast.47, f32[1,1024]{1,0:T(1,128)} %bitcast.53, f32[2,256,128]{2,1,0:T(8,128)} %broadcast_select_fusion.step_ref, ...), custom_call_target="tpu_custom_call" | custom-call | flops 24964497408 | bytes 25165824 | tf_op jit(solution)/shard_map/heads/pallas_call | solution.py:195
  193.4 17.7 %heads.7 = (bf16[1,2048,512]{2,1,0:T(8,128)(2,1)}, f32[1,256,512]{2,1,0:T(8,128)}) custom-call(s32[10]{0:T(128)} %stack.68.meta_ref, f32[1,1024]{1,0:T(1,128)} %bitcast.36, f32[1,1024]{1,0:T(1,128)} %bitcast.42, f32[1,1024]{1,0:T(1,128)} %bitcast.48, f32[1,1024]{1,0:T(1,128)} %bitcast.54, f32[2,256,128]{2,1,0:T(8,128)} %broadcast_select_fusion.step_ref, ...), custom_call_target="tpu_custom_call" | custom-call | flops 8321499136 | bytes 8388608 | tf_op jit(solution)/shard_map/heads/pallas_call | solution.py:195
  212.5 54.1 %tail.2 = (bf16[8,2048,1024]{2,1,0:T(8,128)(2,1)}, bf16[1,2048,1024]{2,1,0:T(8,128)(2,1)}, f32[1,256,512]{2,1,0:T(8,128)}) custom-call(s32[10]{0:T(128)} %stack.68.meta_ref, f32[1,1024]{1,0:T(1,128)} %bitcast.37, f32[1,1024]{1,0:T(1,128)} %bitcast.43, f32[1,1024]{1,0:T(1,128)} %bitcast.49, f32[1,1024]{1,0:T(1,128)} %bitcast.55, ...), custom_call_target="tpu_custom_call" | custom-call | flops 34091302912 | bytes 16777216 | tf_op jit(solution)/shard_map/tail/pallas_call | solution.py:195
  269.6 110.2 %tail.3 = (bf16[8,2048,1024]{2,1,0:T(8,128)(2,1)}, bf16[1,2048,1024]{2,1,0:T(8,128)(2,1)}, bf16[1,2048,1024]{2,1,0:T(8,128)(2,1)}, f32[2,256,512]{2,1,0:T(8,128)}, f32[2,256,512]{2,1,0:T(8,128)}) custom-call(s32[10]{0:T(128)} %stack.68.meta_ref, f32[1,1024]{1,0:T(1,128)} %bitcast.38, f32[1,1024]{1,0:T(1,128)} %bitcast.44, ...), custom_call_target="tpu_custom_call", output_to_operand_aliasing={{0}: (40, {})} | custom-call | flops 84825604096 | bytes 33554432 | tf_op jit(solution)/shard_map/tail/pallas_call | solution.py:195
  381.3 13.4 %collective-permute-done.34.refs_6_ = f32[1,256,512]{2,1,0:T(8,128)S(1)} collective-permute-done((f32[1,256,512]{2,1,0:T(8,128)S(1)}, f32[1,256,512]{2,1,0:T(8,128)S(1)}, u32[]{:S(2)}, u32[]{:S(2)}) %collective-permute-start.34) | collective-permute-done | bytes 524320 | tf_op jit(solution)/shard_map/ppermute | solution.py:359
  394.8 6.8 %collective-permute-done.33.refs_3_.refs_4_.refs_5_ = f32[3,256,512]{2,1,0:T(8,128)S(1)} collective-permute-done((f32[3,256,512]{2,1,0:T(8,128)}, f32[3,256,512]{2,1,0:T(8,128)S(1)}, u32[]{:S(2)}, u32[]{:S(2)}) %collective-permute-start.33) | collective-permute-done | bytes 1572896 | tf_op jit(solution)/shard_map/ppermute | solution.py:348
  402.2 13.4 %collective-permute-done.35.refs_7_ = f32[1,256,512]{2,1,0:T(8,128)S(1)} collective-permute-done((f32[1,256,512]{2,1,0:T(8,128)}, f32[1,256,512]{2,1,0:T(8,128)S(1)}, u32[]{:S(2)}, u32[]{:S(2)}) %collective-permute-start.35) | collective-permute-done | bytes 524320 | tf_op jit(solution)/shard_map/ppermute | solution.py:360
  415.6 8.2 %place.4 = (bf16[8,2048,1024]{2,1,0:T(8,128)(2,1)}, f32[8,256,512]{2,1,0:T(8,128)}) custom-call(s32[8]{0:T(128)S(1)} %stack.73.ids_ref, bf16[1,2048,1024]{2,1,0:T(8,128)(2,1)} %collective-permute-done.32.refs_0_, bf16[1,2048,1024]{2,1,0:T(8,128)(2,1)} %collective-permute-done.29.refs_1_, ...), custom_call_target="tpu_custom_call", output_to_operand_aliasing={{0}: (9, {}), {1}: (10, {})} | custom-call | tf_op jit(solution)/shard_map/place/pallas_call | solution.py:271
  423.8 3.6 place.5.refs_1_
  427.4 3.6 place.6.refs_1_
  431.0 3.6 place.7
  (121 shorter events, 24.5 us)
Async XLA Ops:
  0.6 80.1 %collective-permute-start.4 = (f32[8,256,512]{2,1,0:T(8,128)}, f32[8,256,512]{2,1,0:T(8,128)}, u32[]{:S(2)}, u32[]{:S(2)}) collective-permute-start(f32[8,256,512]{2,1,0:T(8,128)} %bitcast.27), channel_id=1, source_target_pairs={{0,1},{1,0},{2,3},{3,2},{4,5},{5,4},{6,7},{7,6},{8,9},{9,8},{10,11... | collective-permute-start | bytes 12582920 | tf_op jit(solution)/shard_map/ppermute | solution.py:327
  1.9 77.9 %collective-permute-start.2 = (bf16[1024,512]{1,0:T(8,128)(2,1)}, bf16[1024,512]{1,0:T(8,128)(2,1)S(1)}, u32[]{:S(2)}, u32[]{:S(2)}) collective-permute-start(bf16[1024,512]{1,0:T(8,128)(2,1)} %refs_5_.1), channel_id=1, source_target_pairs={{0,1},{1,0},{2,3},{3,2},{4,5},{5,4},{6,7},{7,6},{8,9},{9,8},{10,11... | collective-permute-start | bytes 3145736 | tf_op jit(solution)/shard_map/ppermute | solution.py:326
  8.0 21.6 %collective-permute-start.6 = (bf16[256,1536]{1,0:T(8,128)(2,1)}, bf16[256,1536]{1,0:T(8,128)(2,1)S(1)}, u32[]{:S(2)}, u32[]{:S(2)}) collective-permute-start(bf16[256,1536]{1,0:T(8,128)(2,1)} %get-tuple-element.64), channel_id=1, source_target_pairs={{0,2},{1,3},{2,0},{3,1},{4,6},{5,7},{6,4},{7,5},{8,10},{9,11},{10,... | collective-permute-start | bytes 2359304 | tf_op jit(solution)/shard_map/ppermute | solution.py:329
  16.5 63.8 %collective-permute-start.3 = (bf16[1024,512]{1,0:T(8,128)(2,1)S(1)}, bf16[1024,512]{1,0:T(8,128)(2,1)S(1)}, u32[]{:S(2)}, u32[]{:S(2)}) collective-permute-start(bf16[1024,512]{1,0:T(8,128)(2,1)S(1)} %copy-done.1), channel_id=1, source_target_pairs={{0,1},{1,0},{2,3},{3,2},{4,5},{5,4},{6,7},{7,6},{8,9},{9,8},{10,11... | collective-permute-start | bytes 3145736 | tf_op jit(solution)/shard_map/ppermute | solution.py:326
  16.5 60.7 %collective-permute-start.5 = (bf16[256,1536]{1,0:T(8,128)(2,1)}, bf16[256,1536]{1,0:T(8,128)(2,1)}, u32[]{:S(2)}, u32[]{:S(2)}) collective-permute-start(bf16[256,1536]{1,0:T(8,128)(2,1)} %get-tuple-element.56), channel_id=1, source_target_pairs={{0,2},{1,3},{2,0},{3,1},{4,6},{5,7},{6,4},{7,5},{8,10},{9,11},{10,... | collective-permute-start | bytes 2359304 | tf_op jit(solution)/shard_map/ppermute | solution.py:330
  29.5 53.7 %collective-permute-start.13 = (f32[2,256,512]{2,1,0:T(8,128)}, f32[2,256,512]{2,1,0:T(8,128)S(1)}, u32[]{:S(2)}, u32[]{:S(2)}) collective-permute-start(f32[2,256,512]{2,1,0:T(8,128)} %get-tuple-element.67), channel_id=1, source_target_pairs={{0,2},{1,3},{2,0},{3,1},{4,6},{5,7},{6,4},{7,5},{8,10},{9,11},{10,... | collective-permute-start | bytes 3145736 | tf_op jit(solution)/shard_map/ppermute | solution.py:331
  77.2 21.6 %collective-permute-start.9 = (bf16[256,1536]{1,0:T(8,128)(2,1)}, bf16[256,1536]{1,0:T(8,128)(2,1)S(1)}, u32[]{:S(2)}, u32[]{:S(2)}) collective-permute-start(bf16[256,1536]{1,0:T(8,128)(2,1)} %copy-done.6), channel_id=1, source_target_pairs={{0,12},{4,8},{8,4},{12,0},{1,13},{5,9},{9,5},{13,1},{2,14},{6,10},... | collective-permute-start | bytes 2359304 | tf_op jit(solution)/shard_map/ppermute | solution.py:321
  79.8 35.9 %collective-permute-start.8 = (bf16[256,1536]{1,0:T(8,128)(2,1)}, bf16[256,1536]{1,0:T(8,128)(2,1)S(1)}, u32[]{:S(2)}, u32[]{:S(2)}) collective-permute-start(bf16[256,1536]{1,0:T(8,128)(2,1)} %copy-done.6), channel_id=1, source_target_pairs={{0,8},{4,12},{8,0},{12,4},{1,9},{5,13},{9,1},{13,5},{2,10},{6,14},... | collective-permute-start | bytes 2359304 | tf_op jit(solution)/shard_map/ppermute | solution.py:321
  80.2 35.5 %collective-permute-start.7 = (bf16[256,1536]{1,0:T(8,128)(2,1)}, bf16[256,1536]{1,0:T(8,128)(2,1)S(1)}, u32[]{:S(2)}, u32[]{:S(2)}) collective-permute-start(bf16[256,1536]{1,0:T(8,128)(2,1)} %copy-done.6), channel_id=1, source_target_pairs={{0,4},{4,0},{8,12},{12,8},{1,5},{5,1},{9,13},{13,9},{2,6},{6,2},{1... | collective-permute-start | bytes 2359304 | tf_op jit(solution)/shard_map/ppermute | solution.py:321
  80.7 48.9 %collective-permute-start.12 = (bf16[256,1536]{1,0:T(8,128)(2,1)}, bf16[256,1536]{1,0:T(8,128)(2,1)S(1)}, u32[]{:S(2)}, u32[]{:S(2)}) collective-permute-start(bf16[256,1536]{1,0:T(8,128)(2,1)} %collective-permute-done.5.refs_16_.refs_26_), channel_id=1, source_target_pairs={{0,12},{4,8},{8,4},{12,0},{1,13},{5,9},{9,5},{13,1},{2,14},{6,10},... | collective-permute-start | bytes 2359304 | tf_op jit(solution)/shard_map/ppermute | solution.py:321
  83.3 63.2 %collective-permute-start.11 = (bf16[256,1536]{1,0:T(8,128)(2,1)}, bf16[256,1536]{1,0:T(8,128)(2,1)}, u32[]{:S(2)}, u32[]{:S(2)}) collective-permute-start(bf16[256,1536]{1,0:T(8,128)(2,1)} %collective-permute-done.5.refs_16_.refs_26_), channel_id=1, source_target_pairs={{0,8},{4,12},{8,0},{12,4},{1,9},{5,13},{9,1},{13,5},{2,10},{6,14},... | collective-permute-start | bytes 2359304 | tf_op jit(solution)/shard_map/ppermute | solution.py:321
  98.8 87.9 %collective-permute-start.22 = (bf16[512,1024]{1,0:T(8,128)(2,1)S(1)}, bf16[512,1024]{1,0:T(8,128)(2,1)}, u32[]{:S(2)}, u32[]{:S(2)}) collective-permute-start(bf16[512,1024]{1,0:T(8,128)(2,1)S(1)} %copy-done.5), channel_id=1, source_target_pairs={{0,1},{1,0},{2,3},{3,2},{4,5},{5,4},{6,7},{7,6},{8,9},{9,8},{10,11... | collective-permute-start | bytes 3145736 | tf_op jit(solution)/shard_map/ppermute | solution.py:333
  115.7 71.5 %collective-permute-start.24 = (bf16[1024,512]{1,0:T(8,128)(2,1)}, bf16[1024,512]{1,0:T(8,128)(2,1)}, u32[]{:S(2)}, u32[]{:S(2)}) collective-permute-start(bf16[1024,512]{1,0:T(8,128)(2,1)} %refs_22_.1), channel_id=1, source_target_pairs={{0,1},{1,0},{2,3},{3,2},{4,5},{5,4},{6,7},{7,6},{8,9},{9,8},{10,11... | collective-permute-start | bytes 3145736 | tf_op jit(solution)/shard_map/ppermute | solution.py:333
  115.7 71.5 %collective-permute-start.23 = (bf16[512,1024]{1,0:T(8,128)(2,1)}, bf16[512,1024]{1,0:T(8,128)(2,1)}, u32[]{:S(2)}, u32[]{:S(2)}) collective-permute-start(bf16[512,1024]{1,0:T(8,128)(2,1)} %refs_21_.1), channel_id=1, source_target_pairs={{0,1},{1,0},{2,3},{3,2},{4,5},{5,4},{6,7},{7,6},{8,9},{9,8},{10,11... | collective-permute-start | bytes 3145736 | tf_op jit(solution)/shard_map/ppermute | solution.py:333
  130.5 57.2 %collective-permute-start.26 = (f32[4,256,512]{2,1,0:T(8,128)}, f32[4,256,512]{2,1,0:T(8,128)}, u32[]{:S(2)}, u32[]{:S(2)}) collective-permute-start(f32[4,256,512]{2,1,0:T(8,128)} %get-tuple-element.78), channel_id=1, source_target_pairs={{0,2},{1,3},{2,0},{3,1},{4,6},{5,7},{6,4},{7,5},{8,10},{9,11},{10,... | collective-permute-start | bytes 6291464 | tf_op jit(solution)/shard_map/ppermute | solution.py:332
  146.5 40.1 %collective-permute-start.10 = (bf16[256,1536]{1,0:T(8,128)(2,1)}, bf16[256,1536]{1,0:T(8,128)(2,1)}, u32[]{:S(2)}, u32[]{:S(2)}) collective-permute-start(bf16[256,1536]{1,0:T(8,128)(2,1)} %collective-permute-done.5.refs_16_.refs_26_), channel_id=1, source_target_pairs={{0,4},{4,0},{8,12},{12,8},{1,5},{5,1},{9,13},{13,9},{2,6},{6,2},{1... | collective-permute-start | bytes 2359304 | tf_op jit(solution)/shard_map/ppermute | solution.py:321
  187.7 23.4 %collective-permute-start.25 = (f32[2,256,512]{2,1,0:T(8,128)S(1)}, f32[2,256,512]{2,1,0:T(8,128)S(1)}, u32[]{:S(2)}, u32[]{:S(2)}) collective-permute-start(f32[2,256,512]{2,1,0:T(8,128)S(1)} %collective-permute-done.13.refs_2_), channel_id=1, source_target_pairs={{0,1},{1,0},{2,3},{3,2},{4,5},{5,4},{6,7},{7,6},{8,9},{9,8},{10,11... | collective-permute-start | bytes 3145736 | tf_op jit(solution)/shard_map/ppermute | solution.py:347
  188.9 22.1 %collective-permute-start.18 = (bf16[256,1536]{1,0:T(8,128)(2,1)}, bf16[256,1536]{1,0:T(8,128)(2,1)S(1)}, u32[]{:S(2)}, u32[]{:S(2)}) collective-permute-start(bf16[256,1536]{1,0:T(8,128)(2,1)} %collective-permute-done.5.refs_16_.refs_26_), channel_id=1, source_target_pairs={{0,1},{1,0},{2,3},{3,2},{4,5},{5,4},{6,7},{7,6},{8,9},{9,8},{10,11... | collective-permute-start | bytes 2359304 | tf_op jit(solution)/shard_map/ppermute | solution.py:347
  211.1 57.1 %collective-permute-start.27 = (f32[4,256,512]{2,1,0:T(8,128)}, f32[4,256,512]{2,1,0:T(8,128)S(1)}, u32[]{:S(2)}, u32[]{:S(2)}) collective-permute-start(f32[4,256,512]{2,1,0:T(8,128)} %collective-permute-done.26.refs_4_.refs_5_), channel_id=1, source_target_pairs={{0,1},{1,0},{2,3},{3,2},{4,5},{5,4},{6,7},{7,6},{8,9},{9,8},{10,11... | collective-permute-start | bytes 6291464 | tf_op jit(solution)/shard_map/ppermute | solution.py:353
  266.7 149.0 %collective-permute-start.32 = (bf16[1,2048,1024]{2,1,0:T(8,128)(2,1)}, bf16[1,2048,1024]{2,1,0:T(8,128)(2,1)}, u32[]{:S(2)}, u32[]{:S(2)}) collective-permute-start(bf16[1,2048,1024]{2,1,0:T(8,128)(2,1)} %get-tuple-element.98), channel_id=1, source_target_pairs={{0,1},{1,0},{2,3},{3,2},{4,5},{5,4},{6,7},{7,6},{8,9},{9,8},{10,11... | collective-permute-start | bytes 12582920 | tf_op jit(solution)/shard_map/ppermute | solution.py:358
  267.1 112.8 %collective-permute-start.29 = (bf16[1,2048,1024]{2,1,0:T(8,128)(2,1)}, bf16[1,2048,1024]{2,1,0:T(8,128)(2,1)}, u32[]{:S(2)}, u32[]{:S(2)}) collective-permute-start(bf16[1,2048,1024]{2,1,0:T(8,128)(2,1)} %get-tuple-element.98), channel_id=1, source_target_pairs={{0,2},{1,3},{2,0},{3,1},{4,6},{5,7},{6,4},{7,5},{8,10},{9,11},{10,... | collective-permute-start | bytes 12582920 | tf_op jit(solution)/shard_map/ppermute | solution.py:357
  379.9 44.0 %collective-permute-start.31 = (bf16[1,2048,1024]{2,1,0:T(8,128)(2,1)}, bf16[1,2048,1024]{2,1,0:T(8,128)(2,1)}, u32[]{:S(2)}, u32[]{:S(2)}) collective-permute-start(bf16[1,2048,1024]{2,1,0:T(8,128)(2,1)} %get-tuple-element.99), channel_id=1, source_target_pairs={{0,1},{1,0},{2,3},{3,2},{4,5},{5,4},{6,7},{7,6},{8,9},{9,8},{10,11... | collective-permute-start | bytes 12582920 | tf_op jit(solution)/shard_map/ppermute | solution.py:363
  379.9 47.5 %collective-permute-start.30 = (bf16[1,2048,1024]{2,1,0:T(8,128)(2,1)}, bf16[1,2048,1024]{2,1,0:T(8,128)(2,1)}, u32[]{:S(2)}, u32[]{:S(2)}) collective-permute-start(bf16[1,2048,1024]{2,1,0:T(8,128)(2,1)} %collective-permute-done.29.refs_1_), channel_id=1, source_target_pairs={{0,1},{1,0},{2,3},{3,2},{4,5},{5,4},{6,7},{7,6},{8,9},{9,8},{10,11... | collective-permute-start | bytes 12582920 | tf_op jit(solution)/shard_map/ppermute | solution.py:364
  380.4 50.6 %collective-permute-start.28 = (bf16[1,2048,1024]{2,1,0:T(8,128)(2,1)}, bf16[1,2048,1024]{2,1,0:T(8,128)(2,1)}, u32[]{:S(2)}, u32[]{:S(2)}) collective-permute-start(bf16[1,2048,1024]{2,1,0:T(8,128)(2,1)} %get-tuple-element.97), channel_id=1, source_target_pairs={{0,1},{1,0},{2,3},{3,2},{4,5},{5,4},{6,7},{7,6},{8,9},{9,8},{10,11... | collective-permute-start | bytes 12582920 | tf_op jit(solution)/shard_map/ppermute | solution.py:366
  (36 other events, 938.1 us)

commit v5 on v4

--- a/solution.py
+++ b/solution.py
@@ -59,32 +59,33 @@
         rows_ref[i, 2] = jnp.exp(jnp.full((TILE, 128), TILE, F32) * log_gamma)
 
 
-def head_blocks(hs, w_ref, state_ref, inner, rows_ref, tables):
-    _, key_dim, val_dim = state_ref.shape
+def head_blocks(h, w_ref, state_ref, inner, rows_ref, tables):
+    n_seqs, key_dim, val_dim = state_ref.shape
+    q_raw = dot(h, w_ref[:, :key_dim])
+    k_raw = dot(h, w_ref[:, key_dim:2 * key_dim])
+    values = dot(h, w_ref[:, 2 * key_dim:2 * key_dim + val_dim]).astype(BF16)
+    gates = dot(h, w_ref[:, 2 * key_dim + val_dim:])
     out = []
-    for b, h in enumerate(hs):
-        q_raw = dot(h, w_ref[:, :key_dim])
-        k_raw = dot(h, w_ref[:, key_dim:2 * key_dim])
-        queries = rotate(q_raw, *tables[b]).astype(BF16)
-        keys = (rotate(k_raw, *tables[b]) * key_dim ** -0.5).astype(BF16)
-        values = dot(h, w_ref[:, 2 * key_dim:2 * key_dim + val_dim]).astype(BF16)
+    for i, table in enumerate(tables):
+        at, b = slice(i * TILE, (i + 1) * TILE), i * n_seqs // len(tables)
+        queries = rotate(q_raw[at], *table).astype(BF16)
+        keys = (rotate(k_raw[at], *table) * key_dim ** -0.5).astype(BF16)
         scores = lax.dot_general(queries, keys, (((1,), (1,)), ((), ())), preferred_element_type=F32) * inner
         state = state_ref[b]
         carried = dot(queries, state.astype(BF16)) * widen(rows_ref[0], val_dim)
-        retained = dot(scores.astype(BF16), values) + carried
-        gates = dot(h, w_ref[:, 2 * key_dim + val_dim:])
+        retained = dot(scores.astype(BF16), values[at]) + carried
         faded = (keys.astype(F32) * widen(rows_ref[1], key_dim)).astype(BF16)
-        update = lax.dot_general(faded, values, (((0,), (0,)), ((), ())), preferred_element_type=F32)
+        update = lax.dot_general(faded, values[at], (((0,), (0,)), ((), ())), preferred_element_type=F32)
         state_ref[b] = state * widen(rows_ref[2, 0:1], val_dim) + update
         row_mean = jnp.mean(retained, axis=-1, keepdims=True)
         centered = retained - row_mean
         variance = jnp.mean(centered * centered, axis=-1, keepdims=True)
         normed = centered * lax.rsqrt(variance + GROUP_EPS)
-        out.append((gates * lax.logistic(gates) * normed).astype(BF16))
+        out.append((gates[at] * lax.logistic(gates[at]) * normed).astype(BF16))
     return out
 
 
-def kernel_body(n_seqs, heads, n_z, pieces, with_whole, meta_ref, gain1, bias1, gain2, bias2, step_ref, *refs):
+def kernel_body(n_seqs, n_sub, heads, n_z, pieces, with_whole, meta_ref, gain1, bias1, gain2, bias2, step_ref, *refs):
     it = iter(refs)
 
     def take(n):
@@ -115,17 +116,20 @@
         for copy in copies:
             copy.wait()
 
-    at = pl.multiple_of(pl.program_id(0) * 8, 8)
     cos_b, sin_b = step_ref[0], step_ref[1]
     normed, tables = [], []
     for x_ref, base_ref in zip(x_refs, base_refs):
         normed.append(layer_norm(x_ref[0].astype(F32), gain1[...], bias1[...]).astype(BF16))
-        cos_a, sin_a = base_ref[0, pl.ds(at, 1), :], base_ref[0, pl.ds(at + 1, 1), :]
-        tables.append((cos_a * cos_b - sin_a * sin_b, sin_a * cos_b + cos_a * sin_b))
-    mixed = [head_blocks(normed, weights[i], state_refs[i], inner_ref[i], rows_ref.at[i], tables) for i in range(len(heads))]
+        for j in range(n_sub):
+            at = pl.multiple_of((pl.program_id(0) * n_sub + j) * 8, 8)
+            cos_a, sin_a = base_ref[0, pl.ds(at, 1), :], base_ref[0, pl.ds(at + 1, 1), :]
+            tables.append((cos_a * cos_b - sin_a * sin_b, sin_a * cos_b + cos_a * sin_b))
+    h = below(normed)
+    mixed = [head_blocks(h, weights[i], state_refs[i], inner_ref[i], rows_ref.at[i], tables) for i in range(len(heads))]
+    rows = n_sub * TILE
     if not n_z:
-        for b in range(n_seqs):
-            outs[0][b] = mixed[0][b]
+        for i, block in enumerate(mixed[0]):
+            outs[0][i // n_sub, i % n_sub * TILE:(i % n_sub + 1) * TILE] = block
         return
     mixed = [[ref[0] for ref in refs_of] for refs_of in z_refs] + mixed
     blocks = weights[len(heads):]
@@ -140,16 +144,17 @@
         f = f + dot(act, wb[val_dim:, :d_model])
     x_out = (x_mid.astype(F32) + f.astype(BF16).astype(F32)).astype(BF16)
     for b in range(n_seqs):
-        outs[0][b] = x_out[b * TILE:(b + 1) * TILE]
-        outs[1 + b][0] = x_out[b * TILE:(b + 1) * TILE]
+        outs[0][b] = x_out[b * rows:(b + 1) * rows]
+        outs[1 + b][0] = x_out[b * rows:(b + 1) * rows]
 
 
 def below(blocks):
     return blocks[0] if len(blocks) == 1 else jnp.concatenate(blocks, axis=0)
 
 
-def run(meta, common, seqs, state_rows, heads, states, weights, zs=(), whole=None, pair=False):
+def run(meta, common, seqs, state_rows, heads, states, weights, zs=(), whole=None, pair=False, n_sub=1):
     x, norms, base, step = common
+    tile = n_sub * TILE
     n, chunk_len, d_model = len(seqs), x.shape[1], x.shape[2]
     key_dim, val_dim = states[0].shape[1:]
 
@@ -157,10 +162,10 @@
         return pl.BlockSpec((1,) + shape, lambda t, m: (m[at], 0, 0))
 
     def token_spec(at):
-        return pl.BlockSpec((1, TILE, d_model), lambda t, m: (m[at], t, 0))
+        return pl.BlockSpec((1, tile, d_model), lambda t, m: (m[at], t, 0))
 
     def tile_of(width, count=1, at=0):
-        return pl.BlockSpec((count, TILE, width), lambda t, m: (at, t, 0))
+        return pl.BlockSpec((count, tile, width), lambda t, m: (at, t, 0))
 
     def resident(arr):
         return pl.BlockSpec(arr.shape, lambda t, m: (0,) * arr.ndim, pipeline_mode=pl.Buffered(1))
@@ -184,7 +189,7 @@
         args.append(whole)
         specs.append(ANY)
     if zs:
-        whole_spec = token_spec(seqs[0]) if n == 1 else pl.BlockSpec((n, TILE, d_model), lambda t, m: (m[PAIR], t, 0))
+        whole_spec = token_spec(seqs[0]) if n == 1 else pl.BlockSpec((n, tile, d_model), lambda t, m: (m[PAIR], t, 0))
         outs = [(whole_spec, jax.ShapeDtypeStruct(x.shape, BF16))] + [(tile_of(d_model), jax.ShapeDtypeStruct((1, chunk_len, d_model), BF16))] * n
     else:
         outs = [(tile_of(val_dim, n), jax.ShapeDtypeStruct((n, chunk_len, val_dim), BF16))]
@@ -193,9 +198,9 @@
     flops = n * len(heads) * 2 * (d_model * (2 * key_dim + 2 * val_dim) + TILE * (key_dim + val_dim) + 2 * key_dim * val_dim)
     flops += n * 24 * d_model * val_dim if zs else 0
     return pl.pallas_call(
-        functools.partial(kernel_body, n, tuple(heads), len(zs), tuple(pieces), whole is not None),
+        functools.partial(kernel_body, n, n_sub, tuple(heads), len(zs), tuple(pieces), whole is not None),
         grid_spec=pltpu.PrefetchScalarGridSpec(
-            num_scalar_prefetch=1, grid=(chunk_len // TILE,), in_specs=specs, out_specs=[spec for spec, _ in outs],
+            num_scalar_prefetch=1, grid=(chunk_len // tile,), in_specs=specs, out_specs=[spec for spec, _ in outs],
             scratch_shapes=[pltpu.VMEM((len(heads), TILE, TILE), F32), pltpu.VMEM((len(heads), 3, TILE, 128), F32), pltpu.SemaphoreType.DMA((sum(map(len, pieces)),))]
             + [pltpu.VMEM((d_model, 2 * key_dim + 2 * val_dim), BF16) for _ in weights]),
         out_shape=[shape for _, shape in outs],
@@ -206,21 +211,21 @@
     )(meta, *args)
 
 
-def parts_kernel(meta_ref, w_q, w_k, w_v, w_g, w_o, w_down, w_up, own, heads_ref, mlp_ref, single_ref, twice_ref, sem):
-    rows, group = heads_ref.shape[0], meta_ref[GROUP]
+def parts_kernel(meta_ref, w_q, w_k, w_v, w_g, w_o, w_down, w_up, own, heads_out, mlp_out, single_out, twice_out, heads_buf, mlp_buf, single_buf, twice_buf, sem, sem_out):
+    rows, group = heads_buf.shape[0], meta_ref[GROUP]
     at = pl.ds(pl.multiple_of(group * rows, rows), rows)
     half = pl.ds(pl.multiple_of((group % 2) * rows, rows), rows)
     d_model = w_o.shape[1]
     copies, col = [], 0
     for w in (w_q, w_k, w_v, w_g):
-        copies.append(pltpu.make_async_copy(w.at[at], heads_ref.at[:, pl.ds(col, w.shape[1])], sem.at[len(copies)]))
+        copies.append(pltpu.make_async_copy(w.at[at], heads_buf.at[:, pl.ds(col, w.shape[1])], sem.at[len(copies)]))
         col += w.shape[1]
-    copies.append(pltpu.make_async_copy(w_up.at[at], mlp_ref.at[:, pl.ds(d_model, w_up.shape[1])], sem.at[len(copies)]))
-    copies.append(pltpu.make_async_copy(own.at[pl.ds(meta_ref[OTHER_CHIP], 2)], single_ref, sem.at[len(copies)]))
-    copies.append(pltpu.make_async_copy(own.at[pl.ds(4, 4)], twice_ref, sem.at[len(copies)]))
-    for copy in copies:
+    copies.append(pltpu.make_async_copy(w_up.at[at], mlp_buf.at[:, pl.ds(d_model, w_up.shape[1])], sem.at[len(copies)]))
+    copies.append(pltpu.make_async_copy(own.at[pl.ds(meta_ref[OTHER_CHIP], 2)], single_buf, sem.at[len(copies)]))
+    copies.append(pltpu.make_async_copy(own.at[pl.ds(4, 4)], twice_buf, sem.at[len(copies)]))
+    last = [pltpu.make_async_copy(w.at[half], mlp_buf.at[:, pl.ds(0, d_model)], sem.at[len(copies)]) for w in (w_o, w_down)]
+    for copy in copies[:5]:
         copy.start()
-    last = [pltpu.make_async_copy(w.at[half], mlp_ref.at[:, pl.ds(0, d_model)], sem.at[len(copies)]) for w in (w_o, w_down)]
 
     @pl.when(group < 2)
     def _():
@@ -230,8 +235,16 @@
     def _():
         last[1].start()
 
-    for copy in copies + last[:1]:
-        copy.wait()
+    for copy in copies[5:]:
+        copy.start()
+    pushes = [pltpu.make_async_copy(buf, out, sem_out.at[i]) for i, (buf, out) in
+              enumerate(((heads_buf, heads_out), (mlp_buf, mlp_out), (single_buf, single_out), (twice_buf, twice_out)))]
+    for push, pulls in zip(pushes, (copies[:4], [copies[4], last[0]], copies[5:6], copies[6:])):
+        for pull in pulls:
+            pull.wait()
+        push.start()
+    for push in pushes:
+        push.wait()
 
 
 def cut_parts(meta, head_w, mlp_w, own):
@@ -239,8 +252,8 @@
     shapes = [((n_rows, sum(w.shape[1] for w in head_w)), BF16), ((n_rows, mlp_w[0].shape[1] + mlp_w[2].shape[1]), BF16), ((2,) + own.shape[1:], F32), ((4,) + own.shape[1:], F32)]
     return pl.pallas_call(
         parts_kernel,
-        grid_spec=pltpu.PrefetchScalarGridSpec(num_scalar_prefetch=1, grid=(), in_specs=[ANY] * 8, out_specs=[pl.BlockSpec(memory_space=pltpu.VMEM)] * 4,
-                                               scratch_shapes=[pltpu.SemaphoreType.DMA((8,))]),
+        grid_spec=pltpu.PrefetchScalarGridSpec(num_scalar_prefetch=1, grid=(), in_specs=[ANY] * 8, out_specs=[ANY] * 4,
+                                               scratch_shapes=[pltpu.VMEM(*shape) for shape in shapes] + [pltpu.SemaphoreType.DMA((8,)), pltpu.SemaphoreType.DMA((4,))]),
         out_shape=[jax.ShapeDtypeStruct(shape, dtype) for shape, dtype in shapes],
         name="parts",
     )(meta, *head_w, *mlp_w, own)
@@ -348,12 +361,12 @@
         got_core = to_core(new_core)
 
         w_chip = heads_gathered(wa_quarters)
-        z_chip, new_chip = run(meta, common, one, (STATE_SINGLE,), (2,), (su_chip,), (w_chip,))
+        z_chip, new_chip = run(meta, common, one, (STATE_SINGLE,), (2,), (su_chip,), (w_chip,), n_sub=2)
         z_chip, wa_far, wb_far, wb_core, su_far, st_chip = lax.optimization_barrier((z_chip, wa_far, wb_far, wb_core, su_far, st_chip))
         st_far = to_core(st_chip)
         w_far = heads_gathered(wa_far)
         mlp = (mlp_places(mlp_w), mlp_places(wb_core), heads_gathered(wb_quarters), heads_gathered(wb_far))
-        whole, x_single, new_far = run(meta, common, one, (STATE_SINGLE,), (3,), (su_far,), (w_far, *mlp), ((z_own_single, 0), (z_core, 0), (z_chip, 0)))
+        whole, x_single, new_far = run(meta, common, one, (STATE_SINGLE,), (3,), (su_far,), (w_far, *mlp), ((z_own_single, 0), (z_core, 0), (z_chip, 0)), n_sub=2)
         x_single_chip = to_chip(x_single)
         x_single_core = to_core(x_single)
         got_chip = to_chip(new_chip)

time: 435 us -> 439 us (level)
  no operation moved by 1% of the time
where the time goes in v5:
time: 439 us
  Pallas kernels  295 us (67%)
  waiting for transfers between devices  111 us (25%)
  starting transfers between devices  21.8 us (5%)
  other arithmetic  5.38 us (1%)
  local copies, waits for them, and re-layouts  4.94 us (1%)
    pallas_call x6, Pallas kernels, run(): pl.pallas_call(functools.partial(kernel_body, n, n_sub, tuple(heads), len...  270 us
    ppermute x6, waiting for transfers between devices, gather(): return [part] + [swap('dp', flip)(part) for flip in range(1, n_dp)]  60.1 us
    pallas_call x4, Pallas kernels, place(): pl.pallas_call(functools.partial(place_kernel, tuple((block[1:] for block...  18.9 us
    ppermute x1, waiting for transfers between devices, local_layer(): got_far = to_far(new_far)  13.4 us
    ppermute x1, waiting for transfers between devices, local_layer(): got_chip = to_chip(new_chip)  13.4 us
    ppermute x1, waiting for transfers between devices, local_layer(): wa_part = to_chip(wa_part)  13 us
  transfers between devices with their start and end apart: 36, of which 12 were waited for; matrix products, arithmetic and copies ran while one was open for 1% of the time, Pallas kernels for 66%

profile of v5, /device:TPU:0, one launch (start us, length us, event | category | flops | bytes accessed | tf_op | source)
XLA Modules:
  0.0 438.9 jit_solution(6380630462257398466)
XLA Ops:
  2.6 5.4 %parts.1 = (bf16[256,1536]{1,0:T(8,128)(2,1)}, bf16[256,1536]{1,0:T(8,128)(2,1)}, f32[2,256,512]{2,1,0:T(8,128)}, f32[4,256,512]{2,1,0:T(8,128)}) custom-call(s32[10]{0:T(128)} %stack.68.meta_ref, bf16[1024,256]{1,0:T(8,128)(2,1)} %refs_3_.1, bf16[1024,256]{1,0:T(8,128)(2,1)} %refs_4_.1, bf16[1024,512]{1,0:T(8,128)(2,1)} %refs_5_.1, ...), custom_call_target="tpu_custom_call" | custom-call | tf_op jit(solution)/shard_map/parts/pallas_call | solution.py:253
  7.9 3.0 collective-permute-start.6
  14.7 1.7 broadcast_select_fusion.step_ref
  16.6 13.0 %collective-permute-done.6.refs_3_.refs_12_ = bf16[256,1536]{1,0:T(8,128)(2,1)S(1)} collective-permute-done((bf16[256,1536]{1,0:T(8,128)(2,1)}, bf16[256,1536]{1,0:T(8,128)(2,1)S(1)}, u32[]{:S(2)}, u32[]{:S(2)}) %collective-permute-start.6) | collective-permute-done | bytes 786464 | tf_op jit(solution)/shard_map/ppermute | solution.py:342
  29.5 2.0 collective-permute-start.13
  31.5 30.3 %heads.4 = (bf16[2,2048,512]{2,1,0:T(8,128)(2,1)}, f32[8,256,512]{2,1,0:T(8,128)}) custom-call(s32[10]{0:T(128)} %stack.68.meta_ref, f32[1,1024]{1,0:T(1,128)} %bitcast.33, f32[1,1024]{1,0:T(1,128)} %bitcast.39, f32[1,1024]{1,0:T(1,128)} %bitcast.45, f32[1,1024]{1,0:T(1,128)} %bitcast.51, f32[2,256,128]{2,1,0:T(8,128)} %broadcast_select_fusion.step_ref, ...), custom_call_target="tpu_custom_call" | custom-call | flops 16642998272 | bytes 16777216 | tf_op jit(solution)/shard_map/heads/pallas_call | solution.py:200
  61.9 18.4 %heads.6 = (bf16[1,2048,512]{2,1,0:T(8,128)(2,1)}, f32[1,256,512]{2,1,0:T(8,128)}) custom-call(s32[10]{0:T(128)} %stack.68.meta_ref, f32[1,1024]{1,0:T(1,128)} %bitcast.34, f32[1,1024]{1,0:T(1,128)} %bitcast.40, f32[1,1024]{1,0:T(1,128)} %bitcast.46, f32[1,1024]{1,0:T(1,128)} %bitcast.52, f32[2,256,128]{2,1,0:T(8,128)} %broadcast_select_fusion.step_ref, ...), custom_call_target="tpu_custom_call" | custom-call | flops 8321499136 | bytes 8388608 | tf_op jit(solution)/shard_map/heads/pallas_call | solution.py:200
  80.3 2.6 collective-permute-start.9
  83.9 2.5 collective-permute-start.12
  86.8 15.1 %collective-permute-done.9.refs_6_.refs_15_ = bf16[256,1536]{1,0:T(8,128)(2,1)S(1)} collective-permute-done((bf16[256,1536]{1,0:T(8,128)(2,1)}, bf16[256,1536]{1,0:T(8,128)(2,1)S(1)}, u32[]{:S(2)}, u32[]{:S(2)}) %collective-permute-start.9) | collective-permute-done | bytes 786464 | tf_op jit(solution)/shard_map/ppermute | solution.py:334
  101.9 16.9 %collective-permute-done.8.refs_5_.refs_14_ = bf16[256,1536]{1,0:T(8,128)(2,1)S(1)} collective-permute-done((bf16[256,1536]{1,0:T(8,128)(2,1)}, bf16[256,1536]{1,0:T(8,128)(2,1)S(1)}, u32[]{:S(2)}, u32[]{:S(2)}) %collective-permute-start.8) | collective-permute-done | bytes 786464 | tf_op jit(solution)/shard_map/ppermute | solution.py:334
  119.3 13.4 %collective-permute-done.12.refs_19_.refs_29_ = bf16[256,1536]{1,0:T(8,128)(2,1)S(1)} collective-permute-done((bf16[256,1536]{1,0:T(8,128)(2,1)}, bf16[256,1536]{1,0:T(8,128)(2,1)S(1)}, u32[]{:S(2)}, u32[]{:S(2)}) %collective-permute-start.12) | collective-permute-done | bytes 786464 | tf_op jit(solution)/shard_map/ppermute | solution.py:334
  134.8 14.7 %collective-permute-done.11.refs_18_.refs_28_ = bf16[256,1536]{1,0:T(8,128)(2,1)} collective-permute-done((bf16[256,1536]{1,0:T(8,128)(2,1)}, bf16[256,1536]{1,0:T(8,128)(2,1)}, u32[]{:S(2)}, u32[]{:S(2)}) %collective-permute-start.11) | collective-permute-done | bytes 786464 | tf_op jit(solution)/shard_map/ppermute | solution.py:334
  151.1 42.5 %heads.5 = (bf16[3,2048,512]{2,1,0:T(8,128)(2,1)}, f32[3,256,512]{2,1,0:T(8,128)}) custom-call(s32[10]{0:T(128)} %stack.68.meta_ref, f32[1,1024]{1,0:T(1,128)} %bitcast.35, f32[1,1024]{1,0:T(1,128)} %bitcast.41, f32[1,1024]{1,0:T(1,128)} %bitcast.47, f32[1,1024]{1,0:T(1,128)} %bitcast.53, f32[2,256,128]{2,1,0:T(8,128)} %broadcast_select_fusion.step_ref, ...), custom_call_target="tpu_custom_call" | custom-call | flops 24964497408 | bytes 25165824 | tf_op jit(solution)/shard_map/heads/pallas_call | solution.py:200
  200.4 17.7 %heads.7 = (bf16[1,2048,512]{2,1,0:T(8,128)(2,1)}, f32[1,256,512]{2,1,0:T(8,128)}) custom-call(s32[10]{0:T(128)} %stack.68.meta_ref, f32[1,1024]{1,0:T(1,128)} %bitcast.36, f32[1,1024]{1,0:T(1,128)} %bitcast.42, f32[1,1024]{1,0:T(1,128)} %bitcast.48, f32[1,1024]{1,0:T(1,128)} %bitcast.54, f32[2,256,128]{2,1,0:T(8,128)} %broadcast_select_fusion.step_ref, ...), custom_call_target="tpu_custom_call" | custom-call | flops 8321499136 | bytes 8388608 | tf_op jit(solution)/shard_map/heads/pallas_call | solution.py:200
  219.5 50.6 %tail.2 = (bf16[8,2048,1024]{2,1,0:T(8,128)(2,1)}, bf16[1,2048,1024]{2,1,0:T(8,128)(2,1)}, f32[1,256,512]{2,1,0:T(8,128)}) custom-call(s32[10]{0:T(128)} %stack.68.meta_ref, f32[1,1024]{1,0:T(1,128)} %bitcast.37, f32[1,1024]{1,0:T(1,128)} %bitcast.43, f32[1,1024]{1,0:T(1,128)} %bitcast.49, f32[1,1024]{1,0:T(1,128)} %bitcast.55, ...), custom_call_target="tpu_custom_call" | custom-call | flops 34091302912 | bytes 16777216 | tf_op jit(solution)/shard_map/tail/pallas_call | solution.py:200
  273.1 110.9 %tail.3 = (bf16[8,2048,1024]{2,1,0:T(8,128)(2,1)}, bf16[1,2048,1024]{2,1,0:T(8,128)(2,1)}, bf16[1,2048,1024]{2,1,0:T(8,128)(2,1)}, f32[2,256,512]{2,1,0:T(8,128)}, f32[2,256,512]{2,1,0:T(8,128)}) custom-call(s32[10]{0:T(128)} %stack.68.meta_ref, f32[1,1024]{1,0:T(1,128)} %bitcast.38, f32[1,1024]{1,0:T(1,128)} %bitcast.44, ...), custom_call_target="tpu_custom_call", output_to_operand_aliasing={{0}: (40, {})} | custom-call | flops 84825604096 | bytes 33554432 | tf_op jit(solution)/shard_map/tail/pallas_call | solution.py:200
  385.4 13.4 %collective-permute-done.34.refs_6_ = f32[1,256,512]{2,1,0:T(8,128)S(1)} collective-permute-done((f32[1,256,512]{2,1,0:T(8,128)S(1)}, f32[1,256,512]{2,1,0:T(8,128)S(1)}, u32[]{:S(2)}, u32[]{:S(2)}) %collective-permute-start.34) | collective-permute-done | bytes 524320 | tf_op jit(solution)/shard_map/ppermute | solution.py:372
  398.9 6.8 %collective-permute-done.33.refs_3_.refs_4_.refs_5_ = f32[3,256,512]{2,1,0:T(8,128)S(1)} collective-permute-done((f32[3,256,512]{2,1,0:T(8,128)}, f32[3,256,512]{2,1,0:T(8,128)S(1)}, u32[]{:S(2)}, u32[]{:S(2)}) %collective-permute-start.33) | collective-permute-done | bytes 1572896 | tf_op jit(solution)/shard_map/ppermute | solution.py:361
  406.3 13.4 %collective-permute-done.35.refs_7_ = f32[1,256,512]{2,1,0:T(8,128)S(1)} collective-permute-done((f32[1,256,512]{2,1,0:T(8,128)}, f32[1,256,512]{2,1,0:T(8,128)S(1)}, u32[]{:S(2)}, u32[]{:S(2)}) %collective-permute-start.35) | collective-permute-done | bytes 524320 | tf_op jit(solution)/shard_map/ppermute | solution.py:373
  419.7 8.2 %place.4 = (bf16[8,2048,1024]{2,1,0:T(8,128)(2,1)}, f32[8,256,512]{2,1,0:T(8,128)}) custom-call(s32[8]{0:T(128)S(1)} %stack.73.ids_ref, bf16[1,2048,1024]{2,1,0:T(8,128)(2,1)} %collective-permute-done.32.refs_0_, bf16[1,2048,1024]{2,1,0:T(8,128)(2,1)} %collective-permute-done.29.refs_1_, ...), custom_call_target="tpu_custom_call", output_to_operand_aliasing={{0}: (9, {}), {1}: (10, {})} | custom-call | tf_op jit(solution)/shard_map/place/pallas_call | solution.py:284
  427.9 3.6 place.5.refs_1_
  431.5 3.6 place.6.refs_1_
  435.1 3.6 place.7
  (121 shorter events, 24.6 us)
Async XLA Ops:
  0.6 83.2 %collective-permute-start.4 = (f32[8,256,512]{2,1,0:T(8,128)}, f32[8,256,512]{2,1,0:T(8,128)}, u32[]{:S(2)}, u32[]{:S(2)}) collective-permute-start(f32[8,256,512]{2,1,0:T(8,128)} %bitcast.27), channel_id=1, source_target_pairs={{0,1},{1,0},{2,3},{3,2},{4,5},{5,4},{6,7},{7,6},{8,9},{9,8},{10,11... | collective-permute-start | bytes 12582920 | tf_op jit(solution)/shard_map/ppermute | solution.py:340
  1.9 81.0 %collective-permute-start.2 = (bf16[1024,512]{1,0:T(8,128)(2,1)}, bf16[1024,512]{1,0:T(8,128)(2,1)S(1)}, u32[]{:S(2)}, u32[]{:S(2)}) collective-permute-start(bf16[1024,512]{1,0:T(8,128)(2,1)} %refs_5_.1), channel_id=1, source_target_pairs={{0,1},{1,0},{2,3},{3,2},{4,5},{5,4},{6,7},{7,6},{8,9},{9,8},{10,11... | collective-permute-start | bytes 3145736 | tf_op jit(solution)/shard_map/ppermute | solution.py:339
  7.9 21.6 %collective-permute-start.6 = (bf16[256,1536]{1,0:T(8,128)(2,1)}, bf16[256,1536]{1,0:T(8,128)(2,1)S(1)}, u32[]{:S(2)}, u32[]{:S(2)}) collective-permute-start(bf16[256,1536]{1,0:T(8,128)(2,1)} %get-tuple-element.64), channel_id=1, source_target_pairs={{0,2},{1,3},{2,0},{3,1},{4,6},{5,7},{6,4},{7,5},{8,10},{9,11},{10,... | collective-permute-start | bytes 2359304 | tf_op jit(solution)/shard_map/ppermute | solution.py:342
  16.4 66.9 %collective-permute-start.3 = (bf16[1024,512]{1,0:T(8,128)(2,1)S(1)}, bf16[1024,512]{1,0:T(8,128)(2,1)S(1)}, u32[]{:S(2)}, u32[]{:S(2)}) collective-permute-start(bf16[1024,512]{1,0:T(8,128)(2,1)S(1)} %copy-done.1), channel_id=1, source_target_pairs={{0,1},{1,0},{2,3},{3,2},{4,5},{5,4},{6,7},{7,6},{8,9},{9,8},{10,11... | collective-permute-start | bytes 3145736 | tf_op jit(solution)/shard_map/ppermute | solution.py:339
  16.5 63.8 %collective-permute-start.5 = (bf16[256,1536]{1,0:T(8,128)(2,1)}, bf16[256,1536]{1,0:T(8,128)(2,1)}, u32[]{:S(2)}, u32[]{:S(2)}) collective-permute-start(bf16[256,1536]{1,0:T(8,128)(2,1)} %get-tuple-element.56), channel_id=1, source_target_pairs={{0,2},{1,3},{2,0},{3,1},{4,6},{5,7},{6,4},{7,5},{8,10},{9,11},{10,... | collective-permute-start | bytes 2359304 | tf_op jit(solution)/shard_map/ppermute | solution.py:343
  29.5 56.9 %collective-permute-start.13 = (f32[2,256,512]{2,1,0:T(8,128)}, f32[2,256,512]{2,1,0:T(8,128)S(1)}, u32[]{:S(2)}, u32[]{:S(2)}) collective-permute-start(f32[2,256,512]{2,1,0:T(8,128)} %get-tuple-element.67), channel_id=1, source_target_pairs={{0,2},{1,3},{2,0},{3,1},{4,6},{5,7},{6,4},{7,5},{8,10},{9,11},{10,... | collective-permute-start | bytes 3145736 | tf_op jit(solution)/shard_map/ppermute | solution.py:344
  80.3 21.6 %collective-permute-start.9 = (bf16[256,1536]{1,0:T(8,128)(2,1)}, bf16[256,1536]{1,0:T(8,128)(2,1)S(1)}, u32[]{:S(2)}, u32[]{:S(2)}) collective-permute-start(bf16[256,1536]{1,0:T(8,128)(2,1)} %copy-done.6), channel_id=1, source_target_pairs={{0,12},{4,8},{8,4},{12,0},{1,13},{5,9},{9,5},{13,1},{2,14},{6,10},... | collective-permute-start | bytes 2359304 | tf_op jit(solution)/shard_map/ppermute | solution.py:334
  82.9 35.9 %collective-permute-start.8 = (bf16[256,1536]{1,0:T(8,128)(2,1)}, bf16[256,1536]{1,0:T(8,128)(2,1)S(1)}, u32[]{:S(2)}, u32[]{:S(2)}) collective-permute-start(bf16[256,1536]{1,0:T(8,128)(2,1)} %copy-done.6), channel_id=1, source_target_pairs={{0,8},{4,12},{8,0},{12,4},{1,9},{5,13},{9,1},{13,5},{2,10},{6,14},... | collective-permute-start | bytes 2359304 | tf_op jit(solution)/shard_map/ppermute | solution.py:334
  83.3 35.5 %collective-permute-start.7 = (bf16[256,1536]{1,0:T(8,128)(2,1)}, bf16[256,1536]{1,0:T(8,128)(2,1)S(1)}, u32[]{:S(2)}, u32[]{:S(2)}) collective-permute-start(bf16[256,1536]{1,0:T(8,128)(2,1)} %copy-done.6), channel_id=1, source_target_pairs={{0,4},{4,0},{8,12},{12,8},{1,5},{5,1},{9,13},{13,9},{2,6},{6,2},{1... | collective-permute-start | bytes 2359304 | tf_op jit(solution)/shard_map/ppermute | solution.py:334
  83.9 48.9 %collective-permute-start.12 = (bf16[256,1536]{1,0:T(8,128)(2,1)}, bf16[256,1536]{1,0:T(8,128)(2,1)S(1)}, u32[]{:S(2)}, u32[]{:S(2)}) collective-permute-start(bf16[256,1536]{1,0:T(8,128)(2,1)} %collective-permute-done.5.refs_16_.refs_26_), channel_id=1, source_target_pairs={{0,12},{4,8},{8,4},{12,0},{1,13},{5,9},{9,5},{13,1},{2,14},{6,10},... | collective-permute-start | bytes 2359304 | tf_op jit(solution)/shard_map/ppermute | solution.py:334
  86.4 63.2 %collective-permute-start.11 = (bf16[256,1536]{1,0:T(8,128)(2,1)}, bf16[256,1536]{1,0:T(8,128)(2,1)}, u32[]{:S(2)}, u32[]{:S(2)}) collective-permute-start(bf16[256,1536]{1,0:T(8,128)(2,1)} %collective-permute-done.5.refs_16_.refs_26_), channel_id=1, source_target_pairs={{0,8},{4,12},{8,0},{12,4},{1,9},{5,13},{9,1},{13,5},{2,10},{6,14},... | collective-permute-start | bytes 2359304 | tf_op jit(solution)/shard_map/ppermute | solution.py:334
  101.9 91.8 %collective-permute-start.22 = (bf16[512,1024]{1,0:T(8,128)(2,1)S(1)}, bf16[512,1024]{1,0:T(8,128)(2,1)}, u32[]{:S(2)}, u32[]{:S(2)}) collective-permute-start(bf16[512,1024]{1,0:T(8,128)(2,1)S(1)} %copy-done.5), channel_id=1, source_target_pairs={{0,1},{1,0},{2,3},{3,2},{4,5},{5,4},{6,7},{7,6},{8,9},{9,8},{10,11... | collective-permute-start | bytes 3145736 | tf_op jit(solution)/shard_map/ppermute | solution.py:346
  118.8 75.3 %collective-permute-start.24 = (bf16[1024,512]{1,0:T(8,128)(2,1)}, bf16[1024,512]{1,0:T(8,128)(2,1)}, u32[]{:S(2)}, u32[]{:S(2)}) collective-permute-start(bf16[1024,512]{1,0:T(8,128)(2,1)} %refs_22_.1), channel_id=1, source_target_pairs={{0,1},{1,0},{2,3},{3,2},{4,5},{5,4},{6,7},{7,6},{8,9},{9,8},{10,11... | collective-permute-start | bytes 3145736 | tf_op jit(solution)/shard_map/ppermute | solution.py:346
  118.8 75.4 %collective-permute-start.23 = (bf16[512,1024]{1,0:T(8,128)(2,1)}, bf16[512,1024]{1,0:T(8,128)(2,1)}, u32[]{:S(2)}, u32[]{:S(2)}) collective-permute-start(bf16[512,1024]{1,0:T(8,128)(2,1)} %refs_21_.1), channel_id=1, source_target_pairs={{0,1},{1,0},{2,3},{3,2},{4,5},{5,4},{6,7},{7,6},{8,9},{9,8},{10,11... | collective-permute-start | bytes 3145736 | tf_op jit(solution)/shard_map/ppermute | solution.py:346
  133.7 61.0 %collective-permute-start.26 = (f32[4,256,512]{2,1,0:T(8,128)}, f32[4,256,512]{2,1,0:T(8,128)}, u32[]{:S(2)}, u32[]{:S(2)}) collective-permute-start(f32[4,256,512]{2,1,0:T(8,128)} %get-tuple-element.78), channel_id=1, source_target_pairs={{0,2},{1,3},{2,0},{3,1},{4,6},{5,7},{6,4},{7,5},{8,10},{9,11},{10,... | collective-permute-start | bytes 6291464 | tf_op jit(solution)/shard_map/ppermute | solution.py:345
  149.6 44.0 %collective-permute-start.10 = (bf16[256,1536]{1,0:T(8,128)(2,1)}, bf16[256,1536]{1,0:T(8,128)(2,1)}, u32[]{:S(2)}, u32[]{:S(2)}) collective-permute-start(bf16[256,1536]{1,0:T(8,128)(2,1)} %collective-permute-done.5.refs_16_.refs_26_), channel_id=1, source_target_pairs={{0,4},{4,0},{8,12},{12,8},{1,5},{5,1},{9,13},{13,9},{2,6},{6,2},{1... | collective-permute-start | bytes 2359304 | tf_op jit(solution)/shard_map/ppermute | solution.py:334
  194.7 23.4 %collective-permute-start.25 = (f32[2,256,512]{2,1,0:T(8,128)S(1)}, f32[2,256,512]{2,1,0:T(8,128)S(1)}, u32[]{:S(2)}, u32[]{:S(2)}) collective-permute-start(f32[2,256,512]{2,1,0:T(8,128)S(1)} %collective-permute-done.13.refs_2_), channel_id=1, source_target_pairs={{0,1},{1,0},{2,3},{3,2},{4,5},{5,4},{6,7},{7,6},{8,9},{9,8},{10,11... | collective-permute-start | bytes 3145736 | tf_op jit(solution)/shard_map/ppermute | solution.py:360
  195.9 22.1 %collective-permute-start.18 = (bf16[256,1536]{1,0:T(8,128)(2,1)}, bf16[256,1536]{1,0:T(8,128)(2,1)S(1)}, u32[]{:S(2)}, u32[]{:S(2)}) collective-permute-start(bf16[256,1536]{1,0:T(8,128)(2,1)} %collective-permute-done.5.refs_16_.refs_26_), channel_id=1, source_target_pairs={{0,1},{1,0},{2,3},{3,2},{4,5},{5,4},{6,7},{7,6},{8,9},{9,8},{10,11... | collective-permute-start | bytes 2359304 | tf_op jit(solution)/shard_map/ppermute | solution.py:360
  218.1 53.6 %collective-permute-start.27 = (f32[4,256,512]{2,1,0:T(8,128)}, f32[4,256,512]{2,1,0:T(8,128)S(1)}, u32[]{:S(2)}, u32[]{:S(2)}) collective-permute-start(f32[4,256,512]{2,1,0:T(8,128)} %collective-permute-done.26.refs_4_.refs_5_), channel_id=1, source_target_pairs={{0,1},{1,0},{2,3},{3,2},{4,5},{5,4},{6,7},{7,6},{8,9},{9,8},{10,11... | collective-permute-start | bytes 6291464 | tf_op jit(solution)/shard_map/ppermute | solution.py:366
  270.1 149.6 %collective-permute-start.32 = (bf16[1,2048,1024]{2,1,0:T(8,128)(2,1)}, bf16[1,2048,1024]{2,1,0:T(8,128)(2,1)}, u32[]{:S(2)}, u32[]{:S(2)}) collective-permute-start(bf16[1,2048,1024]{2,1,0:T(8,128)(2,1)} %get-tuple-element.98), channel_id=1, source_target_pairs={{0,1},{1,0},{2,3},{3,2},{4,5},{5,4},{6,7},{7,6},{8,9},{9,8},{10,11... | collective-permute-start | bytes 12582920 | tf_op jit(solution)/shard_map/ppermute | solution.py:371
  270.5 113.5 %collective-permute-start.29 = (bf16[1,2048,1024]{2,1,0:T(8,128)(2,1)}, bf16[1,2048,1024]{2,1,0:T(8,128)(2,1)}, u32[]{:S(2)}, u32[]{:S(2)}) collective-permute-start(bf16[1,2048,1024]{2,1,0:T(8,128)(2,1)} %get-tuple-element.98), channel_id=1, source_target_pairs={{0,2},{1,3},{2,0},{3,1},{4,6},{5,7},{6,4},{7,5},{8,10},{9,11},{10,... | collective-permute-start | bytes 12582920 | tf_op jit(solution)/shard_map/ppermute | solution.py:370
  384.0 44.0 %collective-permute-start.31 = (bf16[1,2048,1024]{2,1,0:T(8,128)(2,1)}, bf16[1,2048,1024]{2,1,0:T(8,128)(2,1)}, u32[]{:S(2)}, u32[]{:S(2)}) collective-permute-start(bf16[1,2048,1024]{2,1,0:T(8,128)(2,1)} %get-tuple-element.99), channel_id=1, source_target_pairs={{0,1},{1,0},{2,3},{3,2},{4,5},{5,4},{6,7},{7,6},{8,9},{9,8},{10,11... | collective-permute-start | bytes 12582920 | tf_op jit(solution)/shard_map/ppermute | solution.py:376
  384.0 47.5 %collective-permute-start.30 = (bf16[1,2048,1024]{2,1,0:T(8,128)(2,1)}, bf16[1,2048,1024]{2,1,0:T(8,128)(2,1)}, u32[]{:S(2)}, u32[]{:S(2)}) collective-permute-start(bf16[1,2048,1024]{2,1,0:T(8,128)(2,1)} %collective-permute-done.29.refs_1_), channel_id=1, source_target_pairs={{0,1},{1,0},{2,3},{3,2},{4,5},{5,4},{6,7},{7,6},{8,9},{9,8},{10,11... | collective-permute-start | bytes 12582920 | tf_op jit(solution)/shard_map/ppermute | solution.py:377
  384.5 50.6 %collective-permute-start.28 = (bf16[1,2048,1024]{2,1,0:T(8,128)(2,1)}, bf16[1,2048,1024]{2,1,0:T(8,128)(2,1)}, u32[]{:S(2)}, u32[]{:S(2)}) collective-permute-start(bf16[1,2048,1024]{2,1,0:T(8,128)(2,1)} %get-tuple-element.97), channel_id=1, source_target_pairs={{0,1},{1,0},{2,3},{3,2},{4,5},{5,4},{6,7},{7,6},{8,9},{9,8},{10,11... | collective-permute-start | bytes 12582920 | tf_op jit(solution)/shard_map/ppermute | solution.py:379
  (36 other events, 951.6 us)

commit v6 on v5

--- a/solution.py
+++ b/solution.py
@@ -59,29 +59,29 @@
         rows_ref[i, 2] = jnp.exp(jnp.full((TILE, 128), TILE, F32) * log_gamma)
 
 
-def head_blocks(h, w_ref, state_ref, inner, rows_ref, tables):
+def head_blocks(hs, w_ref, state_ref, inner, rows_ref, tables):
     n_seqs, key_dim, val_dim = state_ref.shape
-    q_raw = dot(h, w_ref[:, :key_dim])
-    k_raw = dot(h, w_ref[:, key_dim:2 * key_dim])
-    values = dot(h, w_ref[:, 2 * key_dim:2 * key_dim + val_dim]).astype(BF16)
-    gates = dot(h, w_ref[:, 2 * key_dim + val_dim:])
     out = []
-    for i, table in enumerate(tables):
-        at, b = slice(i * TILE, (i + 1) * TILE), i * n_seqs // len(tables)
-        queries = rotate(q_raw[at], *table).astype(BF16)
-        keys = (rotate(k_raw[at], *table) * key_dim ** -0.5).astype(BF16)
+    for i, (h, table) in enumerate(zip(hs, tables)):
+        b = i * n_seqs // len(tables)
+        q_raw = dot(h, w_ref[:, :key_dim])
+        k_raw = dot(h, w_ref[:, key_dim:2 * key_dim])
+        queries = rotate(q_raw, *table).astype(BF16)
+        keys = (rotate(k_raw, *table) * key_dim ** -0.5).astype(BF16)
+        values = dot(h, w_ref[:, 2 * key_dim:2 * key_dim + val_dim]).astype(BF16)
         scores = lax.dot_general(queries, keys, (((1,), (1,)), ((), ())), preferred_element_type=F32) * inner
         state = state_ref[b]
         carried = dot(queries, state.astype(BF16)) * widen(rows_ref[0], val_dim)
-        retained = dot(scores.astype(BF16), values[at]) + carried
+        retained = dot(scores.astype(BF16), values) + carried
+        gates = dot(h, w_ref[:, 2 * key_dim + val_dim:])
         faded = (keys.astype(F32) * widen(rows_ref[1], key_dim)).astype(BF16)
-        update = lax.dot_general(faded, values[at], (((0,), (0,)), ((), ())), preferred_element_type=F32)
+        update = lax.dot_general(faded, values, (((0,), (0,)), ((), ())), preferred_element_type=F32)
         state_ref[b] = state * widen(rows_ref[2, 0:1], val_dim) + update
         row_mean = jnp.mean(retained, axis=-1, keepdims=True)
         centered = retained - row_mean
         variance = jnp.mean(centered * centered, axis=-1, keepdims=True)
         normed = centered * lax.rsqrt(variance + GROUP_EPS)
-        out.append((gates[at] * lax.logistic(gates[at]) * normed).astype(BF16))
+        out.append((gates * lax.logistic(gates) * normed).astype(BF16))
     return out
 
 
@@ -92,22 +92,23 @@
         return [next(it) for _ in range(n)]
 
     x_refs, base_refs, s_refs, z_refs = take(n_seqs), take(n_seqs), [take(n_seqs) for _ in heads], [take(n_seqs) for _ in range(n_z)]
-    sources = [take(len(p)) for p in pieces]
+    sources = take(len(pieces))
     take(with_whole)
     outs = take(1 + n_seqs if n_z else 1)
     state_refs = take(len(heads))
     inner_ref, rows_ref, sem = take(3)
-    weights = take(len(pieces))
+    weights = list(it)
 
     @pl.when(pl.program_id(0) == 0)
     def _():
         copies = []
-        for w_ref, refs_in, places in zip(weights, sources, pieces):
-            for ref, (row, col, flip) in zip(refs_in, places):
+        for ref, cuts in zip(sources, pieces):
+            for to, row, col, first, width, flip, skip in cuts:
                 if flip is not None:
-                    row = pl.multiple_of((meta_ref[GROUP] ^ flip) * ref.shape[0], 256)
-                dst = w_ref.at[pl.ds(row, ref.shape[0]), pl.ds(col, ref.shape[1])]
-                copies.append(pltpu.make_async_copy(ref, dst, sem.at[len(copies)]))
+                    quarter = meta_ref[GROUP] ^ flip
+                    row = pl.multiple_of(row + quarter * ref.shape[0] + quarter // 2 * skip, 256)
+                dst = weights[to].at[pl.ds(row, ref.shape[0]), pl.ds(col, width)]
+                copies.append(pltpu.make_async_copy(ref.at[:, pl.ds(first, width)], dst, sem.at[len(copies)]))
                 copies[-1].start()
         fill_decays([log_decay(meta_ref[HEAD] ^ head) for head in heads], inner_ref, rows_ref)
         for per_head, state_ref in zip(s_refs, state_refs):
@@ -124,24 +125,24 @@
             at = pl.multiple_of((pl.program_id(0) * n_sub + j) * 8, 8)
             cos_a, sin_a = base_ref[0, pl.ds(at, 1), :], base_ref[0, pl.ds(at + 1, 1), :]
             tables.append((cos_a * cos_b - sin_a * sin_b, sin_a * cos_b + cos_a * sin_b))
-    h = below(normed)
-    mixed = [head_blocks(h, weights[i], state_refs[i], inner_ref[i], rows_ref.at[i], tables) for i in range(len(heads))]
+    hs = [h[j * TILE:(j + 1) * TILE] for h in normed for j in range(n_sub)]
+    mixed = [head_blocks(hs, weights[i], state_refs[i], inner_ref[i], rows_ref.at[i], tables) for i in range(len(heads))]
     rows = n_sub * TILE
     if not n_z:
         for i, block in enumerate(mixed[0]):
             outs[0][i // n_sub, i % n_sub * TILE:(i % n_sub + 1) * TILE] = block
         return
     mixed = [[ref[0] for ref in refs_of] for refs_of in z_refs] + mixed
-    blocks = weights[len(heads):]
-    val_dim, d_model = mixed[0][0].shape[1], x_refs[0].shape[2]
-    u = sum(dot(below(z), wb[:val_dim, :d_model]) for z, wb in zip(mixed, blocks))
+    w_od, w_up = weights[len(heads):]
+    width = w_up.shape[1]
+    u = dot(jnp.concatenate([below(z) for z in mixed], axis=1), w_od[:width])
     x_mid = (below([x_ref[0] for x_ref in x_refs]).astype(F32) + u.astype(BF16).astype(F32)).astype(BF16)
     h_two = layer_norm(x_mid.astype(F32), gain2[...], bias2[...]).astype(BF16)
-    f = jnp.zeros(u.shape, F32)
-    for wb in blocks:
-        up = dot(h_two, wb[:, d_model:])
-        act = (up * 0.5 * (1.0 + lax.erf(up * 0.5 ** 0.5))).astype(BF16)
-        f = f + dot(act, wb[val_dim:, :d_model])
+    acts = []
+    for at in range(0, width, width // 4):
+        up = dot(h_two, w_up[:, at:at + width // 4])
+        acts.append((up * 0.5 * (1.0 + lax.erf(up * 0.5 ** 0.5))).astype(BF16))
+    f = dot(jnp.concatenate(acts, axis=1), w_od[width:])
     x_out = (x_mid.astype(F32) + f.astype(BF16).astype(F32)).astype(BF16)
     for b in range(n_seqs):
         outs[0][b] = x_out[b * rows:(b + 1) * rows]
@@ -178,11 +179,12 @@
     for z, first in zs:
         specs += [tile_of(val_dim, 1, first + b) for b in range(n)]
         args += [z] * n
-    pieces = []
-    for weight in weights:
-        pieces.append(tuple(place for _, place in weight))
-        args += [arr for arr, _ in weight]
-        specs += [ANY] * len(weight)
+    pieces = [cuts for _, cuts in weights]
+    args += [arr for arr, _ in weights]
+    specs += [ANY] * len(weights)
+    scratch = [(d_model, 2 * key_dim + 2 * val_dim)] * len(heads)
+    if zs:
+        scratch += [(2 * NUM_HEADS * val_dim, d_model), (d_model, NUM_HEADS * val_dim)]
     aliases = {}
     if whole is not None:
         aliases = {len(args) + 1: 0}
@@ -202,7 +204,7 @@
         grid_spec=pltpu.PrefetchScalarGridSpec(
             num_scalar_prefetch=1, grid=(chunk_len // tile,), in_specs=specs, out_specs=[spec for spec, _ in outs],
             scratch_shapes=[pltpu.VMEM((len(heads), TILE, TILE), F32), pltpu.VMEM((len(heads), 3, TILE, 128), F32), pltpu.SemaphoreType.DMA((sum(map(len, pieces)),))]
-            + [pltpu.VMEM((d_model, 2 * key_dim + 2 * val_dim), BF16) for _ in weights]),
+            + [pltpu.VMEM(shape, BF16) for shape in scratch]),
         out_shape=[shape for _, shape in outs],
         compiler_params=pltpu.CompilerParams(dimension_semantics=("arbitrary",), vmem_limit_bytes=58 << 20),
         cost_estimate=pl.CostEstimate(flops=chunk_len * flops, bytes_accessed=n * chunk_len * d_model * (8 if zs else 4), transcendentals=0),
@@ -321,14 +323,22 @@
         own = kv_state[:, 0]
         key_dim, val_dim = own.shape[1:]
 
-        def head_places(arrs):
-            return [(w, (0, col, None)) for w, col in zip(arrs, (0, key_dim, 2 * key_dim, 2 * key_dim + val_dim))]
-
-        def mlp_places(arrs):
-            return [(w, at) for w, at in zip(arrs, ((0, 0, None), (val_dim, 0, None), (0, d_model, None)))]
-
-        def heads_gathered(quarters):
-            return [(w, (0, 0, flip)) for flip, w in enumerate(quarters)]
+        def head_places(arrs, to=0):
+            return [(w, ((to, 0, col, 0, w.shape[1], None, 0),)) for w, col in zip(arrs, (0, key_dim, 2 * key_dim, 2 * key_dim + val_dim))]
+
+        def heads_gathered(quarters, to=0):
+            return [(w, ((to, 0, 0, 0, w.shape[1], flip, 0),)) for flip, w in enumerate(quarters)]
+
+        def mlp_places(arrs, i, to):
+            at, down = i * val_dim, NUM_HEADS * val_dim
+            return [(w, ((t, row, col, 0, w.shape[1], None, 0),)) for w, (t, row, col) in zip(arrs, ((to, at, 0), (to, down + at, 0), (to + 1, 0, at)))]
+
+        def mlp_gathered(quarters, i, to):
+            at, skip = i * val_dim, (NUM_HEADS - 1) * val_dim
+            return [(w, ((to, at, 0, 0, d_model, flip, skip), (to + 1, 0, at, d_model, val_dim, flip, 0))) for flip, w in enumerate(quarters)]
+
+        def mlp(to):
+            return mlp_places(mlp_w, 0, to) + mlp_places(wb_core, 1, to) + mlp_gathered(wb_quarters, 2, to) + mlp_gathered(wb_far, 3, to)
 
         def gather(part):
             return [part] + [swap("dp", flip)(part) for flip in range(1, n_dp)]
@@ -349,29 +359,26 @@
         common = (x_in, norms, *rope_tables(start_pos, chunk_len, key_dim))
         all_seqs, pair_seqs, one = (SEQ, SEQ + 1, SEQ + 2), (SEQ + 1, SEQ + 2), (SEQ,)
 
-        z_own_single, new_own_single = run(meta, common, one, one, (0,), (own,), (head_places(head_w),))
+        z_own_single, new_own_single = run(meta, common, one, one, (0,), (own,), head_places(head_w))
         z_own_single, wa_part = lax.optimization_barrier((z_own_single, wa_part))
         wa_quarters = gather(wa_part)
-        z_own, new_states = run(meta, common, pair_seqs, pair_seqs, (0,), (own,), (head_places(head_w),), pair=True)
+        z_own, new_states = run(meta, common, pair_seqs, pair_seqs, (0,), (own,), head_places(head_w), pair=True)
         z_own, wa_core, s_core, wb_part = lax.optimization_barrier((z_own, wa_core, s_core, wb_part))
         wb_quarters = gather(wb_part)
-        z_core, new_core = run(meta, common, all_seqs, all_seqs, (1,), (s_core,), (head_places(wa_core),))
+        z_core, new_core = run(meta, common, all_seqs, all_seqs, (1,), (s_core,), head_places(wa_core))
         z_core, wa_quarters, wb_quarters, su_chip = lax.optimization_barrier((z_core, wa_quarters, wb_quarters, su_chip))
         wa_far, wb_far, su_far = [to_core(w) for w in wa_quarters], [to_core(w) for w in wb_quarters], to_core(su_chip)
         got_core = to_core(new_core)
 
-        w_chip = heads_gathered(wa_quarters)
-        z_chip, new_chip = run(meta, common, one, (STATE_SINGLE,), (2,), (su_chip,), (w_chip,), n_sub=2)
+        z_chip, new_chip = run(meta, common, one, (STATE_SINGLE,), (2,), (su_chip,), heads_gathered(wa_quarters))
         z_chip, wa_far, wb_far, wb_core, su_far, st_chip = lax.optimization_barrier((z_chip, wa_far, wb_far, wb_core, su_far, st_chip))
         st_far = to_core(st_chip)
-        w_far = heads_gathered(wa_far)
-        mlp = (mlp_places(mlp_w), mlp_places(wb_core), heads_gathered(wb_quarters), heads_gathered(wb_far))
-        whole, x_single, new_far = run(meta, common, one, (STATE_SINGLE,), (3,), (su_far,), (w_far, *mlp), ((z_own_single, 0), (z_core, 0), (z_chip, 0)), n_sub=2)
+        whole, x_single, new_far = run(meta, common, one, (STATE_SINGLE,), (3,), (su_far,), heads_gathered(wa_far) + mlp(1), ((z_own_single, 0), (z_core, 0), (z_chip, 0)), n_sub=2)
         x_single_chip = to_chip(x_single)
         x_single_core = to_core(x_single)
         got_chip = to_chip(new_chip)
         got_far = to_far(new_far)
-        whole, x_a, x_b, _, _ = run(meta, common, pair_seqs, (STATE_TWICE, STATE_TWICE + 1), (2, 3), (st_chip, st_far), (w_chip, w_far, *mlp),
+        whole, x_a, x_b, _, _ = run(meta, common, pair_seqs, (STATE_TWICE, STATE_TWICE + 1), (2, 3), (st_chip, st_far), heads_gathered(wa_quarters) + heads_gathered(wa_far, 1) + mlp(2),
                                     ((z_own, 0), (z_core, 1)), whole)
         x_a_core = to_core(x_a)
         x_single_far = to_core(x_single_chip)

time: 439 us -> 431 us (0.982)
  Pallas kernels: 295 us -> 286 us
    pallas_call x6, Pallas kernels: 270 us -> 262 us  [run(): pl.pallas_call(functools.partial(kernel_body, n, n_sub, tuple(heads), len...]
where the time goes in v6:
time: 431 us; the launch traced here: 430 us
  Pallas kernels  286 us (66%)
  waiting for transfers between devices  111 us (26%)
  starting transfers between devices  21.8 us (5%)
  other arithmetic  5.38 us (1%)
  local copies, waits for them, and re-layouts  4.94 us (1%)
    pallas_call x6, Pallas kernels, run(): pl.pallas_call(functools.partial(kernel_body, n, n_sub, tuple(heads), len...  262 us
    ppermute x6, waiting for transfers between devices, gather(): return [part] + [swap('dp', flip)(part) for flip in range(1, n_dp)]  60.1 us
    pallas_call x4, Pallas kernels, place(): pl.pallas_call(functools.partial(place_kernel, tuple((block[1:] for block...  18.9 us
    ppermute x1, waiting for transfers between devices, local_layer(): got_far = to_far(new_far)  13.4 us
    ppermute x1, waiting for transfers between devices, local_layer(): got_chip = to_chip(new_chip)  13.4 us
    ppermute x1, waiting for transfers between devices, local_layer(): wa_part = to_chip(wa_part)  13 us
  transfers between devices with their start and end apart: 36, of which 12 were waited for; matrix products, arithmetic and copies ran while one was open for 1% of the time, Pallas kernels for 66%

profile of v6, /device:TPU:0, one launch (start us, length us, event | category | flops | bytes accessed | tf_op | source)
XLA Modules:
  0.0 430.2 jit_solution(12327266454970304355)
XLA Ops:
  2.6 5.4 %parts.1 = (bf16[256,1536]{1,0:T(8,128)(2,1)}, bf16[256,1536]{1,0:T(8,128)(2,1)}, f32[2,256,512]{2,1,0:T(8,128)}, f32[4,256,512]{2,1,0:T(8,128)}) custom-call(s32[10]{0:T(128)} %stack.68.meta_ref, bf16[1024,256]{1,0:T(8,128)(2,1)} %refs_3_.1, bf16[1024,256]{1,0:T(8,128)(2,1)} %refs_4_.1, bf16[1024,512]{1,0:T(8,128)(2,1)} %refs_5_.1, ...), custom_call_target="tpu_custom_call" | custom-call | tf_op jit(solution)/shard_map/parts/pallas_call | solution.py:255
  7.9 3.0 collective-permute-start.6
  14.7 1.7 broadcast_select_fusion.step_ref
  16.6 13.0 %collective-permute-done.6.refs_3_.refs_12_ = bf16[256,1536]{1,0:T(8,128)(2,1)S(1)} collective-permute-done((bf16[256,1536]{1,0:T(8,128)(2,1)}, bf16[256,1536]{1,0:T(8,128)(2,1)S(1)}, u32[]{:S(2)}, u32[]{:S(2)}) %collective-permute-start.6) | collective-permute-done | bytes 786464 | tf_op jit(solution)/shard_map/ppermute | solution.py:352
  29.5 2.0 collective-permute-start.13
  31.5 27.8 %heads.4 = (bf16[2,2048,512]{2,1,0:T(8,128)(2,1)}, f32[8,256,512]{2,1,0:T(8,128)}) custom-call(s32[10]{0:T(128)} %stack.68.meta_ref, f32[1,1024]{1,0:T(1,128)} %bitcast.33, f32[1,1024]{1,0:T(1,128)} %bitcast.39, f32[1,1024]{1,0:T(1,128)} %bitcast.45, f32[1,1024]{1,0:T(1,128)} %bitcast.51, f32[2,256,128]{2,1,0:T(8,128)} %broadcast_select_fusion.step_ref, ...), custom_call_target="tpu_custom_call" | custom-call | flops 16642998272 | bytes 16777216 | tf_op jit(solution)/shard_map/heads/pallas_call | solution.py:202
  59.4 17.8 %heads.6 = (bf16[1,2048,512]{2,1,0:T(8,128)(2,1)}, f32[1,256,512]{2,1,0:T(8,128)}) custom-call(s32[10]{0:T(128)} %stack.68.meta_ref, f32[1,1024]{1,0:T(1,128)} %bitcast.34, f32[1,1024]{1,0:T(1,128)} %bitcast.40, f32[1,1024]{1,0:T(1,128)} %bitcast.46, f32[1,1024]{1,0:T(1,128)} %bitcast.52, f32[2,256,128]{2,1,0:T(8,128)} %broadcast_select_fusion.step_ref, ...), custom_call_target="tpu_custom_call" | custom-call | flops 8321499136 | bytes 8388608 | tf_op jit(solution)/shard_map/heads/pallas_call | solution.py:202
  77.2 2.6 collective-permute-start.9
  80.7 2.5 collective-permute-start.12
  83.7 15.1 %collective-permute-done.9.refs_6_.refs_15_ = bf16[256,1536]{1,0:T(8,128)(2,1)S(1)} collective-permute-done((bf16[256,1536]{1,0:T(8,128)(2,1)}, bf16[256,1536]{1,0:T(8,128)(2,1)S(1)}, u32[]{:S(2)}, u32[]{:S(2)}) %collective-permute-start.9) | collective-permute-done | bytes 786464 | tf_op jit(solution)/shard_map/ppermute | solution.py:344
  98.8 16.9 %collective-permute-done.8.refs_5_.refs_14_ = bf16[256,1536]{1,0:T(8,128)(2,1)S(1)} collective-permute-done((bf16[256,1536]{1,0:T(8,128)(2,1)}, bf16[256,1536]{1,0:T(8,128)(2,1)S(1)}, u32[]{:S(2)}, u32[]{:S(2)}) %collective-permute-start.8) | collective-permute-done | bytes 786464 | tf_op jit(solution)/shard_map/ppermute | solution.py:344
  116.2 13.4 %collective-permute-done.12.refs_19_.refs_29_ = bf16[256,1536]{1,0:T(8,128)(2,1)S(1)} collective-permute-done((bf16[256,1536]{1,0:T(8,128)(2,1)}, bf16[256,1536]{1,0:T(8,128)(2,1)S(1)}, u32[]{:S(2)}, u32[]{:S(2)}) %collective-permute-start.12) | collective-permute-done | bytes 786464 | tf_op jit(solution)/shard_map/ppermute | solution.py:344
  131.7 14.7 %collective-permute-done.11.refs_18_.refs_28_ = bf16[256,1536]{1,0:T(8,128)(2,1)} collective-permute-done((bf16[256,1536]{1,0:T(8,128)(2,1)}, bf16[256,1536]{1,0:T(8,128)(2,1)}, u32[]{:S(2)}, u32[]{:S(2)}) %collective-permute-start.11) | collective-permute-done | bytes 786464 | tf_op jit(solution)/shard_map/ppermute | solution.py:344
  148.0 38.6 %heads.5 = (bf16[3,2048,512]{2,1,0:T(8,128)(2,1)}, f32[3,256,512]{2,1,0:T(8,128)}) custom-call(s32[10]{0:T(128)} %stack.68.meta_ref, f32[1,1024]{1,0:T(1,128)} %bitcast.35, f32[1,1024]{1,0:T(1,128)} %bitcast.41, f32[1,1024]{1,0:T(1,128)} %bitcast.47, f32[1,1024]{1,0:T(1,128)} %bitcast.53, f32[2,256,128]{2,1,0:T(8,128)} %broadcast_select_fusion.step_ref, ...), custom_call_target="tpu_custom_call" | custom-call | flops 24964497408 | bytes 25165824 | tf_op jit(solution)/shard_map/heads/pallas_call | solution.py:202
  193.3 17.7 %heads.7 = (bf16[1,2048,512]{2,1,0:T(8,128)(2,1)}, f32[1,256,512]{2,1,0:T(8,128)}) custom-call(s32[10]{0:T(128)} %stack.68.meta_ref, f32[1,1024]{1,0:T(1,128)} %bitcast.36, f32[1,1024]{1,0:T(1,128)} %bitcast.42, f32[1,1024]{1,0:T(1,128)} %bitcast.48, f32[1,1024]{1,0:T(1,128)} %bitcast.54, f32[2,256,128]{2,1,0:T(8,128)} %broadcast_select_fusion.step_ref, ...), custom_call_target="tpu_custom_call" | custom-call | flops 8321499136 | bytes 8388608 | tf_op jit(solution)/shard_map/heads/pallas_call | solution.py:202
  212.5 49.6 %tail.2 = (bf16[8,2048,1024]{2,1,0:T(8,128)(2,1)}, bf16[1,2048,1024]{2,1,0:T(8,128)(2,1)}, f32[1,256,512]{2,1,0:T(8,128)}) custom-call(s32[10]{0:T(128)} %stack.68.meta_ref, f32[1,1024]{1,0:T(1,128)} %bitcast.37, f32[1,1024]{1,0:T(1,128)} %bitcast.43, f32[1,1024]{1,0:T(1,128)} %bitcast.49, f32[1,1024]{1,0:T(1,128)} %bitcast.55, ...), custom_call_target="tpu_custom_call" | custom-call | flops 34091302912 | bytes 16777216 | tf_op jit(solution)/shard_map/tail/pallas_call | solution.py:202
  265.0 110.2 %tail.3 = (bf16[8,2048,1024]{2,1,0:T(8,128)(2,1)}, bf16[1,2048,1024]{2,1,0:T(8,128)(2,1)}, bf16[1,2048,1024]{2,1,0:T(8,128)(2,1)}, f32[2,256,512]{2,1,0:T(8,128)}, f32[2,256,512]{2,1,0:T(8,128)}) custom-call(s32[10]{0:T(128)} %stack.68.meta_ref, f32[1,1024]{1,0:T(1,128)} %bitcast.38, f32[1,1024]{1,0:T(1,128)} %bitcast.44, ...), custom_call_target="tpu_custom_call", output_to_operand_aliasing={{0}: (40, {})} | custom-call | flops 84825604096 | bytes 33554432 | tf_op jit(solution)/shard_map/tail/pallas_call | solution.py:202
  376.7 13.4 %collective-permute-done.34.refs_6_ = f32[1,256,512]{2,1,0:T(8,128)S(1)} collective-permute-done((f32[1,256,512]{2,1,0:T(8,128)S(1)}, f32[1,256,512]{2,1,0:T(8,128)S(1)}, u32[]{:S(2)}, u32[]{:S(2)}) %collective-permute-start.34) | collective-permute-done | bytes 524320 | tf_op jit(solution)/shard_map/ppermute | solution.py:379
  390.1 6.8 %collective-permute-done.33.refs_3_.refs_4_.refs_5_ = f32[3,256,512]{2,1,0:T(8,128)S(1)} collective-permute-done((f32[3,256,512]{2,1,0:T(8,128)}, f32[3,256,512]{2,1,0:T(8,128)S(1)}, u32[]{:S(2)}, u32[]{:S(2)}) %collective-permute-start.33) | collective-permute-done | bytes 1572896 | tf_op jit(solution)/shard_map/ppermute | solution.py:371
  397.6 13.4 %collective-permute-done.35.refs_7_ = f32[1,256,512]{2,1,0:T(8,128)S(1)} collective-permute-done((f32[1,256,512]{2,1,0:T(8,128)}, f32[1,256,512]{2,1,0:T(8,128)S(1)}, u32[]{:S(2)}, u32[]{:S(2)}) %collective-permute-start.35) | collective-permute-done | bytes 524320 | tf_op jit(solution)/shard_map/ppermute | solution.py:380
  411.0 8.2 %place.4 = (bf16[8,2048,1024]{2,1,0:T(8,128)(2,1)}, f32[8,256,512]{2,1,0:T(8,128)}) custom-call(s32[8]{0:T(128)S(1)} %stack.73.ids_ref, bf16[1,2048,1024]{2,1,0:T(8,128)(2,1)} %collective-permute-done.32.refs_0_, bf16[1,2048,1024]{2,1,0:T(8,128)(2,1)} %collective-permute-done.29.refs_1_, ...), custom_call_target="tpu_custom_call", output_to_operand_aliasing={{0}: (9, {}), {1}: (10, {})} | custom-call | tf_op jit(solution)/shard_map/place/pallas_call | solution.py:286
  419.2 3.6 place.5.refs_1_
  422.8 3.6 place.6.refs_1_
  426.4 3.6 place.7
  (121 shorter events, 24.6 us)
Async XLA Ops:
  0.6 80.1 %collective-permute-start.4 = (f32[8,256,512]{2,1,0:T(8,128)}, f32[8,256,512]{2,1,0:T(8,128)}, u32[]{:S(2)}, u32[]{:S(2)}) collective-permute-start(f32[8,256,512]{2,1,0:T(8,128)} %bitcast.27), channel_id=1, source_target_pairs={{0,1},{1,0},{2,3},{3,2},{4,5},{5,4},{6,7},{7,6},{8,9},{9,8},{10,11... | collective-permute-start | bytes 12582920 | tf_op jit(solution)/shard_map/ppermute | solution.py:350
  1.9 77.8 %collective-permute-start.2 = (bf16[1024,512]{1,0:T(8,128)(2,1)}, bf16[1024,512]{1,0:T(8,128)(2,1)S(1)}, u32[]{:S(2)}, u32[]{:S(2)}) collective-permute-start(bf16[1024,512]{1,0:T(8,128)(2,1)} %refs_5_.1), channel_id=1, source_target_pairs={{0,1},{1,0},{2,3},{3,2},{4,5},{5,4},{6,7},{7,6},{8,9},{9,8},{10,11... | collective-permute-start | bytes 3145736 | tf_op jit(solution)/shard_map/ppermute | solution.py:349
  7.9 21.6 %collective-permute-start.6 = (bf16[256,1536]{1,0:T(8,128)(2,1)}, bf16[256,1536]{1,0:T(8,128)(2,1)S(1)}, u32[]{:S(2)}, u32[]{:S(2)}) collective-permute-start(bf16[256,1536]{1,0:T(8,128)(2,1)} %get-tuple-element.64), channel_id=1, source_target_pairs={{0,2},{1,3},{2,0},{3,1},{4,6},{5,7},{6,4},{7,5},{8,10},{9,11},{10,... | collective-permute-start | bytes 2359304 | tf_op jit(solution)/shard_map/ppermute | solution.py:352
  16.4 63.8 %collective-permute-start.3 = (bf16[1024,512]{1,0:T(8,128)(2,1)S(1)}, bf16[1024,512]{1,0:T(8,128)(2,1)S(1)}, u32[]{:S(2)}, u32[]{:S(2)}) collective-permute-start(bf16[1024,512]{1,0:T(8,128)(2,1)S(1)} %copy-done.1), channel_id=1, source_target_pairs={{0,1},{1,0},{2,3},{3,2},{4,5},{5,4},{6,7},{7,6},{8,9},{9,8},{10,11... | collective-permute-start | bytes 3145736 | tf_op jit(solution)/shard_map/ppermute | solution.py:349
  16.5 60.7 %collective-permute-start.5 = (bf16[256,1536]{1,0:T(8,128)(2,1)}, bf16[256,1536]{1,0:T(8,128)(2,1)}, u32[]{:S(2)}, u32[]{:S(2)}) collective-permute-start(bf16[256,1536]{1,0:T(8,128)(2,1)} %get-tuple-element.56), channel_id=1, source_target_pairs={{0,2},{1,3},{2,0},{3,1},{4,6},{5,7},{6,4},{7,5},{8,10},{9,11},{10,... | collective-permute-start | bytes 2359304 | tf_op jit(solution)/shard_map/ppermute | solution.py:353
  29.5 53.7 %collective-permute-start.13 = (f32[2,256,512]{2,1,0:T(8,128)}, f32[2,256,512]{2,1,0:T(8,128)S(1)}, u32[]{:S(2)}, u32[]{:S(2)}) collective-permute-start(f32[2,256,512]{2,1,0:T(8,128)} %get-tuple-element.67), channel_id=1, source_target_pairs={{0,2},{1,3},{2,0},{3,1},{4,6},{5,7},{6,4},{7,5},{8,10},{9,11},{10,... | collective-permute-start | bytes 3145736 | tf_op jit(solution)/shard_map/ppermute | solution.py:354
  77.2 21.6 %collective-permute-start.9 = (bf16[256,1536]{1,0:T(8,128)(2,1)}, bf16[256,1536]{1,0:T(8,128)(2,1)S(1)}, u32[]{:S(2)}, u32[]{:S(2)}) collective-permute-start(bf16[256,1536]{1,0:T(8,128)(2,1)} %copy-done.6), channel_id=1, source_target_pairs={{0,12},{4,8},{8,4},{12,0},{1,13},{5,9},{9,5},{13,1},{2,14},{6,10},... | collective-permute-start | bytes 2359304 | tf_op jit(solution)/shard_map/ppermute | solution.py:344
  79.7 35.9 %collective-permute-start.8 = (bf16[256,1536]{1,0:T(8,128)(2,1)}, bf16[256,1536]{1,0:T(8,128)(2,1)S(1)}, u32[]{:S(2)}, u32[]{:S(2)}) collective-permute-start(bf16[256,1536]{1,0:T(8,128)(2,1)} %copy-done.6), channel_id=1, source_target_pairs={{0,8},{4,12},{8,0},{12,4},{1,9},{5,13},{9,1},{13,5},{2,10},{6,14},... | collective-permute-start | bytes 2359304 | tf_op jit(solution)/shard_map/ppermute | solution.py:344
  80.2 35.5 %collective-permute-start.7 = (bf16[256,1536]{1,0:T(8,128)(2,1)}, bf16[256,1536]{1,0:T(8,128)(2,1)S(1)}, u32[]{:S(2)}, u32[]{:S(2)}) collective-permute-start(bf16[256,1536]{1,0:T(8,128)(2,1)} %copy-done.6), channel_id=1, source_target_pairs={{0,4},{4,0},{8,12},{12,8},{1,5},{5,1},{9,13},{13,9},{2,6},{6,2},{1... | collective-permute-start | bytes 2359304 | tf_op jit(solution)/shard_map/ppermute | solution.py:344
  80.7 48.9 %collective-permute-start.12 = (bf16[256,1536]{1,0:T(8,128)(2,1)}, bf16[256,1536]{1,0:T(8,128)(2,1)S(1)}, u32[]{:S(2)}, u32[]{:S(2)}) collective-permute-start(bf16[256,1536]{1,0:T(8,128)(2,1)} %collective-permute-done.5.refs_16_.refs_26_), channel_id=1, source_target_pairs={{0,12},{4,8},{8,4},{12,0},{1,13},{5,9},{9,5},{13,1},{2,14},{6,10},... | collective-permute-start | bytes 2359304 | tf_op jit(solution)/shard_map/ppermute | solution.py:344
  83.2 63.2 %collective-permute-start.11 = (bf16[256,1536]{1,0:T(8,128)(2,1)}, bf16[256,1536]{1,0:T(8,128)(2,1)}, u32[]{:S(2)}, u32[]{:S(2)}) collective-permute-start(bf16[256,1536]{1,0:T(8,128)(2,1)} %collective-permute-done.5.refs_16_.refs_26_), channel_id=1, source_target_pairs={{0,8},{4,12},{8,0},{12,4},{1,9},{5,13},{9,1},{13,5},{2,10},{6,14},... | collective-permute-start | bytes 2359304 | tf_op jit(solution)/shard_map/ppermute | solution.py:344
  98.8 87.9 %collective-permute-start.22 = (bf16[512,1024]{1,0:T(8,128)(2,1)S(1)}, bf16[512,1024]{1,0:T(8,128)(2,1)}, u32[]{:S(2)}, u32[]{:S(2)}) collective-permute-start(bf16[512,1024]{1,0:T(8,128)(2,1)S(1)} %copy-done.5), channel_id=1, source_target_pairs={{0,1},{1,0},{2,3},{3,2},{4,5},{5,4},{6,7},{7,6},{8,9},{9,8},{10,11... | collective-permute-start | bytes 3145736 | tf_op jit(solution)/shard_map/ppermute | solution.py:356
  115.7 71.5 %collective-permute-start.24 = (bf16[1024,512]{1,0:T(8,128)(2,1)}, bf16[1024,512]{1,0:T(8,128)(2,1)}, u32[]{:S(2)}, u32[]{:S(2)}) collective-permute-start(bf16[1024,512]{1,0:T(8,128)(2,1)} %refs_22_.1), channel_id=1, source_target_pairs={{0,1},{1,0},{2,3},{3,2},{4,5},{5,4},{6,7},{7,6},{8,9},{9,8},{10,11... | collective-permute-start | bytes 3145736 | tf_op jit(solution)/shard_map/ppermute | solution.py:356
  115.7 71.5 %collective-permute-start.23 = (bf16[512,1024]{1,0:T(8,128)(2,1)}, bf16[512,1024]{1,0:T(8,128)(2,1)}, u32[]{:S(2)}, u32[]{:S(2)}) collective-permute-start(bf16[512,1024]{1,0:T(8,128)(2,1)} %refs_21_.1), channel_id=1, source_target_pairs={{0,1},{1,0},{2,3},{3,2},{4,5},{5,4},{6,7},{7,6},{8,9},{9,8},{10,11... | collective-permute-start | bytes 3145736 | tf_op jit(solution)/shard_map/ppermute | solution.py:356
  130.5 57.2 %collective-permute-start.26 = (f32[4,256,512]{2,1,0:T(8,128)}, f32[4,256,512]{2,1,0:T(8,128)}, u32[]{:S(2)}, u32[]{:S(2)}) collective-permute-start(f32[4,256,512]{2,1,0:T(8,128)} %get-tuple-element.78), channel_id=1, source_target_pairs={{0,2},{1,3},{2,0},{3,1},{4,6},{5,7},{6,4},{7,5},{8,10},{9,11},{10,... | collective-permute-start | bytes 6291464 | tf_op jit(solution)/shard_map/ppermute | solution.py:355
  146.4 40.2 %collective-permute-start.10 = (bf16[256,1536]{1,0:T(8,128)(2,1)}, bf16[256,1536]{1,0:T(8,128)(2,1)}, u32[]{:S(2)}, u32[]{:S(2)}) collective-permute-start(bf16[256,1536]{1,0:T(8,128)(2,1)} %collective-permute-done.5.refs_16_.refs_26_), channel_id=1, source_target_pairs={{0,4},{4,0},{8,12},{12,8},{1,5},{5,1},{9,13},{13,9},{2,6},{6,2},{1... | collective-permute-start | bytes 2359304 | tf_op jit(solution)/shard_map/ppermute | solution.py:344
  187.7 23.4 %collective-permute-start.25 = (f32[2,256,512]{2,1,0:T(8,128)S(1)}, f32[2,256,512]{2,1,0:T(8,128)S(1)}, u32[]{:S(2)}, u32[]{:S(2)}) collective-permute-start(f32[2,256,512]{2,1,0:T(8,128)S(1)} %collective-permute-done.13.refs_2_), channel_id=1, source_target_pairs={{0,1},{1,0},{2,3},{3,2},{4,5},{5,4},{6,7},{7,6},{8,9},{9,8},{10,11... | collective-permute-start | bytes 3145736 | tf_op jit(solution)/shard_map/ppermute | solution.py:370
  188.9 22.1 %collective-permute-start.18 = (bf16[256,1536]{1,0:T(8,128)(2,1)}, bf16[256,1536]{1,0:T(8,128)(2,1)S(1)}, u32[]{:S(2)}, u32[]{:S(2)}) collective-permute-start(bf16[256,1536]{1,0:T(8,128)(2,1)} %collective-permute-done.5.refs_16_.refs_26_), channel_id=1, source_target_pairs={{0,1},{1,0},{2,3},{3,2},{4,5},{5,4},{6,7},{7,6},{8,9},{9,8},{10,11... | collective-permute-start | bytes 2359304 | tf_op jit(solution)/shard_map/ppermute | solution.py:370
  211.1 52.6 %collective-permute-start.27 = (f32[4,256,512]{2,1,0:T(8,128)}, f32[4,256,512]{2,1,0:T(8,128)S(1)}, u32[]{:S(2)}, u32[]{:S(2)}) collective-permute-start(f32[4,256,512]{2,1,0:T(8,128)} %collective-permute-done.26.refs_4_.refs_5_), channel_id=1, source_target_pairs={{0,1},{1,0},{2,3},{3,2},{4,5},{5,4},{6,7},{7,6},{8,9},{9,8},{10,11... | collective-permute-start | bytes 6291464 | tf_op jit(solution)/shard_map/ppermute | solution.py:375
  262.1 148.9 %collective-permute-start.32 = (bf16[1,2048,1024]{2,1,0:T(8,128)(2,1)}, bf16[1,2048,1024]{2,1,0:T(8,128)(2,1)}, u32[]{:S(2)}, u32[]{:S(2)}) collective-permute-start(bf16[1,2048,1024]{2,1,0:T(8,128)(2,1)} %get-tuple-element.98), channel_id=1, source_target_pairs={{0,1},{1,0},{2,3},{3,2},{4,5},{5,4},{6,7},{7,6},{8,9},{9,8},{10,11... | collective-permute-start | bytes 12582920 | tf_op jit(solution)/shard_map/ppermute | solution.py:378
  262.5 112.8 %collective-permute-start.29 = (bf16[1,2048,1024]{2,1,0:T(8,128)(2,1)}, bf16[1,2048,1024]{2,1,0:T(8,128)(2,1)}, u32[]{:S(2)}, u32[]{:S(2)}) collective-permute-start(bf16[1,2048,1024]{2,1,0:T(8,128)(2,1)} %get-tuple-element.98), channel_id=1, source_target_pairs={{0,2},{1,3},{2,0},{3,1},{4,6},{5,7},{6,4},{7,5},{8,10},{9,11},{10,... | collective-permute-start | bytes 12582920 | tf_op jit(solution)/shard_map/ppermute | solution.py:377
  375.2 44.0 %collective-permute-start.31 = (bf16[1,2048,1024]{2,1,0:T(8,128)(2,1)}, bf16[1,2048,1024]{2,1,0:T(8,128)(2,1)}, u32[]{:S(2)}, u32[]{:S(2)}) collective-permute-start(bf16[1,2048,1024]{2,1,0:T(8,128)(2,1)} %get-tuple-element.99), channel_id=1, source_target_pairs={{0,1},{1,0},{2,3},{3,2},{4,5},{5,4},{6,7},{7,6},{8,9},{9,8},{10,11... | collective-permute-start | bytes 12582920 | tf_op jit(solution)/shard_map/ppermute | solution.py:383
  375.3 47.5 %collective-permute-start.30 = (bf16[1,2048,1024]{2,1,0:T(8,128)(2,1)}, bf16[1,2048,1024]{2,1,0:T(8,128)(2,1)}, u32[]{:S(2)}, u32[]{:S(2)}) collective-permute-start(bf16[1,2048,1024]{2,1,0:T(8,128)(2,1)} %collective-permute-done.29.refs_1_), channel_id=1, source_target_pairs={{0,1},{1,0},{2,3},{3,2},{4,5},{5,4},{6,7},{7,6},{8,9},{9,8},{10,11... | collective-permute-start | bytes 12582920 | tf_op jit(solution)/shard_map/ppermute | solution.py:384
  375.8 50.6 %collective-permute-start.28 = (bf16[1,2048,1024]{2,1,0:T(8,128)(2,1)}, bf16[1,2048,1024]{2,1,0:T(8,128)(2,1)}, u32[]{:S(2)}, u32[]{:S(2)}) collective-permute-start(bf16[1,2048,1024]{2,1,0:T(8,128)(2,1)} %get-tuple-element.97), channel_id=1, source_target_pairs={{0,1},{1,0},{2,3},{3,2},{4,5},{5,4},{6,7},{7,6},{8,9},{9,8},{10,11... | collective-permute-start | bytes 12582920 | tf_op jit(solution)/shard_map/ppermute | solution.py:386
  (36 other events, 937.9 us)

commit v7 on v6

--- a/solution.py
+++ b/solution.py
@@ -85,16 +85,17 @@
     return out
 
 
-def kernel_body(n_seqs, n_sub, heads, n_z, pieces, with_whole, meta_ref, gain1, bias1, gain2, bias2, step_ref, *refs):
+def kernel_body(n_seqs, n_sub, has_h, heads, n_z, pieces, with_whole, meta_ref, gain1, bias1, gain2, bias2, step_ref, *refs):
     it = iter(refs)
 
     def take(n):
         return [next(it) for _ in range(n)]
 
-    x_refs, base_refs, s_refs, z_refs = take(n_seqs), take(n_seqs), [take(n_seqs) for _ in heads], [take(n_seqs) for _ in range(n_z)]
+    x_refs, h_refs = take(n_seqs if n_z or not has_h else 0), take(n_seqs if has_h else 0)
+    base_refs, s_refs, z_refs = take(n_seqs), [take(n_seqs) for _ in heads], [take(n_seqs) for _ in range(n_z)]
     sources = take(len(pieces))
     take(with_whole)
-    outs = take(1 + n_seqs if n_z else 1)
+    outs = take(1 + n_seqs if n_z else 1 if has_h else 2)
     state_refs = take(len(heads))
     inner_ref, rows_ref, sem = take(3)
     weights = list(it)
@@ -118,13 +119,18 @@
             copy.wait()
 
     cos_b, sin_b = step_ref[0], step_ref[1]
-    normed, tables = [], []
-    for x_ref, base_ref in zip(x_refs, base_refs):
-        normed.append(layer_norm(x_ref[0].astype(F32), gain1[...], bias1[...]).astype(BF16))
+    tables = []
+    for base_ref in base_refs:
         for j in range(n_sub):
             at = pl.multiple_of((pl.program_id(0) * n_sub + j) * 8, 8)
             cos_a, sin_a = base_ref[0, pl.ds(at, 1), :], base_ref[0, pl.ds(at + 1, 1), :]
             tables.append((cos_a * cos_b - sin_a * sin_b, sin_a * cos_b + cos_a * sin_b))
+    if has_h:
+        normed = [h_ref[0] for h_ref in h_refs]
+    else:
+        normed = [layer_norm(x_ref[0].astype(F32), gain1[...], bias1[...]).astype(BF16) for x_ref in x_refs]
+        for b, h in enumerate(normed):
+            outs[1][b] = h
     hs = [h[j * TILE:(j + 1) * TILE] for h in normed for j in range(n_sub)]
     mixed = [head_blocks(hs, weights[i], state_refs[i], inner_ref[i], rows_ref.at[i], tables) for i in range(len(heads))]
     rows = n_sub * TILE
@@ -153,7 +159,7 @@
     return blocks[0] if len(blocks) == 1 else jnp.concatenate(blocks, axis=0)
 
 
-def run(meta, common, seqs, state_rows, heads, states, weights, zs=(), whole=None, pair=False, n_sub=1):
+def run(meta, common, seqs, state_rows, heads, states, weights, zs=(), whole=None, pair=False, n_sub=1, hs=()):
     x, norms, base, step = common
     tile = n_sub * TILE
     n, chunk_len, d_model = len(seqs), x.shape[1], x.shape[2]
@@ -171,8 +177,12 @@
     def resident(arr):
         return pl.BlockSpec(arr.shape, lambda t, m: (0,) * arr.ndim, pipeline_mode=pl.Buffered(1))
 
-    specs = [resident(arr) for arr in (*norms, step)] + [token_spec(at) for at in seqs] + [row_spec(base.shape[1:], at) for at in seqs]
-    args = [*norms, step] + [x] * n + [base] * n
+    specs, args = [resident(arr) for arr in (*norms, step)], [*norms, step]
+    if zs or not hs:
+        specs += [token_spec(at) for at in seqs]
+        args += [x] * n
+    specs += [tile_of(d_model, 1, at) for _, at in hs] + [row_spec(base.shape[1:], at) for at in seqs]
+    args += [h for h, _ in hs] + [base] * n
     for state in states:
         specs += [row_spec(state.shape[1:], at) for at in state_rows]
         args += [state] * n
@@ -194,13 +204,13 @@
         whole_spec = token_spec(seqs[0]) if n == 1 else pl.BlockSpec((n, tile, d_model), lambda t, m: (m[PAIR], t, 0))
         outs = [(whole_spec, jax.ShapeDtypeStruct(x.shape, BF16))] + [(tile_of(d_model), jax.ShapeDtypeStruct((1, chunk_len, d_model), BF16))] * n
     else:
-        outs = [(tile_of(val_dim, n), jax.ShapeDtypeStruct((n, chunk_len, val_dim), BF16))]
+        outs = [(tile_of(width, n), jax.ShapeDtypeStruct((n, chunk_len, width), BF16)) for width in ((val_dim,) if hs else (val_dim, d_model))]
     state_out = pl.BlockSpec((n, key_dim, val_dim), lambda t, m: (m[PAIR] if pair else 0, 0, 0))
     outs += [(state_out, jax.ShapeDtypeStruct((x.shape[0] if pair else n, key_dim, val_dim), F32))] * len(heads)
     flops = n * len(heads) * 2 * (d_model * (2 * key_dim + 2 * val_dim) + TILE * (key_dim + val_dim) + 2 * key_dim * val_dim)
     flops += n * 24 * d_model * val_dim if zs else 0
     return pl.pallas_call(
-        functools.partial(kernel_body, n, n_sub, tuple(heads), len(zs), tuple(pieces), whole is not None),
+        functools.partial(kernel_body, n, n_sub, bool(hs), tuple(heads), len(zs), tuple(pieces), whole is not None),
         grid_spec=pltpu.PrefetchScalarGridSpec(
             num_scalar_prefetch=1, grid=(chunk_len // tile,), in_specs=specs, out_specs=[spec for spec, _ in outs],
             scratch_shapes=[pltpu.VMEM((len(heads), TILE, TILE), F32), pltpu.VMEM((len(heads), 3, TILE, 128), F32), pltpu.SemaphoreType.DMA((sum(map(len, pieces)),))]
@@ -359,27 +369,28 @@
         common = (x_in, norms, *rope_tables(start_pos, chunk_len, key_dim))
         all_seqs, pair_seqs, one = (SEQ, SEQ + 1, SEQ + 2), (SEQ + 1, SEQ + 2), (SEQ,)
 
-        z_own_single, new_own_single = run(meta, common, one, one, (0,), (own,), head_places(head_w))
+        z_own_single, h_single, new_own_single = run(meta, common, one, one, (0,), (own,), head_places(head_w), n_sub=2)
         z_own_single, wa_part = lax.optimization_barrier((z_own_single, wa_part))
         wa_quarters = gather(wa_part)
-        z_own, new_states = run(meta, common, pair_seqs, pair_seqs, (0,), (own,), head_places(head_w), pair=True)
+        z_own, h_twice, new_states = run(meta, common, pair_seqs, pair_seqs, (0,), (own,), head_places(head_w), pair=True)
         z_own, wa_core, s_core, wb_part = lax.optimization_barrier((z_own, wa_core, s_core, wb_part))
         wb_quarters = gather(wb_part)
-        z_core, new_core = run(meta, common, all_seqs, all_seqs, (1,), (s_core,), head_places(wa_core))
+        hs_single, hs_twice = ((h_single, 0),), ((h_twice, 0), (h_twice, 1))
+        z_core, new_core = run(meta, common, all_seqs, all_seqs, (1,), (s_core,), head_places(wa_core), hs=hs_single + hs_twice)
         z_core, wa_quarters, wb_quarters, su_chip = lax.optimization_barrier((z_core, wa_quarters, wb_quarters, su_chip))
         wa_far, wb_far, su_far = [to_core(w) for w in wa_quarters], [to_core(w) for w in wb_quarters], to_core(su_chip)
         got_core = to_core(new_core)
 
-        z_chip, new_chip = run(meta, common, one, (STATE_SINGLE,), (2,), (su_chip,), heads_gathered(wa_quarters))
+        z_chip, new_chip = run(meta, common, one, (STATE_SINGLE,), (2,), (su_chip,), heads_gathered(wa_quarters), n_sub=2, hs=hs_single)
         z_chip, wa_far, wb_far, wb_core, su_far, st_chip = lax.optimization_barrier((z_chip, wa_far, wb_far, wb_core, su_far, st_chip))
         st_far = to_core(st_chip)
-        whole, x_single, new_far = run(meta, common, one, (STATE_SINGLE,), (3,), (su_far,), heads_gathered(wa_far) + mlp(1), ((z_own_single, 0), (z_core, 0), (z_chip, 0)), n_sub=2)
+        whole, x_single, new_far = run(meta, common, one, (STATE_SINGLE,), (3,), (su_far,), heads_gathered(wa_far) + mlp(1), ((z_own_single, 0), (z_core, 0), (z_chip, 0)), n_sub=2, hs=hs_single)
         x_single_chip = to_chip(x_single)
         x_single_core = to_core(x_single)
         got_chip = to_chip(new_chip)
         got_far = to_far(new_far)
         whole, x_a, x_b, _, _ = run(meta, common, pair_seqs, (STATE_TWICE, STATE_TWICE + 1), (2, 3), (st_chip, st_far), heads_gathered(wa_quarters) + heads_gathered(wa_far, 1) + mlp(2),
-                                    ((z_own, 0), (z_core, 1)), whole)
+                                    ((z_own, 0), (z_core, 1)), whole, hs=hs_twice)
         x_a_core = to_core(x_a)
         x_single_far = to_core(x_single_chip)
 
@@ -387,14 +398,14 @@
 
         single_o, twice_o = 2 * chip + other, 4 + 2 * other
         far_c, far_o = 2 * (1 - chip) + core, 2 * (1 - chip) + other
-        ids = jnp.stack([single_o, far_c, single, single_o, twice_o, twice_o + 1, far_c, far_o, twice_o, far_o, twice_o + 1]).astype(jnp.int32)
+        ids = jnp.stack([single_o, far_c, single, single_o, twice_o, twice_o + 1, far_c, twice_o, far_o, twice_o + 1, far_o]).astype(jnp.int32)
         cuts = chunk_len // TILE
         near = [(x_single_core, 0, 0, cuts), (x_single_chip, 0, 0, cuts)]
-        near += [(arr, at, 1, 1) for arr, at in ((new_own_single, 0), (got_core, 0), (got_core, 1), (got_core, 2), (got_chip, 0), (got_far, 0))]
-        whole, new_states = place(ids[:8], near, (whole, new_states))
-        whole, = place(ids[8:9], [(x_a_core, 0, 0, cuts)], (whole,))
-        whole, = place(ids[9:10], [(x_single_far, 0, 0, cuts)], (whole,))
-        whole, = place(ids[10:], [(x_b_core, 0, 0, cuts)], (whole,))
+        near += [(arr, at, 1, 1) for arr, at in ((new_own_single, 0), (got_core, 0), (got_core, 1), (got_core, 2), (got_chip, 0))]
+        whole, new_states = place(ids[:7], near, (whole, new_states))
+        whole, = place(ids[7:8], [(x_a_core, 0, 0, cuts)], (whole,))
+        whole, = place(ids[8:9], [(x_single_far, 0, 0, cuts)], (whole,))
+        whole, new_states = place(ids[9:], [(x_b_core, 0, 0, cuts), (got_far, 0, 1, 1)], (whole, new_states))
         return whole, new_states[:, None]
 
     in_specs = (P("dp", None, None), P("dp"), P("dp", "tp", None, None), P(), P(), P(None, "tp"), P(None, "tp"), P(None, "tp"), P(None, "tp"), P("tp", None), P(), P(), P(None, "tp"), P("tp", None))

time: 431 us -> 407 us (0.944)
  waiting for transfers between devices: 111 us -> 100 us
  Pallas kernels: 286 us -> 276 us
    ppermute x1, waiting for transfers between devices: 13.4 us -> 0.01 us  [local_layer(): got_far = to_far(new_far)]
    pallas_call x6, Pallas kernels: 262 us -> 251 us  [run(): pl.pallas_call(functools.partial(kernel_body, n, n_sub, bool(hs), tuple(h...]
  transfers between devices with their start and end apart: 36 -> 36, of which waited for: 12 -> 11; matrix products, arithmetic and copies ran while one was open for 1% -> 1% of each run, Pallas kernels for 66% -> 67%
where the time goes in v7:
time: 407 us
  Pallas kernels  276 us (68%)
  waiting for transfers between devices  100 us (25%)
  starting transfers between devices  21.8 us (5%)
  local copies, waits for them, and re-layouts  5 us (1%)
    pallas_call x6, Pallas kernels, run(): pl.pallas_call(functools.partial(kernel_body, n, n_sub, bool(hs), tuple(h...  251 us
    ppermute x6, waiting for transfers between devices, gather(): return [part] + [swap('dp', flip)(part) for flip in range(1, n_dp)]  60.4 us
    pallas_call x4, Pallas kernels, place(): pl.pallas_call(functools.partial(place_kernel, tuple((block[1:] for block...  19.5 us
    ppermute x1, waiting for transfers between devices, local_layer(): wa_part = to_chip(wa_part)  16 us
    ppermute x1, waiting for transfers between devices, local_layer(): got_chip = to_chip(new_chip)  12.8 us
  transfers between devices with their start and end apart: 36, of which 11 were waited for; matrix products, arithmetic and copies ran while one was open for 1% of the time, Pallas kernels for 67%

profile of v7, /device:TPU:0, one launch (start us, length us, event | category | flops | bytes accessed | tf_op | source)
XLA Modules:
  0.0 407.0 jit_solution(15529209118920292563)
XLA Ops:
  2.6 5.4 %parts.1 = (bf16[256,1536]{1,0:T(8,128)(2,1)}, bf16[256,1536]{1,0:T(8,128)(2,1)}, f32[2,256,512]{2,1,0:T(8,128)}, f32[4,256,512]{2,1,0:T(8,128)}) custom-call(s32[10]{0:T(128)} %stack.72.meta_ref, bf16[1024,256]{1,0:T(8,128)(2,1)} %w_q.1, bf16[1024,256]{1,0:T(8,128)(2,1)} %w_k.1, bf16[1024,512]{1,0:T(8,128)(2,1)} %w_v.1, bf16[1024,512]{1,0:T(8,128)(2,1)} %w_g.1, ...), custom_call_target="tpu_custom_call" | custom-call | tf_op jit(solution)/shard_map/parts/pallas_call | solution.py:265
  8.0 3.0 collective-permute-start.6
  13.7 16.0 %collective-permute-done.6.refs_3_.refs_14_ = bf16[256,1536]{1,0:T(8,128)(2,1)} collective-permute-done((bf16[256,1536]{1,0:T(8,128)(2,1)}, bf16[256,1536]{1,0:T(8,128)(2,1)}, u32[]{:S(2)}, u32[]{:S(2)}) %collective-permute-start.6) | collective-permute-done | bytes 786464 | tf_op jit(solution)/shard_map/ppermute | solution.py:362
  29.7 2.0 collective-permute-start.13
  31.7 28.5 %heads.4 = (bf16[2,2048,512]{2,1,0:T(8,128)(2,1)}, bf16[2,2048,1024]{2,1,0:T(8,128)(2,1)}, f32[8,256,512]{2,1,0:T(8,128)}) custom-call(s32[10]{0:T(128)} %stack.72.meta_ref, f32[1,1024]{1,0:T(1,128)} %bitcast.33, f32[1,1024]{1,0:T(1,128)} %bitcast.39, f32[1,1024]{1,0:T(1,128)} %bitcast.45, f32[1,1024]{1,0:T(1,128)} %bitcast.51, ...), custom_call_target="tpu_custom_call" | custom-call | flops 16642998272 | bytes 16777216 | tf_op jit(solution)/shard_map/heads/pallas_call | solution.py:212
  60.3 16.5 %heads.5 = (bf16[1,2048,512]{2,1,0:T(8,128)(2,1)}, bf16[1,2048,1024]{2,1,0:T(8,128)(2,1)}, f32[1,256,512]{2,1,0:T(8,128)}) custom-call(s32[10]{0:T(128)} %stack.72.meta_ref, f32[1,1024]{1,0:T(1,128)} %bitcast.34, f32[1,1024]{1,0:T(1,128)} %bitcast.40, f32[1,1024]{1,0:T(1,128)} %bitcast.46, f32[1,1024]{1,0:T(1,128)} %bitcast.52, ...), custom_call_target="tpu_custom_call" | custom-call | flops 8321499136 | bytes 8388608 | tf_op jit(solution)/shard_map/heads/pallas_call | solution.py:212
  76.8 2.6 collective-permute-start.9
  80.4 2.5 collective-permute-start.12
  83.3 15.2 %collective-permute-done.9.refs_6_.refs_17_ = bf16[256,1536]{1,0:T(8,128)(2,1)} collective-permute-done((bf16[256,1536]{1,0:T(8,128)(2,1)}, bf16[256,1536]{1,0:T(8,128)(2,1)}, u32[]{:S(2)}, u32[]{:S(2)}) %collective-permute-start.9) | collective-permute-done | bytes 786464 | tf_op jit(solution)/shard_map/ppermute | solution.py:354
  98.5 16.8 %collective-permute-done.8.refs_5_.refs_16_ = bf16[256,1536]{1,0:T(8,128)(2,1)S(1)} collective-permute-done((bf16[256,1536]{1,0:T(8,128)(2,1)}, bf16[256,1536]{1,0:T(8,128)(2,1)S(1)}, u32[]{:S(2)}, u32[]{:S(2)}) %collective-permute-start.8) | collective-permute-done | bytes 786464 | tf_op jit(solution)/shard_map/ppermute | solution.py:354
  116.2 13.0 %collective-permute-done.12.refs_20_.refs_31_ = bf16[256,1536]{1,0:T(8,128)(2,1)S(1)} collective-permute-done((bf16[256,1536]{1,0:T(8,128)(2,1)}, bf16[256,1536]{1,0:T(8,128)(2,1)S(1)}, u32[]{:S(2)}, u32[]{:S(2)}) %collective-permute-start.12) | collective-permute-done | bytes 786464 | tf_op jit(solution)/shard_map/ppermute | solution.py:354
  130.7 15.4 %collective-permute-done.11.refs_19_.refs_30_ = bf16[256,1536]{1,0:T(8,128)(2,1)} collective-permute-done((bf16[256,1536]{1,0:T(8,128)(2,1)}, bf16[256,1536]{1,0:T(8,128)(2,1)}, u32[]{:S(2)}, u32[]{:S(2)}) %collective-permute-start.11) | collective-permute-done | bytes 786464 | tf_op jit(solution)/shard_map/ppermute | solution.py:354
  146.1 1.5 collective-permute-start.10
  147.6 34.6 %heads.6 = (bf16[3,2048,512]{2,1,0:T(8,128)(2,1)}, f32[3,256,512]{2,1,0:T(8,128)}) custom-call(s32[10]{0:T(128)} %stack.72.meta_ref, f32[1,1024]{1,0:T(1,128)} %bitcast.35, f32[1,1024]{1,0:T(1,128)} %bitcast.41, f32[1,1024]{1,0:T(1,128)} %bitcast.47, f32[1,1024]{1,0:T(1,128)} %bitcast.53, f32[2,256,128]{2,1,0:T(8,128)} %broadcast_select_fusion.step_ref, ...), custom_call_target="tpu_custom_call" | custom-call | flops 24964497408 | bytes 25165824 | tf_op jit(solution)/shard_map/heads/pallas_call | solution.py:212
  188.4 14.9 %heads.7 = (bf16[1,2048,512]{2,1,0:T(8,128)(2,1)}, f32[1,256,512]{2,1,0:T(8,128)}) custom-call(s32[10]{0:T(128)} %stack.72.meta_ref, f32[1,1024]{1,0:T(1,128)} %bitcast.36, f32[1,1024]{1,0:T(1,128)} %bitcast.42, f32[1,1024]{1,0:T(1,128)} %bitcast.48, f32[1,1024]{1,0:T(1,128)} %bitcast.54, f32[2,256,128]{2,1,0:T(8,128)} %broadcast_select_fusion.step_ref, ...), custom_call_target="tpu_custom_call" | custom-call | flops 8321499136 | bytes 8388608 | tf_op jit(solution)/shard_map/heads/pallas_call | solution.py:212
  205.3 48.6 %tail.2 = (bf16[8,2048,1024]{2,1,0:T(8,128)(2,1)}, bf16[1,2048,1024]{2,1,0:T(8,128)(2,1)}, f32[1,256,512]{2,1,0:T(8,128)}) custom-call(s32[10]{0:T(128)} %stack.72.meta_ref, f32[1,1024]{1,0:T(1,128)} %bitcast.37, f32[1,1024]{1,0:T(1,128)} %bitcast.43, f32[1,1024]{1,0:T(1,128)} %bitcast.49, f32[1,1024]{1,0:T(1,128)} %bitcast.55, ...), custom_call_target="tpu_custom_call" | custom-call | flops 34091302912 | bytes 16777216 | tf_op jit(solution)/shard_map/tail/pallas_call | solution.py:212
  256.2 108.1 %tail.3 = (bf16[8,2048,1024]{2,1,0:T(8,128)(2,1)}, bf16[1,2048,1024]{2,1,0:T(8,128)(2,1)}, bf16[1,2048,1024]{2,1,0:T(8,128)(2,1)}, f32[2,256,512]{2,1,0:T(8,128)}, f32[2,256,512]{2,1,0:T(8,128)}) custom-call(s32[10]{0:T(128)} %stack.72.meta_ref, f32[1,1024]{1,0:T(1,128)} %bitcast.38, f32[1,1024]{1,0:T(1,128)} %bitcast.44, ...), custom_call_target="tpu_custom_call", output_to_operand_aliasing={{0}: (42, {})} | custom-call | flops 84825604096 | bytes 33554432 | tf_op jit(solution)/shard_map/tail/pallas_call | solution.py:212
  364.9 1.5 collective-permute-start.35
  366.4 12.8 %collective-permute-done.35.refs_6_ = f32[1,256,512]{2,1,0:T(8,128)S(1)} collective-permute-done((f32[1,256,512]{2,1,0:T(8,128)S(1)}, f32[1,256,512]{2,1,0:T(8,128)S(1)}, u32[]{:S(2)}, u32[]{:S(2)}) %collective-permute-start.35) | collective-permute-done | bytes 524320 | tf_op jit(solution)/shard_map/ppermute | solution.py:390
  379.2 6.8 %collective-permute-done.34.refs_3_.refs_4_.refs_5_ = f32[3,256,512]{2,1,0:T(8,128)S(1)} collective-permute-done((f32[3,256,512]{2,1,0:T(8,128)}, f32[3,256,512]{2,1,0:T(8,128)S(1)}, u32[]{:S(2)}, u32[]{:S(2)}) %collective-permute-start.34) | collective-permute-done | bytes 1572896 | tf_op jit(solution)/shard_map/ppermute | solution.py:382
  387.3 8.0 %place.4 = (bf16[8,2048,1024]{2,1,0:T(8,128)(2,1)}, f32[8,256,512]{2,1,0:T(8,128)}) custom-call(s32[7]{0:T(128)S(1)} %stack.76.ids_ref, bf16[1,2048,1024]{2,1,0:T(8,128)(2,1)} %collective-permute-done.33.refs_0_, bf16[1,2048,1024]{2,1,0:T(8,128)(2,1)} %collective-permute-done.30.refs_1_, ...), custom_call_target="tpu_custom_call", output_to_operand_aliasing={{0}: (8, {}), {1}: (9, {})} | custom-call | tf_op jit(solution)/shard_map/place/pallas_call | solution.py:296
  395.3 3.6 place.5.refs_1_
  398.9 3.6 place.6.refs_2_
  402.5 4.3 %place.7 = (bf16[8,2048,1024]{2,1,0:T(8,128)(2,1)}, f32[8,256,512]{2,1,0:T(8,128)}) custom-call(s32[2]{0:T(128)S(1)} %pad_add_fusion.ids_ref, bf16[1,2048,1024]{2,1,0:T(8,128)(2,1)} %collective-permute-done.28.refs_0_, f32[1,256,512]{2,1,0:T(8,128)S(1)} %collective-permute-done.29.refs_1_, ...), custom_call_target="tpu_custom_call", output_to_operand_aliasing={{0}: (3, {}), {1}: (4, {})} | custom-call | tf_op jit(solution)/shard_map/place/pallas_call | solution.py:296
  (110 shorter events, 20.7 us)
Async XLA Ops:
  0.6 79.7 %collective-permute-start.4 = (f32[8,256,512]{2,1,0:T(8,128)}, f32[8,256,512]{2,1,0:T(8,128)}, u32[]{:S(2)}, u32[]{:S(2)}) collective-permute-start(f32[8,256,512]{2,1,0:T(8,128)} %bitcast.27), channel_id=1, source_target_pairs={{0,1},{1,0},{2,3},{3,2},{4,5},{5,4},{6,7},{7,6},{8,9},{9,8},{10,11... | collective-permute-start | bytes 12582920 | tf_op jit(solution)/shard_map/ppermute | solution.py:360
  1.9 77.5 %collective-permute-start.2 = (bf16[1024,512]{1,0:T(8,128)(2,1)}, bf16[1024,512]{1,0:T(8,128)(2,1)S(1)}, u32[]{:S(2)}, u32[]{:S(2)}) collective-permute-start(bf16[1024,512]{1,0:T(8,128)(2,1)} %w_v.1), channel_id=1, source_target_pairs={{0,1},{1,0},{2,3},{3,2},{4,5},{5,4},{6,7},{7,6},{8,9},{9,8},{10,11... | collective-permute-start | bytes 3145736 | tf_op jit(solution)/shard_map/ppermute | solution.py:359
  8.0 21.7 %collective-permute-start.6 = (bf16[256,1536]{1,0:T(8,128)(2,1)}, bf16[256,1536]{1,0:T(8,128)(2,1)}, u32[]{:S(2)}, u32[]{:S(2)}) collective-permute-start(bf16[256,1536]{1,0:T(8,128)(2,1)} %get-tuple-element.70), channel_id=1, source_target_pairs={{0,2},{1,3},{2,0},{3,1},{4,6},{5,7},{6,4},{7,5},{8,10},{9,11},{10,... | collective-permute-start | bytes 2359304 | tf_op jit(solution)/shard_map/ppermute | solution.py:362
  13.6 66.3 %collective-permute-start.3 = (bf16[1024,512]{1,0:T(8,128)(2,1)S(1)}, bf16[1024,512]{1,0:T(8,128)(2,1)}, u32[]{:S(2)}, u32[]{:S(2)}) collective-permute-start(bf16[1024,512]{1,0:T(8,128)(2,1)S(1)} %copy-done.1), channel_id=1, source_target_pairs={{0,1},{1,0},{2,3},{3,2},{4,5},{5,4},{6,7},{7,6},{8,9},{9,8},{10,11... | collective-permute-start | bytes 3145736 | tf_op jit(solution)/shard_map/ppermute | solution.py:359
  13.6 63.2 %collective-permute-start.5 = (bf16[256,1536]{1,0:T(8,128)(2,1)}, bf16[256,1536]{1,0:T(8,128)(2,1)}, u32[]{:S(2)}, u32[]{:S(2)}) collective-permute-start(bf16[256,1536]{1,0:T(8,128)(2,1)} %get-tuple-element.62), channel_id=1, source_target_pairs={{0,2},{1,3},{2,0},{3,1},{4,6},{5,7},{6,4},{7,5},{8,10},{9,11},{10,... | collective-permute-start | bytes 2359304 | tf_op jit(solution)/shard_map/ppermute | solution.py:363
  29.7 53.2 %collective-permute-start.13 = (f32[2,256,512]{2,1,0:T(8,128)}, f32[2,256,512]{2,1,0:T(8,128)}, u32[]{:S(2)}, u32[]{:S(2)}) collective-permute-start(f32[2,256,512]{2,1,0:T(8,128)} %get-tuple-element.73), channel_id=1, source_target_pairs={{0,2},{1,3},{2,0},{3,1},{4,6},{5,7},{6,4},{7,5},{8,10},{9,11},{10,... | collective-permute-start | bytes 3145736 | tf_op jit(solution)/shard_map/ppermute | solution.py:364
  76.8 21.7 %collective-permute-start.9 = (bf16[256,1536]{1,0:T(8,128)(2,1)}, bf16[256,1536]{1,0:T(8,128)(2,1)}, u32[]{:S(2)}, u32[]{:S(2)}) collective-permute-start(bf16[256,1536]{1,0:T(8,128)(2,1)} %collective-permute-done.6.refs_3_.refs_14_), channel_id=1, source_target_pairs={{0,12},{4,8},{8,4},{12,0},{1,13},{5,9},{9,5},{13,1},{2,14},{6,10},... | collective-permute-start | bytes 2359304 | tf_op jit(solution)/shard_map/ppermute | solution.py:354
  79.4 35.9 %collective-permute-start.8 = (bf16[256,1536]{1,0:T(8,128)(2,1)}, bf16[256,1536]{1,0:T(8,128)(2,1)S(1)}, u32[]{:S(2)}, u32[]{:S(2)}) collective-permute-start(bf16[256,1536]{1,0:T(8,128)(2,1)} %collective-permute-done.6.refs_3_.refs_14_), channel_id=1, source_target_pairs={{0,8},{4,12},{8,0},{12,4},{1,9},{5,13},{9,1},{13,5},{2,10},{6,14},... | collective-permute-start | bytes 2359304 | tf_op jit(solution)/shard_map/ppermute | solution.py:354
  79.8 35.5 %collective-permute-start.7 = (bf16[256,1536]{1,0:T(8,128)(2,1)}, bf16[256,1536]{1,0:T(8,128)(2,1)S(1)}, u32[]{:S(2)}, u32[]{:S(2)}) collective-permute-start(bf16[256,1536]{1,0:T(8,128)(2,1)} %collective-permute-done.6.refs_3_.refs_14_), channel_id=1, source_target_pairs={{0,4},{4,0},{8,12},{12,8},{1,5},{5,1},{9,13},{13,9},{2,6},{6,2},{1... | collective-permute-start | bytes 2359304 | tf_op jit(solution)/shard_map/ppermute | solution.py:354
  80.4 48.9 %collective-permute-start.12 = (bf16[256,1536]{1,0:T(8,128)(2,1)}, bf16[256,1536]{1,0:T(8,128)(2,1)S(1)}, u32[]{:S(2)}, u32[]{:S(2)}) collective-permute-start(bf16[256,1536]{1,0:T(8,128)(2,1)} %collective-permute-done.5.refs_17_.refs_28_), channel_id=1, source_target_pairs={{0,12},{4,8},{8,4},{12,0},{1,13},{5,9},{9,5},{13,1},{2,14},{6,10},... | collective-permute-start | bytes 2359304 | tf_op jit(solution)/shard_map/ppermute | solution.py:354
  82.9 63.2 %collective-permute-start.11 = (bf16[256,1536]{1,0:T(8,128)(2,1)}, bf16[256,1536]{1,0:T(8,128)(2,1)}, u32[]{:S(2)}, u32[]{:S(2)}) collective-permute-start(bf16[256,1536]{1,0:T(8,128)(2,1)} %collective-permute-done.5.refs_17_.refs_28_), channel_id=1, source_target_pairs={{0,8},{4,12},{8,0},{12,4},{1,9},{5,13},{9,1},{13,5},{2,10},{6,14},... | collective-permute-start | bytes 2359304 | tf_op jit(solution)/shard_map/ppermute | solution.py:354
  98.5 83.7 %collective-permute-start.22 = (bf16[512,1024]{1,0:T(8,128)(2,1)S(1)}, bf16[512,1024]{1,0:T(8,128)(2,1)S(1)}, u32[]{:S(2)}, u32[]{:S(2)}) collective-permute-start(bf16[512,1024]{1,0:T(8,128)(2,1)S(1)} %copy-done.2), channel_id=1, source_target_pairs={{0,1},{1,0},{2,3},{3,2},{4,5},{5,4},{6,7},{7,6},{8,9},{9,8},{10,11... | collective-permute-start | bytes 3145736 | tf_op jit(solution)/shard_map/ppermute | solution.py:366
  115.3 67.4 %collective-permute-start.24 = (bf16[1024,512]{1,0:T(8,128)(2,1)S(1)}, bf16[1024,512]{1,0:T(8,128)(2,1)}, u32[]{:S(2)}, u32[]{:S(2)}) collective-permute-start(bf16[1024,512]{1,0:T(8,128)(2,1)S(1)} %copy-done.4), channel_id=1, source_target_pairs={{0,1},{1,0},{2,3},{3,2},{4,5},{5,4},{6,7},{7,6},{8,9},{9,8},{10,11... | collective-permute-start | bytes 3145736 | tf_op jit(solution)/shard_map/ppermute | solution.py:366
  115.4 67.4 %collective-permute-start.23 = (bf16[512,1024]{1,0:T(8,128)(2,1)S(1)}, bf16[512,1024]{1,0:T(8,128)(2,1)}, u32[]{:S(2)}, u32[]{:S(2)}) collective-permute-start(bf16[512,1024]{1,0:T(8,128)(2,1)S(1)} %copy-done.3), channel_id=1, source_target_pairs={{0,1},{1,0},{2,3},{3,2},{4,5},{5,4},{6,7},{7,6},{8,9},{9,8},{10,11... | collective-permute-start | bytes 3145736 | tf_op jit(solution)/shard_map/ppermute | solution.py:366
  130.1 53.1 %collective-permute-start.26 = (f32[4,256,512]{2,1,0:T(8,128)}, f32[4,256,512]{2,1,0:T(8,128)}, u32[]{:S(2)}, u32[]{:S(2)}) collective-permute-start(f32[4,256,512]{2,1,0:T(8,128)} %get-tuple-element.84), channel_id=1, source_target_pairs={{0,2},{1,3},{2,0},{3,1},{4,6},{5,7},{6,4},{7,5},{8,10},{9,11},{10,... | collective-permute-start | bytes 6291464 | tf_op jit(solution)/shard_map/ppermute | solution.py:365
  146.1 36.1 %collective-permute-start.10 = (bf16[256,1536]{1,0:T(8,128)(2,1)}, bf16[256,1536]{1,0:T(8,128)(2,1)}, u32[]{:S(2)}, u32[]{:S(2)}) collective-permute-start(bf16[256,1536]{1,0:T(8,128)(2,1)} %collective-permute-done.5.refs_17_.refs_28_), channel_id=1, source_target_pairs={{0,4},{4,0},{8,12},{12,8},{1,5},{5,1},{9,13},{13,9},{2,6},{6,2},{1... | collective-permute-start | bytes 2359304 | tf_op jit(solution)/shard_map/ppermute | solution.py:354
  183.3 20.1 %collective-permute-start.25 = (f32[2,256,512]{2,1,0:T(8,128)}, f32[2,256,512]{2,1,0:T(8,128)S(1)}, u32[]{:S(2)}, u32[]{:S(2)}) collective-permute-start(f32[2,256,512]{2,1,0:T(8,128)} %collective-permute-done.13.refs_2_), channel_id=1, source_target_pairs={{0,1},{1,0},{2,3},{3,2},{4,5},{5,4},{6,7},{7,6},{8,9},{9,8},{10,11... | collective-permute-start | bytes 3145736 | tf_op jit(solution)/shard_map/ppermute | solution.py:381
  184.7 18.6 %collective-permute-start.18 = (bf16[256,1536]{1,0:T(8,128)(2,1)}, bf16[256,1536]{1,0:T(8,128)(2,1)S(1)}, u32[]{:S(2)}, u32[]{:S(2)}) collective-permute-start(bf16[256,1536]{1,0:T(8,128)(2,1)} %collective-permute-done.5.refs_17_.refs_28_), channel_id=1, source_target_pairs={{0,1},{1,0},{2,3},{3,2},{4,5},{5,4},{6,7},{7,6},{8,9},{9,8},{10,11... | collective-permute-start | bytes 2359304 | tf_op jit(solution)/shard_map/ppermute | solution.py:381
  204.2 50.6 %collective-permute-start.27 = (f32[4,256,512]{2,1,0:T(8,128)}, f32[4,256,512]{2,1,0:T(8,128)S(1)}, u32[]{:S(2)}, u32[]{:S(2)}) collective-permute-start(f32[4,256,512]{2,1,0:T(8,128)} %collective-permute-done.26.refs_6_.refs_7_), channel_id=1, source_target_pairs={{0,1},{1,0},{2,3},{3,2},{4,5},{5,4},{6,7},{7,6},{8,9},{9,8},{10,11... | collective-permute-start | bytes 6291464 | tf_op jit(solution)/shard_map/ppermute | solution.py:386
  253.9 133.4 %collective-permute-start.33 = (bf16[1,2048,1024]{2,1,0:T(8,128)(2,1)}, bf16[1,2048,1024]{2,1,0:T(8,128)(2,1)}, u32[]{:S(2)}, u32[]{:S(2)}) collective-permute-start(bf16[1,2048,1024]{2,1,0:T(8,128)(2,1)} %get-tuple-element.105), channel_id=1, source_target_pairs={{0,1},{1,0},{2,3},{3,2},{4,5},{5,4},{6,7},{7,6},{8,9},{9,8},{10,11... | collective-permute-start | bytes 12582920 | tf_op jit(solution)/shard_map/ppermute | solution.py:389
  254.3 110.0 %collective-permute-start.30 = (bf16[1,2048,1024]{2,1,0:T(8,128)(2,1)}, bf16[1,2048,1024]{2,1,0:T(8,128)(2,1)}, u32[]{:S(2)}, u32[]{:S(2)}) collective-permute-start(bf16[1,2048,1024]{2,1,0:T(8,128)(2,1)} %get-tuple-element.105), channel_id=1, source_target_pairs={{0,2},{1,3},{2,0},{3,1},{4,6},{5,7},{6,4},{7,5},{8,10},{9,11},{10,... | collective-permute-start | bytes 12582920 | tf_op jit(solution)/shard_map/ppermute | solution.py:388
  364.3 31.0 %collective-permute-start.32 = (bf16[1,2048,1024]{2,1,0:T(8,128)(2,1)}, bf16[1,2048,1024]{2,1,0:T(8,128)(2,1)}, u32[]{:S(2)}, u32[]{:S(2)}) collective-permute-start(bf16[1,2048,1024]{2,1,0:T(8,128)(2,1)} %get-tuple-element.106), channel_id=1, source_target_pairs={{0,1},{1,0},{2,3},{3,2},{4,5},{5,4},{6,7},{7,6},{8,9},{9,8},{10,11... | collective-permute-start | bytes 12582920 | tf_op jit(solution)/shard_map/ppermute | solution.py:394
  364.3 34.6 %collective-permute-start.31 = (bf16[1,2048,1024]{2,1,0:T(8,128)(2,1)}, bf16[1,2048,1024]{2,1,0:T(8,128)(2,1)}, u32[]{:S(2)}, u32[]{:S(2)}) collective-permute-start(bf16[1,2048,1024]{2,1,0:T(8,128)(2,1)} %collective-permute-done.30.refs_1_), channel_id=1, source_target_pairs={{0,1},{1,0},{2,3},{3,2},{4,5},{5,4},{6,7},{7,6},{8,9},{9,8},{10,11... | collective-permute-start | bytes 12582920 | tf_op jit(solution)/shard_map/ppermute | solution.py:395
  364.8 37.7 %collective-permute-start.28 = (bf16[1,2048,1024]{2,1,0:T(8,128)(2,1)}, bf16[1,2048,1024]{2,1,0:T(8,128)(2,1)}, u32[]{:S(2)}, u32[]{:S(2)}) collective-permute-start(bf16[1,2048,1024]{2,1,0:T(8,128)(2,1)} %get-tuple-element.103), channel_id=1, source_target_pairs={{0,1},{1,0},{2,3},{3,2},{4,5},{5,4},{6,7},{7,6},{8,9},{9,8},{10,11... | collective-permute-start | bytes 12582920 | tf_op jit(solution)/shard_map/ppermute | solution.py:397
  (30 other events, 695.6 us)

commit v8 on v7

--- a/solution.py
+++ b/solution.py
@@ -100,22 +100,25 @@
     inner_ref, rows_ref, sem = take(3)
     weights = list(it)
 
+    early, late, slot = [], [], 0
+    for ref, cuts in zip(sources, pieces):
+        for to, row, col, first, width, flip, skip in cuts:
+            if flip is not None:
+                quarter = meta_ref[GROUP] ^ flip
+                row = pl.multiple_of(row + quarter * ref.shape[0] + quarter // 2 * skip, 256)
+            dst = weights[to].at[pl.ds(row, ref.shape[0]), pl.ds(col, width)]
+            (early if to < len(heads) else late).append(pltpu.make_async_copy(ref.at[:, pl.ds(first, width)], dst, sem.at[slot]))
+            slot += 1
+
     @pl.when(pl.program_id(0) == 0)
     def _():
-        copies = []
-        for ref, cuts in zip(sources, pieces):
-            for to, row, col, first, width, flip, skip in cuts:
-                if flip is not None:
-                    quarter = meta_ref[GROUP] ^ flip
-                    row = pl.multiple_of(row + quarter * ref.shape[0] + quarter // 2 * skip, 256)
-                dst = weights[to].at[pl.ds(row, ref.shape[0]), pl.ds(col, width)]
-                copies.append(pltpu.make_async_copy(ref.at[:, pl.ds(first, width)], dst, sem.at[len(copies)]))
-                copies[-1].start()
+        for copy in early + late:
+            copy.start()
         fill_decays([log_decay(meta_ref[HEAD] ^ head) for head in heads], inner_ref, rows_ref)
         for per_head, state_ref in zip(s_refs, state_refs):
             for b, s_ref in enumerate(per_head):
                 state_ref[b] = s_ref[0]
-        for copy in copies:
+        for copy in early:
             copy.wait()
 
     cos_b, sin_b = step_ref[0], step_ref[1]
@@ -138,6 +141,12 @@
         for i, block in enumerate(mixed[0]):
             outs[0][i // n_sub, i % n_sub * TILE:(i % n_sub + 1) * TILE] = block
         return
+
+    @pl.when(pl.program_id(0) == 0)
+    def _():
+        for copy in late:
+            copy.wait()
+
     mixed = [[ref[0] for ref in refs_of] for refs_of in z_refs] + mixed
     w_od, w_up = weights[len(heads):]
     width = w_up.shape[1]
@@ -216,7 +225,7 @@
             scratch_shapes=[pltpu.VMEM((len(heads), TILE, TILE), F32), pltpu.VMEM((len(heads), 3, TILE, 128), F32), pltpu.SemaphoreType.DMA((sum(map(len, pieces)),))]
             + [pltpu.VMEM(shape, BF16) for shape in scratch]),
         out_shape=[shape for _, shape in outs],
-        compiler_params=pltpu.CompilerParams(dimension_semantics=("arbitrary",), vmem_limit_bytes=58 << 20),
+        compiler_params=pltpu.CompilerParams(dimension_semantics=("arbitrary",), vmem_limit_bytes=62 << 20),
         cost_estimate=pl.CostEstimate(flops=chunk_len * flops, bytes_accessed=n * chunk_len * d_model * (8 if zs else 4), transcendentals=0),
         input_output_aliases=aliases,
         name="tail" if zs else "heads",
@@ -372,7 +381,7 @@
         z_own_single, h_single, new_own_single = run(meta, common, one, one, (0,), (own,), head_places(head_w), n_sub=2)
         z_own_single, wa_part = lax.optimization_barrier((z_own_single, wa_part))
         wa_quarters = gather(wa_part)
-        z_own, h_twice, new_states = run(meta, common, pair_seqs, pair_seqs, (0,), (own,), head_places(head_w), pair=True)
+        z_own, h_twice, new_states = run(meta, common, pair_seqs, pair_seqs, (0,), (own,), head_places(head_w), pair=True, n_sub=2)
         z_own, wa_core, s_core, wb_part = lax.optimization_barrier((z_own, wa_core, s_core, wb_part))
         wb_quarters = gather(wb_part)
         hs_single, hs_twice = ((h_single, 0),), ((h_twice, 0), (h_twice, 1))

time: 407 us -> 400 us (0.983)
    pallas_call x6, Pallas kernels: 251 us -> 247 us  [run(): pl.pallas_call(functools.partial(kernel_body, n, n_sub, bool(hs), tuple(h...]
where the time goes in v8:
time: 400 us; the launch traced here: 399 us
  Pallas kernels  272 us (68%)
  waiting for transfers between devices  100 us (25%)
  starting transfers between devices  21.6 us (5%)
    pallas_call x6, Pallas kernels, run(): pl.pallas_call(functools.partial(kernel_body, n, n_sub, bool(hs), tuple(h...  247 us
    ppermute x6, waiting for transfers between devices, gather(): return [part] + [swap('dp', flip)(part) for flip in range(1, n_dp)]  61.7 us
    pallas_call x4, Pallas kernels, place(): pl.pallas_call(functools.partial(place_kernel, tuple((block[1:] for block...  19.5 us
    ppermute x1, waiting for transfers between devices, local_layer(): wa_part = to_chip(wa_part)  14.5 us
    ppermute x1, waiting for transfers between devices, local_layer(): got_chip = to_chip(new_chip)  12.8 us
    ppermute x6, starting transfers between devices, gather(): return [part] + [swap('dp', flip)(part) for flip in range(1, n_dp)]  8.04 us
  transfers between devices with their start and end apart: 36, of which 11 were waited for; matrix products, arithmetic and copies ran while one was open for 1% of the time, Pallas kernels for 67%

profile of v8, /device:TPU:0, one launch (start us, length us, event | category | flops | bytes accessed | tf_op | source)
XLA Modules:
  0.0 399.3 jit_solution(603213610518682409)
XLA Ops:
  2.6 5.4 %parts.1 = (bf16[256,1536]{1,0:T(8,128)(2,1)}, bf16[256,1536]{1,0:T(8,128)(2,1)}, f32[2,256,512]{2,1,0:T(8,128)}, f32[4,256,512]{2,1,0:T(8,128)}) custom-call(s32[10]{0:T(128)} %stack.72.meta_ref, bf16[1024,256]{1,0:T(8,128)(2,1)} %w_q.1, bf16[1024,256]{1,0:T(8,128)(2,1)} %w_k.1, bf16[1024,512]{1,0:T(8,128)(2,1)} %w_v.1, bf16[1024,512]{1,0:T(8,128)(2,1)} %w_g.1, ...), custom_call_target="tpu_custom_call" | custom-call | tf_op jit(solution)/shard_map/parts/pallas_call | solution.py:274
  8.0 3.0 collective-permute-start.6
  15.1 14.5 %collective-permute-done.6.refs_3_.refs_14_ = bf16[256,1536]{1,0:T(8,128)(2,1)} collective-permute-done((bf16[256,1536]{1,0:T(8,128)(2,1)}, bf16[256,1536]{1,0:T(8,128)(2,1)}, u32[]{:S(2)}, u32[]{:S(2)}) %collective-permute-start.6) | collective-permute-done | bytes 786464 | tf_op jit(solution)/shard_map/ppermute | solution.py:371
  29.7 2.0 collective-permute-start.13
  31.7 27.7 %heads.4 = (bf16[2,2048,512]{2,1,0:T(8,128)(2,1)}, bf16[2,2048,1024]{2,1,0:T(8,128)(2,1)}, f32[8,256,512]{2,1,0:T(8,128)}) custom-call(s32[10]{0:T(128)} %stack.72.meta_ref, f32[1,1024]{1,0:T(1,128)} %bitcast.33, f32[1,1024]{1,0:T(1,128)} %bitcast.39, f32[1,1024]{1,0:T(1,128)} %bitcast.45, f32[1,1024]{1,0:T(1,128)} %bitcast.51, ...), custom_call_target="tpu_custom_call" | custom-call | flops 16642998272 | bytes 16777216 | tf_op jit(solution)/shard_map/heads/pallas_call | solution.py:221
  59.4 16.3 %heads.5 = (bf16[1,2048,512]{2,1,0:T(8,128)(2,1)}, bf16[1,2048,1024]{2,1,0:T(8,128)(2,1)}, f32[1,256,512]{2,1,0:T(8,128)}) custom-call(s32[10]{0:T(128)} %stack.72.meta_ref, f32[1,1024]{1,0:T(1,128)} %bitcast.34, f32[1,1024]{1,0:T(1,128)} %bitcast.40, f32[1,1024]{1,0:T(1,128)} %bitcast.46, f32[1,1024]{1,0:T(1,128)} %bitcast.52, ...), custom_call_target="tpu_custom_call" | custom-call | flops 8321499136 | bytes 8388608 | tf_op jit(solution)/shard_map/heads/pallas_call | solution.py:221
  75.7 2.6 collective-permute-start.9
  79.3 2.5 collective-permute-start.12
  82.3 15.2 %collective-permute-done.9.refs_6_.refs_17_ = bf16[256,1536]{1,0:T(8,128)(2,1)} collective-permute-done((bf16[256,1536]{1,0:T(8,128)(2,1)}, bf16[256,1536]{1,0:T(8,128)(2,1)}, u32[]{:S(2)}, u32[]{:S(2)}) %collective-permute-start.9) | collective-permute-done | bytes 786464 | tf_op jit(solution)/shard_map/ppermute | solution.py:363
  97.4 16.9 %collective-permute-done.8.refs_5_.refs_16_ = bf16[256,1536]{1,0:T(8,128)(2,1)} collective-permute-done((bf16[256,1536]{1,0:T(8,128)(2,1)}, bf16[256,1536]{1,0:T(8,128)(2,1)}, u32[]{:S(2)}, u32[]{:S(2)}) %collective-permute-start.8) | collective-permute-done | bytes 786464 | tf_op jit(solution)/shard_map/ppermute | solution.py:363
  114.9 13.4 %collective-permute-done.12.refs_20_.refs_31_ = bf16[256,1536]{1,0:T(8,128)(2,1)} collective-permute-done((bf16[256,1536]{1,0:T(8,128)(2,1)}, bf16[256,1536]{1,0:T(8,128)(2,1)}, u32[]{:S(2)}, u32[]{:S(2)}) %collective-permute-start.12) | collective-permute-done | bytes 786464 | tf_op jit(solution)/shard_map/ppermute | solution.py:363
  128.8 16.1 %collective-permute-done.11.refs_19_.refs_30_ = bf16[256,1536]{1,0:T(8,128)(2,1)} collective-permute-done((bf16[256,1536]{1,0:T(8,128)(2,1)}, bf16[256,1536]{1,0:T(8,128)(2,1)}, u32[]{:S(2)}, u32[]{:S(2)}) %collective-permute-start.11) | collective-permute-done | bytes 786464 | tf_op jit(solution)/shard_map/ppermute | solution.py:363
  145.0 1.5 collective-permute-start.10
  146.5 34.8 %heads.6 = (bf16[3,2048,512]{2,1,0:T(8,128)(2,1)}, f32[3,256,512]{2,1,0:T(8,128)}) custom-call(s32[10]{0:T(128)} %stack.72.meta_ref, f32[1,1024]{1,0:T(1,128)} %bitcast.35, f32[1,1024]{1,0:T(1,128)} %bitcast.41, f32[1,1024]{1,0:T(1,128)} %bitcast.47, f32[1,1024]{1,0:T(1,128)} %bitcast.53, f32[2,256,128]{2,1,0:T(8,128)} %broadcast_select_fusion.step_ref, ...), custom_call_target="tpu_custom_call" | custom-call | flops 24964497408 | bytes 25165824 | tf_op jit(solution)/shard_map/heads/pallas_call | solution.py:221
  182.4 1.5 collective-permute-done.14.refs_7_.refs_18_
  187.5 14.7 %heads.7 = (bf16[1,2048,512]{2,1,0:T(8,128)(2,1)}, f32[1,256,512]{2,1,0:T(8,128)}) custom-call(s32[10]{0:T(128)} %stack.72.meta_ref, f32[1,1024]{1,0:T(1,128)} %bitcast.36, f32[1,1024]{1,0:T(1,128)} %bitcast.42, f32[1,1024]{1,0:T(1,128)} %bitcast.48, f32[1,1024]{1,0:T(1,128)} %bitcast.54, f32[2,256,128]{2,1,0:T(8,128)} %broadcast_select_fusion.step_ref, ...), custom_call_target="tpu_custom_call" | custom-call | flops 8321499136 | bytes 8388608 | tf_op jit(solution)/shard_map/heads/pallas_call | solution.py:221
  202.7 47.2 %tail.2 = (bf16[8,2048,1024]{2,1,0:T(8,128)(2,1)}, bf16[1,2048,1024]{2,1,0:T(8,128)(2,1)}, f32[1,256,512]{2,1,0:T(8,128)}) custom-call(s32[10]{0:T(128)} %stack.72.meta_ref, f32[1,1024]{1,0:T(1,128)} %bitcast.37, f32[1,1024]{1,0:T(1,128)} %bitcast.43, f32[1,1024]{1,0:T(1,128)} %bitcast.49, f32[1,1024]{1,0:T(1,128)} %bitcast.55, ...), custom_call_target="tpu_custom_call" | custom-call | flops 34091302912 | bytes 16777216 | tf_op jit(solution)/shard_map/tail/pallas_call | solution.py:221
  250.6 105.9 %tail.3 = (bf16[8,2048,1024]{2,1,0:T(8,128)(2,1)}, bf16[1,2048,1024]{2,1,0:T(8,128)(2,1)}, bf16[1,2048,1024]{2,1,0:T(8,128)(2,1)}, f32[2,256,512]{2,1,0:T(8,128)}, f32[2,256,512]{2,1,0:T(8,128)}) custom-call(s32[10]{0:T(128)} %stack.72.meta_ref, f32[1,1024]{1,0:T(1,128)} %bitcast.38, f32[1,1024]{1,0:T(1,128)} %bitcast.44, ...), custom_call_target="tpu_custom_call", output_to_operand_aliasing={{0}: (42, {})} | custom-call | flops 84825604096 | bytes 33554432 | tf_op jit(solution)/shard_map/tail/pallas_call | solution.py:221
  358.7 12.8 %collective-permute-done.35.refs_6_ = f32[1,256,512]{2,1,0:T(8,128)S(1)} collective-permute-done((f32[1,256,512]{2,1,0:T(8,128)S(1)}, f32[1,256,512]{2,1,0:T(8,128)S(1)}, u32[]{:S(2)}, u32[]{:S(2)}) %collective-permute-start.35) | collective-permute-done | bytes 524320 | tf_op jit(solution)/shard_map/ppermute | solution.py:399
  371.4 6.8 %collective-permute-done.34.refs_3_.refs_4_.refs_5_ = f32[3,256,512]{2,1,0:T(8,128)S(1)} collective-permute-done((f32[3,256,512]{2,1,0:T(8,128)}, f32[3,256,512]{2,1,0:T(8,128)S(1)}, u32[]{:S(2)}, u32[]{:S(2)}) %collective-permute-start.34) | collective-permute-done | bytes 1572896 | tf_op jit(solution)/shard_map/ppermute | solution.py:391
  379.6 8.0 %place.4 = (bf16[8,2048,1024]{2,1,0:T(8,128)(2,1)}, f32[8,256,512]{2,1,0:T(8,128)}) custom-call(s32[7]{0:T(128)S(1)} %stack.76.ids_ref, bf16[1,2048,1024]{2,1,0:T(8,128)(2,1)} %collective-permute-done.33.refs_0_, bf16[1,2048,1024]{2,1,0:T(8,128)(2,1)} %collective-permute-done.30.refs_1_, ...), custom_call_target="tpu_custom_call", output_to_operand_aliasing={{0}: (8, {}), {1}: (9, {})} | custom-call | tf_op jit(solution)/shard_map/place/pallas_call | solution.py:305
  387.6 3.6 place.5.refs_1_
  391.2 3.6 place.6.refs_2_
  394.8 4.3 %place.7 = (bf16[8,2048,1024]{2,1,0:T(8,128)(2,1)}, f32[8,256,512]{2,1,0:T(8,128)}) custom-call(s32[2]{0:T(128)S(1)} %pad_add_fusion.ids_ref, bf16[1,2048,1024]{2,1,0:T(8,128)(2,1)} %collective-permute-done.28.refs_0_, f32[1,256,512]{2,1,0:T(8,128)S(1)} %collective-permute-done.29.refs_1_, ...), custom_call_target="tpu_custom_call", output_to_operand_aliasing={{0}: (3, {}), {1}: (4, {})} | custom-call | tf_op jit(solution)/shard_map/place/pallas_call | solution.py:305
  (88 shorter events, 17.9 us)
Async XLA Ops:
  0.6 78.6 %collective-permute-start.4 = (f32[8,256,512]{2,1,0:T(8,128)}, f32[8,256,512]{2,1,0:T(8,128)}, u32[]{:S(2)}, u32[]{:S(2)}) collective-permute-start(f32[8,256,512]{2,1,0:T(8,128)} %bitcast.27), channel_id=1, source_target_pairs={{0,1},{1,0},{2,3},{3,2},{4,5},{5,4},{6,7},{7,6},{8,9},{9,8},{10,11... | collective-permute-start | bytes 12582920 | tf_op jit(solution)/shard_map/ppermute | solution.py:369
  1.9 76.4 %collective-permute-start.2 = (bf16[1024,512]{1,0:T(8,128)(2,1)}, bf16[1024,512]{1,0:T(8,128)(2,1)}, u32[]{:S(2)}, u32[]{:S(2)}) collective-permute-start(bf16[1024,512]{1,0:T(8,128)(2,1)} %w_v.1), channel_id=1, source_target_pairs={{0,1},{1,0},{2,3},{3,2},{4,5},{5,4},{6,7},{7,6},{8,9},{9,8},{10,11... | collective-permute-start | bytes 3145736 | tf_op jit(solution)/shard_map/ppermute | solution.py:368
  8.0 21.7 %collective-permute-start.6 = (bf16[256,1536]{1,0:T(8,128)(2,1)}, bf16[256,1536]{1,0:T(8,128)(2,1)}, u32[]{:S(2)}, u32[]{:S(2)}) collective-permute-start(bf16[256,1536]{1,0:T(8,128)(2,1)} %get-tuple-element.70), channel_id=1, source_target_pairs={{0,2},{1,3},{2,0},{3,1},{4,6},{5,7},{6,4},{7,5},{8,10},{9,11},{10,... | collective-permute-start | bytes 2359304 | tf_op jit(solution)/shard_map/ppermute | solution.py:371
  13.5 65.2 %collective-permute-start.3 = (bf16[1024,512]{1,0:T(8,128)(2,1)S(1)}, bf16[1024,512]{1,0:T(8,128)(2,1)}, u32[]{:S(2)}, u32[]{:S(2)}) collective-permute-start(bf16[1024,512]{1,0:T(8,128)(2,1)S(1)} %copy-done.1), channel_id=1, source_target_pairs={{0,1},{1,0},{2,3},{3,2},{4,5},{5,4},{6,7},{7,6},{8,9},{9,8},{10,11... | collective-permute-start | bytes 3145736 | tf_op jit(solution)/shard_map/ppermute | solution.py:368
  15.1 60.6 %collective-permute-start.5 = (bf16[256,1536]{1,0:T(8,128)(2,1)}, bf16[256,1536]{1,0:T(8,128)(2,1)}, u32[]{:S(2)}, u32[]{:S(2)}) collective-permute-start(bf16[256,1536]{1,0:T(8,128)(2,1)} %get-tuple-element.62), channel_id=1, source_target_pairs={{0,2},{1,3},{2,0},{3,1},{4,6},{5,7},{6,4},{7,5},{8,10},{9,11},{10,... | collective-permute-start | bytes 2359304 | tf_op jit(solution)/shard_map/ppermute | solution.py:372
  29.7 52.1 %collective-permute-start.13 = (f32[2,256,512]{2,1,0:T(8,128)}, f32[2,256,512]{2,1,0:T(8,128)}, u32[]{:S(2)}, u32[]{:S(2)}) collective-permute-start(f32[2,256,512]{2,1,0:T(8,128)} %get-tuple-element.73), channel_id=1, source_target_pairs={{0,2},{1,3},{2,0},{3,1},{4,6},{5,7},{6,4},{7,5},{8,10},{9,11},{10,... | collective-permute-start | bytes 3145736 | tf_op jit(solution)/shard_map/ppermute | solution.py:373
  75.7 21.7 %collective-permute-start.9 = (bf16[256,1536]{1,0:T(8,128)(2,1)}, bf16[256,1536]{1,0:T(8,128)(2,1)}, u32[]{:S(2)}, u32[]{:S(2)}) collective-permute-start(bf16[256,1536]{1,0:T(8,128)(2,1)} %collective-permute-done.6.refs_3_.refs_14_), channel_id=1, source_target_pairs={{0,12},{4,8},{8,4},{12,0},{1,13},{5,9},{9,5},{13,1},{2,14},{6,10},... | collective-permute-start | bytes 2359304 | tf_op jit(solution)/shard_map/ppermute | solution.py:363
  78.3 36.0 %collective-permute-start.8 = (bf16[256,1536]{1,0:T(8,128)(2,1)}, bf16[256,1536]{1,0:T(8,128)(2,1)}, u32[]{:S(2)}, u32[]{:S(2)}) collective-permute-start(bf16[256,1536]{1,0:T(8,128)(2,1)} %collective-permute-done.6.refs_3_.refs_14_), channel_id=1, source_target_pairs={{0,8},{4,12},{8,0},{12,4},{1,9},{5,13},{9,1},{13,5},{2,10},{6,14},... | collective-permute-start | bytes 2359304 | tf_op jit(solution)/shard_map/ppermute | solution.py:363
  78.8 35.6 %collective-permute-start.7 = (bf16[256,1536]{1,0:T(8,128)(2,1)}, bf16[256,1536]{1,0:T(8,128)(2,1)}, u32[]{:S(2)}, u32[]{:S(2)}) collective-permute-start(bf16[256,1536]{1,0:T(8,128)(2,1)} %collective-permute-done.6.refs_3_.refs_14_), channel_id=1, source_target_pairs={{0,4},{4,0},{8,12},{12,8},{1,5},{5,1},{9,13},{13,9},{2,6},{6,2},{1... | collective-permute-start | bytes 2359304 | tf_op jit(solution)/shard_map/ppermute | solution.py:363
  79.3 49.0 %collective-permute-start.12 = (bf16[256,1536]{1,0:T(8,128)(2,1)}, bf16[256,1536]{1,0:T(8,128)(2,1)}, u32[]{:S(2)}, u32[]{:S(2)}) collective-permute-start(bf16[256,1536]{1,0:T(8,128)(2,1)} %collective-permute-done.5.refs_17_.refs_28_), channel_id=1, source_target_pairs={{0,12},{4,8},{8,4},{12,0},{1,13},{5,9},{9,5},{13,1},{2,14},{6,10},... | collective-permute-start | bytes 2359304 | tf_op jit(solution)/shard_map/ppermute | solution.py:363
  81.8 63.2 %collective-permute-start.11 = (bf16[256,1536]{1,0:T(8,128)(2,1)}, bf16[256,1536]{1,0:T(8,128)(2,1)}, u32[]{:S(2)}, u32[]{:S(2)}) collective-permute-start(bf16[256,1536]{1,0:T(8,128)(2,1)} %collective-permute-done.5.refs_17_.refs_28_), channel_id=1, source_target_pairs={{0,8},{4,12},{8,0},{12,4},{1,9},{5,13},{9,1},{13,5},{2,10},{6,14},... | collective-permute-start | bytes 2359304 | tf_op jit(solution)/shard_map/ppermute | solution.py:363
  97.4 83.9 %collective-permute-start.22 = (bf16[512,1024]{1,0:T(8,128)(2,1)}, bf16[512,1024]{1,0:T(8,128)(2,1)S(1)}, u32[]{:S(2)}, u32[]{:S(2)}) collective-permute-start(bf16[512,1024]{1,0:T(8,128)(2,1)} %refs_22_.1), channel_id=1, source_target_pairs={{0,1},{1,0},{2,3},{3,2},{4,5},{5,4},{6,7},{7,6},{8,9},{9,8},{10,11... | collective-permute-start | bytes 3145736 | tf_op jit(solution)/shard_map/ppermute | solution.py:375
  114.3 67.5 %collective-permute-start.24 = (bf16[1024,512]{1,0:T(8,128)(2,1)}, bf16[1024,512]{1,0:T(8,128)(2,1)}, u32[]{:S(2)}, u32[]{:S(2)}) collective-permute-start(bf16[1024,512]{1,0:T(8,128)(2,1)} %refs_24_.1), channel_id=1, source_target_pairs={{0,1},{1,0},{2,3},{3,2},{4,5},{5,4},{6,7},{7,6},{8,9},{9,8},{10,11... | collective-permute-start | bytes 3145736 | tf_op jit(solution)/shard_map/ppermute | solution.py:375
  114.4 67.5 %collective-permute-start.23 = (bf16[512,1024]{1,0:T(8,128)(2,1)}, bf16[512,1024]{1,0:T(8,128)(2,1)}, u32[]{:S(2)}, u32[]{:S(2)}) collective-permute-start(bf16[512,1024]{1,0:T(8,128)(2,1)} %refs_23_.1), channel_id=1, source_target_pairs={{0,1},{1,0},{2,3},{3,2},{4,5},{5,4},{6,7},{7,6},{8,9},{9,8},{10,11... | collective-permute-start | bytes 3145736 | tf_op jit(solution)/shard_map/ppermute | solution.py:375
  128.3 54.1 %collective-permute-start.26 = (f32[4,256,512]{2,1,0:T(8,128)}, f32[4,256,512]{2,1,0:T(8,128)}, u32[]{:S(2)}, u32[]{:S(2)}) collective-permute-start(f32[4,256,512]{2,1,0:T(8,128)} %get-tuple-element.84), channel_id=1, source_target_pairs={{0,2},{1,3},{2,0},{3,1},{4,6},{5,7},{6,4},{7,5},{8,10},{9,11},{10,... | collective-permute-start | bytes 6291464 | tf_op jit(solution)/shard_map/ppermute | solution.py:374
  145.0 36.3 %collective-permute-start.10 = (bf16[256,1536]{1,0:T(8,128)(2,1)}, bf16[256,1536]{1,0:T(8,128)(2,1)}, u32[]{:S(2)}, u32[]{:S(2)}) collective-permute-start(bf16[256,1536]{1,0:T(8,128)(2,1)} %collective-permute-done.5.refs_17_.refs_28_), channel_id=1, source_target_pairs={{0,4},{4,0},{8,12},{12,8},{1,5},{5,1},{9,13},{13,9},{2,6},{6,2},{1... | collective-permute-start | bytes 2359304 | tf_op jit(solution)/shard_map/ppermute | solution.py:363
  182.4 19.9 %collective-permute-start.25 = (f32[2,256,512]{2,1,0:T(8,128)}, f32[2,256,512]{2,1,0:T(8,128)}, u32[]{:S(2)}, u32[]{:S(2)}) collective-permute-start(f32[2,256,512]{2,1,0:T(8,128)} %collective-permute-done.13.refs_2_), channel_id=1, source_target_pairs={{0,1},{1,0},{2,3},{3,2},{4,5},{5,4},{6,7},{7,6},{8,9},{9,8},{10,11... | collective-permute-start | bytes 3145736 | tf_op jit(solution)/shard_map/ppermute | solution.py:390
  184.0 18.3 %collective-permute-start.18 = (bf16[256,1536]{1,0:T(8,128)(2,1)}, bf16[256,1536]{1,0:T(8,128)(2,1)}, u32[]{:S(2)}, u32[]{:S(2)}) collective-permute-start(bf16[256,1536]{1,0:T(8,128)(2,1)} %collective-permute-done.5.refs_17_.refs_28_), channel_id=1, source_target_pairs={{0,1},{1,0},{2,3},{3,2},{4,5},{5,4},{6,7},{7,6},{8,9},{9,8},{10,11... | collective-permute-start | bytes 2359304 | tf_op jit(solution)/shard_map/ppermute | solution.py:390
  202.3 48.3 %collective-permute-start.27 = (f32[4,256,512]{2,1,0:T(8,128)}, f32[4,256,512]{2,1,0:T(8,128)}, u32[]{:S(2)}, u32[]{:S(2)}) collective-permute-start(f32[4,256,512]{2,1,0:T(8,128)} %collective-permute-done.26.refs_6_.refs_7_), channel_id=1, source_target_pairs={{0,1},{1,0},{2,3},{3,2},{4,5},{5,4},{6,7},{7,6},{8,9},{9,8},{10,11... | collective-permute-start | bytes 6291464 | tf_op jit(solution)/shard_map/ppermute | solution.py:395
  249.9 129.7 %collective-permute-start.33 = (bf16[1,2048,1024]{2,1,0:T(8,128)(2,1)}, bf16[1,2048,1024]{2,1,0:T(8,128)(2,1)}, u32[]{:S(2)}, u32[]{:S(2)}) collective-permute-start(bf16[1,2048,1024]{2,1,0:T(8,128)(2,1)} %get-tuple-element.105), channel_id=1, source_target_pairs={{0,1},{1,0},{2,3},{3,2},{4,5},{5,4},{6,7},{7,6},{8,9},{9,8},{10,11... | collective-permute-start | bytes 12582920 | tf_op jit(solution)/shard_map/ppermute | solution.py:398
  250.1 106.6 %collective-permute-start.30 = (bf16[1,2048,1024]{2,1,0:T(8,128)(2,1)}, bf16[1,2048,1024]{2,1,0:T(8,128)(2,1)}, u32[]{:S(2)}, u32[]{:S(2)}) collective-permute-start(bf16[1,2048,1024]{2,1,0:T(8,128)(2,1)} %get-tuple-element.105), channel_id=1, source_target_pairs={{0,2},{1,3},{2,0},{3,1},{4,6},{5,7},{6,4},{7,5},{8,10},{9,11},{10,... | collective-permute-start | bytes 12582920 | tf_op jit(solution)/shard_map/ppermute | solution.py:397
  356.5 31.0 %collective-permute-start.32 = (bf16[1,2048,1024]{2,1,0:T(8,128)(2,1)}, bf16[1,2048,1024]{2,1,0:T(8,128)(2,1)}, u32[]{:S(2)}, u32[]{:S(2)}) collective-permute-start(bf16[1,2048,1024]{2,1,0:T(8,128)(2,1)} %get-tuple-element.106), channel_id=1, source_target_pairs={{0,1},{1,0},{2,3},{3,2},{4,5},{5,4},{6,7},{7,6},{8,9},{9,8},{10,11... | collective-permute-start | bytes 12582920 | tf_op jit(solution)/shard_map/ppermute | solution.py:403
  356.7 34.5 %collective-permute-start.31 = (bf16[1,2048,1024]{2,1,0:T(8,128)(2,1)}, bf16[1,2048,1024]{2,1,0:T(8,128)(2,1)}, u32[]{:S(2)}, u32[]{:S(2)}) collective-permute-start(bf16[1,2048,1024]{2,1,0:T(8,128)(2,1)} %collective-permute-done.30.refs_1_), channel_id=1, source_target_pairs={{0,1},{1,0},{2,3},{3,2},{4,5},{5,4},{6,7},{7,6},{8,9},{9,8},{10,11... | collective-permute-start | bytes 12582920 | tf_op jit(solution)/shard_map/ppermute | solution.py:404
  357.1 37.7 %collective-permute-start.28 = (bf16[1,2048,1024]{2,1,0:T(8,128)(2,1)}, bf16[1,2048,1024]{2,1,0:T(8,128)(2,1)}, u32[]{:S(2)}, u32[]{:S(2)}) collective-permute-start(bf16[1,2048,1024]{2,1,0:T(8,128)(2,1)} %get-tuple-element.103), channel_id=1, source_target_pairs={{0,1},{1,0},{2,3},{3,2},{4,5},{5,4},{6,7},{7,6},{8,9},{9,8},{10,11... | collective-permute-start | bytes 12582920 | tf_op jit(solution)/shard_map/ppermute | solution.py:406
  (19 other events, 404.2 us)
